TPU v7x, 16 devices: a whole 2x2x2 slice. The times are simulated.
16 devices in a mesh: model: 2 (over z), data: 8 (over y, x, core).
Axes of the slice: x: 2, y: 2, z: 2, core: 2. Of those that a mesh axis runs over, the one named last changes fastest.
Arguments:
- dec_in: bfloat16 [128, 384, 512], P('data')
- enc_out: bfloat16 [128, 192, 512], P('data')
- grad_out: bfloat16 [128, 384, 512], P('data')
- rel_bias: bfloat16 [32, 6], P(None, 'model')
- self_q: bfloat16 [512, 384], P('data', 'model')
- self_k: bfloat16 [512, 384], P('data', 'model')
- self_v: bfloat16 [512, 384], P('data', 'model')
- self_o: bfloat16 [384, 512], P('model', 'data')
- cross_q: bfloat16 [512, 384], P('data', 'model')
- cross_k: bfloat16 [512, 384], P('data', 'model')
- cross_v: bfloat16 [512, 384], P('data', 'model')
- cross_o: bfloat16 [384, 512], P('model', 'data')
- mlp_wi_0: bfloat16 [512, 1024], P('data', 'model')
- mlp_wi_1: bfloat16 [512, 1024], P('data', 'model')
- mlp_wo: bfloat16 [1024, 512], P('model', 'data')
- norm_self: bfloat16 [512], P('data')
- norm_cross: bfloat16 [512], P('data')
- norm_mlp: bfloat16 [512], P('data')
Outputs:
- output 1: bfloat16 [128, 384, 512], P('data')
- output 2: bfloat16 [128, 384, 512], P('data')
- output 3: bfloat16 [128, 192, 512], P('data')
- output 4: float32 [32, 6], P(None, 'model')
- output 5: float32 [512, 384], P('data', 'model')
- output 6: float32 [512, 384], P('data', 'model')
- output 7: float32 [512, 384], P('data', 'model')
- output 8: float32 [384, 512], P('model', 'data')
- output 9: float32 [512, 384], P('data', 'model')
- output 10: float32 [512, 384], P('data', 'model')
- output 11: float32 [512, 384], P('data', 'model')
- output 12: float32 [384, 512], P('model', 'data')
- output 13: float32 [512, 1024], P('data', 'model')
- output 14: float32 [512, 1024], P('data', 'model')
- output 15: float32 [1024, 512], P('model', 'data')
- output 16: float32 [512], P('data')
- output 17: float32 [512], P('data')
- output 18: float32 [512], P('data')
All inputs are finite; a program needn't handle non-finite values.
Results may differ from a plain program's by a relative error of at most 0.02.
Values are sent between devices in bfloat16 or wider.
A program may use at most 1 GiB of HBM per device.

v0:
```python
import math
import jax
import jax.numpy as jnp
from jax import lax
from jax.sharding import PartitionSpec as P

EPS = 1e-6
NUM_BUCKETS = 32
MASK_VALUE = -1e9
BUCKET_EDGES = tuple(math.ceil(16 * 8.0 ** (bucket_no / 16.0)) for bucket_no in range(1, 16))


def bucket_table(seq_len):
    positions = jnp.arange(seq_len)
    rel_dist = jnp.maximum(positions[:, None] - positions[None, :], 0)
    bucket_edges = jnp.array(BUCKET_EDGES, dtype=jnp.int32)
    bucket_ids = jnp.minimum(rel_dist, 16) + jnp.sum((rel_dist[:, :, None] >= bucket_edges).astype(jnp.int32), axis=-1)
    one_hot = (bucket_ids[:, :, None] == jnp.arange(NUM_BUCKETS)).astype(jnp.bfloat16)
    return one_hot, positions[:, None] >= positions[None, :]


def gelu_tanh(pre_act):
    return jax.nn.gelu(pre_act, approximate=True)


def norm_fwd(act_in, gain_vec):
    act_f = act_in.astype(jnp.float32)
    inv_rms = lax.rsqrt(jnp.mean(act_f * act_f, axis=-1, keepdims=True) + EPS)
    unit_act = act_f * inv_rms
    return (unit_act * gain_vec.astype(jnp.float32)).astype(jnp.bfloat16), unit_act, inv_rms


def norm_bwd(d_norm, unit_act, inv_rms, gain_vec):
    d_norm_f = d_norm.astype(jnp.float32)
    d_unit = d_norm_f * gain_vec.astype(jnp.float32)
    d_act = inv_rms * (d_unit - unit_act * jnp.mean(d_unit * unit_act, axis=-1, keepdims=True))
    return d_act, jnp.sum(d_norm_f * unit_act, axis=(0, 1))


def project(act_in, weight):
    return jnp.einsum("bsd,dhe->bshe", act_in, weight, preferred_element_type=jnp.float32).astype(jnp.bfloat16)


def back_in(d_heads, weight):
    return jnp.einsum("bshe,dhe->bsd", d_heads, weight, preferred_element_type=jnp.float32)


def in_grad(act_in, d_heads):
    grad_w = jnp.einsum("bsd,bshe->dhe", act_in, d_heads, preferred_element_type=jnp.float32)
    return grad_w.reshape(grad_w.shape[0], -1)


def out_proj(context, weight):
    return jnp.einsum("crif,ife->cre", context, weight, preferred_element_type=jnp.float32)


def out_grad(context, d_res):
    grad_w = jnp.einsum("crif,cre->ife", context, d_res, preferred_element_type=jnp.float32)
    return grad_w.reshape(-1, grad_w.shape[2])


def ctx_grad(d_res, weight):
    return jnp.einsum("cre,ife->crif", d_res, weight, preferred_element_type=jnp.float32).astype(jnp.bfloat16)


def attn_fwd(q_heads, k_heads, v_heads, pos_bias, key_mask):
    logits = jnp.einsum("bqhe,bkhe->bhqk", q_heads, k_heads, preferred_element_type=jnp.float32)
    logits = jnp.where(key_mask, logits.astype(jnp.bfloat16).astype(jnp.float32) + pos_bias, MASK_VALUE)
    attn_probs = jax.nn.softmax(logits, axis=-1)
    context = jnp.einsum("bhqk,bkhe->bqhe", attn_probs.astype(jnp.bfloat16), v_heads, preferred_element_type=jnp.float32)
    return attn_probs, context.astype(jnp.bfloat16)


def attn_bwd(d_context, attn_probs, q_heads, k_heads, v_heads):
    d_probs = jnp.einsum("bqhe,bkhe->bhqk", d_context, v_heads, preferred_element_type=jnp.float32)
    d_probs = d_probs.astype(jnp.bfloat16).astype(jnp.float32)
    d_logits = attn_probs * (d_probs - jnp.sum(attn_probs * d_probs, axis=-1, keepdims=True))
    d_logits_b = d_logits.astype(jnp.bfloat16)
    d_query = jnp.einsum("bhqk,bkhe->bqhe", d_logits_b, k_heads, preferred_element_type=jnp.float32)
    d_key = jnp.einsum("bhqk,bqhe->bkhe", d_logits_b, q_heads, preferred_element_type=jnp.float32)
    d_value = jnp.einsum("bhqk,bqhe->bkhe", attn_probs.astype(jnp.bfloat16), d_context, preferred_element_type=jnp.float32)
    return d_logits, d_query.astype(jnp.bfloat16), d_key.astype(jnp.bfloat16), d_value.astype(jnp.bfloat16)


def residual(base_val, delta_val):
    return (base_val.astype(jnp.float32) + delta_val.astype(jnp.float32)).astype(jnp.bfloat16)


def gather_in(w_shard, heads_dev):
    w_full = lax.all_gather(w_shard, "data", axis=0, tiled=True)
    return w_full.reshape(w_full.shape[0], heads_dev, -1)


def gather_out(w_shard, heads_dev):
    w_full = lax.all_gather(w_shard, "data", axis=1, tiled=True)
    return w_full.reshape(heads_dev, -1, w_full.shape[1])


def gather_data(w_shard, dim_idx):
    return lax.all_gather(w_shard, "data", axis=dim_idx, tiled=True)


def model_sum(partial):
    return lax.psum(partial.astype(jnp.bfloat16), "model")


def data_scatter(grad_full, dim_idx):
    return lax.psum_scatter(grad_full, "data", scatter_dimension=dim_idx, tiled=True)


def layer_shard(dec_in, enc_out, grad_out, rel_bias, self_q, self_k, self_v, self_o, cross_q, cross_k, cross_v, cross_o, mlp_wi_0, mlp_wi_1, mlp_wo, norm_self, norm_cross, norm_mlp):
    heads_dev = rel_bias.shape[1]
    one_hot, causal = bucket_table(dec_in.shape[1])
    pos_bias = jnp.einsum("qkr,rh->hqk", one_hot, rel_bias, preferred_element_type=jnp.float32)
    gain_1 = gather_data(norm_self, 0)
    gain_2 = gather_data(norm_cross, 0)
    gain_3 = gather_data(norm_mlp, 0)

    normed_1, unit_1, inv_1 = norm_fwd(dec_in, gain_1)
    q_self = project(normed_1, gather_in(self_q, heads_dev))
    k_self = project(normed_1, gather_in(self_k, heads_dev))
    v_self = project(normed_1, gather_in(self_v, heads_dev))
    probs_self, ctx_self = attn_fwd(q_self, k_self, v_self, pos_bias, causal)
    mid_1 = residual(dec_in, model_sum(out_proj(ctx_self, gather_out(self_o, heads_dev))))

    normed_2, unit_2, inv_2 = norm_fwd(mid_1, gain_2)
    q_cross = project(normed_2, gather_in(cross_q, heads_dev))
    k_cross = project(enc_out, gather_in(cross_k, heads_dev))
    v_cross = project(enc_out, gather_in(cross_v, heads_dev))
    probs_cross, ctx_cross = attn_fwd(q_cross, k_cross, v_cross, 0.0, True)
    mid_2 = residual(mid_1, model_sum(out_proj(ctx_cross, gather_out(cross_o, heads_dev))))

    normed_3, unit_3, inv_3 = norm_fwd(mid_2, gain_3)
    pre_0 = jnp.einsum("bsd,df->bsf", normed_3, gather_data(mlp_wi_0, 0), preferred_element_type=jnp.float32).astype(jnp.bfloat16)
    pre_1 = jnp.einsum("bsd,df->bsf", normed_3, gather_data(mlp_wi_1, 0), preferred_element_type=jnp.float32).astype(jnp.bfloat16)
    gelu_0, gelu_pull = jax.vjp(gelu_tanh, pre_0.astype(jnp.float32))
    hidden = (gelu_0 * pre_1.astype(jnp.float32)).astype(jnp.bfloat16)
    mlp_part = jnp.einsum("bsf,fd->bsd", hidden, gather_data(mlp_wo, 1), preferred_element_type=jnp.float32)
    dec_out = residual(mid_2, model_sum(mlp_part))

    d_hidden = jnp.einsum("bsd,fd->bsf", grad_out, gather_data(mlp_wo, 1), preferred_element_type=jnp.float32)
    d_hidden = d_hidden.astype(jnp.bfloat16).astype(jnp.float32)
    d_pre_0 = gelu_pull(d_hidden * pre_1.astype(jnp.float32))[0].astype(jnp.bfloat16)
    d_pre_1 = (d_hidden * gelu_0).astype(jnp.bfloat16)
    d_norm_3 = model_sum(jnp.einsum("bsf,df->bsd", d_pre_0, gather_data(mlp_wi_0, 0), preferred_element_type=jnp.float32) + jnp.einsum("bsf,df->bsd", d_pre_1, gather_data(mlp_wi_1, 0), preferred_element_type=jnp.float32))
    grad_mlp_wo = data_scatter(jnp.einsum("bsf,bsd->fd", hidden, grad_out, preferred_element_type=jnp.float32), 1)
    grad_wi_0 = data_scatter(jnp.einsum("bsd,bsf->df", normed_3, d_pre_0, preferred_element_type=jnp.float32), 0)
    grad_wi_1 = data_scatter(jnp.einsum("bsd,bsf->df", normed_3, d_pre_1, preferred_element_type=jnp.float32), 0)
    d_act_3, d_gain_3 = norm_bwd(d_norm_3, unit_3, inv_3, gain_3)
    d_mid_2 = residual(grad_out, d_act_3)

    grad_cross_o = data_scatter(out_grad(ctx_cross, d_mid_2), 1)
    d_ctx_cross = ctx_grad(d_mid_2, gather_out(cross_o, heads_dev))
    _, dq_cross, dk_cross, dv_cross = attn_bwd(d_ctx_cross, probs_cross, q_cross, k_cross, v_cross)
    d_norm_2 = model_sum(back_in(dq_cross, gather_in(cross_q, heads_dev)))
    grad_enc = model_sum(back_in(dk_cross, gather_in(cross_k, heads_dev)) + back_in(dv_cross, gather_in(cross_v, heads_dev)))
    grad_cross_q = data_scatter(in_grad(normed_2, dq_cross), 0)
    grad_cross_k = data_scatter(in_grad(enc_out, dk_cross), 0)
    grad_cross_v = data_scatter(in_grad(enc_out, dv_cross), 0)
    d_act_2, d_gain_2 = norm_bwd(d_norm_2, unit_2, inv_2, gain_2)
    d_mid_1 = residual(d_mid_2, d_act_2)

    grad_self_o = data_scatter(out_grad(ctx_self, d_mid_1), 1)
    d_ctx_self = ctx_grad(d_mid_1, gather_out(self_o, heads_dev))
    d_logit_self, dq_self, dk_self, dv_self = attn_bwd(d_ctx_self, probs_self, q_self, k_self, v_self)
    bias_part = jnp.einsum("qkr,hqk->rh", one_hot.astype(jnp.float32), jnp.sum(d_logit_self, axis=0))
    grad_bias = lax.psum(bias_part, "data")
    d_norm_1 = model_sum(back_in(dq_self, gather_in(self_q, heads_dev)) + back_in(dk_self, gather_in(self_k, heads_dev)) + back_in(dv_self, gather_in(self_v, heads_dev)))
    grad_self_q = data_scatter(in_grad(normed_1, dq_self), 0)
    grad_self_k = data_scatter(in_grad(normed_1, dk_self), 0)
    grad_self_v = data_scatter(in_grad(normed_1, dv_self), 0)
    d_act_1, d_gain_1 = norm_bwd(d_norm_1, unit_1, inv_1, gain_1)
    grad_dec = residual(d_mid_1, d_act_1)
    return (dec_out, grad_dec, grad_enc, grad_bias, grad_self_q, grad_self_k, grad_self_v, grad_self_o, grad_cross_q, grad_cross_k, grad_cross_v, grad_cross_o, grad_wi_0, grad_wi_1, grad_mlp_wo, data_scatter(d_gain_1, 0), data_scatter(d_gain_2, 0), data_scatter(d_gain_3, 0))


def solution(mesh):
    row_spec = P("data", None, None)
    col_in = P("data", "model")
    col_out = P("model", "data")
    gain_spec = P("data")
    bias_spec = P(None, "model")
    arg_specs = (row_spec, row_spec, row_spec, bias_spec, col_in, col_in, col_in, col_out, col_in, col_in, col_in, col_out, col_in, col_in, col_out, gain_spec, gain_spec, gain_spec)
    out_specs = (row_spec, row_spec, row_spec) + arg_specs[3:]
    return jax.shard_map(layer_shard, mesh=mesh, in_specs=arg_specs, out_specs=out_specs, check_vma=False)
```

profile of v0, /device:TPU:0, one launch (start us, length us, event | category | flops | bytes accessed | tf_op | source)
XLA Modules:
  0.0 1769.3 jit_solution(13552121901065540431)
XLA Ops:
  13.4 15.4 all-reduce.7
  97.6 27.8 %copy.110 = pred[384,384,32]{1,2,0:T(32,128)(4,1)} copy(pred[384,384,32]{0,2,1:T(32,128)(4,1)} %iota_compare_fusion) | data formatting | bytes 9437184 | tf_op jit(solution)/shard_map/eq | solution.py:18
  146.8 27.9 %fusion.187 = (f32[16,3,384]{2,1,0:T(4,128)S(1)}, f32[16,3,384,384]{2,3,1,0:T(8,128)}) fusion(bf16[16,3,384,384]{2,3,1,0:T(8,128)(2,1)} %convolution_convert_fusion.1, f32[3,384,384]{1,2,0:T(8,128)} %copy.111, pred[384,384]{0,1:T(8,128)(4,1)S(1)} %copy-done.45), kind=kOutput, calls=%fused_computation.206 | output fusion | flops 56623488 | bytes 44457984 | tf_op jit(solution)/shard_map/sub | solution.py:69
  239.1 104.8 %all-reduce.15.cloned.1.call-done = bf16[16,384,512]{2,1,0:T(8,128)(2,1)} async-done(((bf16[16,384,512]{2,1,0:T(8,128)(2,1)}), bf16[16,384,512]{2,1,0:T(8,128)(2,1)}) %all-reduce.15.cloned.1.call-update) | async-done | bytes 6291472 | tf_op jit(solution)/shard_map/psum | solution.py:104
  413.2 110.5 %all-reduce.17.cloned.1.call-done = bf16[16,384,512]{2,1,0:T(8,128)(2,1)} async-done(((bf16[16,384,512]{2,1,0:T(8,128)(2,1)}), bf16[16,384,512]{2,1,0:T(8,128)(2,1)}) %all-reduce.17.cloned.1.call-update) | async-done | bytes 6291472 | tf_op jit(solution)/shard_map/psum | solution.py:104
  543.7 15.6 fusion.43
  578.0 149.3 %all-reduce.19.cloned.1.call-done = bf16[16,384,512]{2,1,0:T(8,128)(2,1)} async-done(((bf16[16,384,512]{2,1,0:T(8,128)(2,1)}), bf16[16,384,512]{2,1,0:T(8,128)(2,1)}) %all-reduce.19.cloned.1.call-update) | async-done | bytes 6291472 | tf_op jit(solution)/shard_map/psum | solution.py:104
  804.6 120.9 %all-reduce.21.cloned.1.call-done = bf16[16,384,512]{2,1,0:T(8,128)(2,1)} async-done(((bf16[16,384,512]{2,1,0:T(8,128)(2,1)}), bf16[16,384,512]{2,1,0:T(8,128)(2,1)}) %all-reduce.21.cloned.1.call-update) | async-done | bytes 6291472 | tf_op jit(solution)/shard_map/psum | solution.py:104
  961.0 18.0 %fusion.1 = (f32[16,3,384]{2,1,0:T(4,128)S(1)}, bf16[16,3,384,384]{2,3,1,0:T(8,128)(2,1)}) fusion(f32[16,3,384,384]{2,3,1,0:T(8,128)} %get-tuple-element.43, f32[16,3,384]{2,1,0:T(4,128)S(1)} %copy-done.47, bf16[16,384,3,64]{1,3,2,0:T(8,128)(2,1)} %copy-done.19, bf16[16,384,3,64]{1,3,2,0:T(8,128)(2,1)} %convolution_convert_fusion.13), kind=kOutput, calls=%fused_computation.3 | convolution fusion | flops 941340672 | bytes 47333376 | tf_op jit(solution)/shard_map/bqhe,bkhe->bhqk/dot_general | solution.py:75
  979.0 23.0 %fusion.17 = (bf16[3,384,384]{1,2,0:T(8,128)(2,1)}, bf16[16,3,384,384]{2,3,1,0:T(8,128)(2,1)}) fusion(bf16[16,3,384,384]{2,3,1,0:T(8,128)(2,1)} %get-tuple-element.51, f32[16,3,384]{2,1,0:T(4,128)S(1)} %get-tuple-element.50, f32[16,3,384,384]{2,3,1,0:T(8,128)} %get-tuple-element.43, f32[16,3,384]{2,1,0:T(4,128)S(1)} %copy-done.47), kind=kLoop, calls=%fused_computation.36 | loop fusion | flops 42024960 | bytes 57655296 | tf_op jit(solution)/shard_map/reduce_sum | solution.py:166
  1070.0 13.7 convolution_bitcast_fusion.1
  1133.7 266.0 %all-reduce.23.cloned.1.call-done = (bf16[16,384,512]{2,1,0:T(8,128)(2,1)}, bf16[16,384,512]{2,1,0:T(8,128)(2,1)}, bf16[16,192,512]{2,1,0:T(8,128)(2,1)}) async-done(((bf16[16,384,512]{2,1,0:T(8,128)(2,1)}, bf16[16,384,512]{2,1,0:T(8,128)(2,1)}, bf16[16,192,512]{2,1,0:T(8,128)(2,1)}), (bf16[16,384,512]{2,1,0:T(8,128)(2,1)}, bf16[16,384,512]{2,1,0:T(8,128)(2,1)}, ...) | async-done | bytes 15728656 | tf_op jit(solution)/shard_map/psum | solution.py:104
  1408.2 14.8 fusion.32
  1423.0 14.1 all-reduce.6
  1438.9 28.7 %reduce-scatter.30.cloned.1.call-done = f32[64,512]{1,0:T(8,128)} async-done(((f32[512,512]{1,0:T(8,128)}), f32[64,512]{1,0:T(8,128)}) %reduce-scatter.30.cloned.1.call-update) | async-done | bytes 131088 | tf_op jit(solution)/shard_map/reduce_scatter | solution.py:108
  1467.6 34.0 %reduce-scatter.32.cloned.1.call-done = f32[512,64]{0,1:T(8,128)} async-done(((f32[512,512]{0,1:T(8,128)}), f32[512,64]{0,1:T(8,128)}) %reduce-scatter.32.cloned.1.call-update) | async-done | bytes 131088 | tf_op jit(solution)/shard_map/reduce_scatter | solution.py:108
  1501.7 32.2 %reduce-scatter.26.cloned.1.call-done = f32[192,64]{0,1:T(8,128)} async-done(((f32[192,512]{0,1:T(8,128)}), f32[192,64]{0,1:T(8,128)}) %reduce-scatter.26.cloned.1.call-update) | async-done | bytes 49168 | tf_op jit(solution)/shard_map/reduce_scatter | solution.py:108
  1533.9 32.0 %reduce-scatter.24.cloned.1.call-done = f32[64,192]{1,0:T(8,128)} async-done(((f32[512,192]{1,0:T(8,128)}), f32[64,192]{1,0:T(8,128)}) %reduce-scatter.24.cloned.1.call-update) | async-done | bytes 49168 | tf_op jit(solution)/shard_map/reduce_scatter | solution.py:108
  1565.9 32.2 %reduce-scatter.20.cloned.1.call-done = f32[64,192]{1,0:T(8,128)} async-done(((f32[512,192]{1,0:T(8,128)}), f32[64,192]{1,0:T(8,128)}) %reduce-scatter.20.cloned.1.call-update) | async-done | bytes 49168 | tf_op jit(solution)/shard_map/reduce_scatter | solution.py:108
  1598.1 32.0 %reduce-scatter.22.cloned.1.call-done = f32[64,192]{1,0:T(8,128)} async-done(((f32[512,192]{1,0:T(8,128)}), f32[64,192]{1,0:T(8,128)}) %reduce-scatter.22.cloned.1.call-update) | async-done | bytes 49168 | tf_op jit(solution)/shard_map/reduce_scatter | solution.py:108
  1630.1 32.2 %reduce-scatter.18.cloned.1.call-done = f32[192,64]{0,1:T(8,128)} async-done(((f32[192,512]{0,1:T(8,128)}), f32[192,64]{0,1:T(8,128)}) %reduce-scatter.18.cloned.1.call-update) | async-done | bytes 49168 | tf_op jit(solution)/shard_map/reduce_scatter | solution.py:108
  1662.3 32.0 %reduce-scatter.16.cloned.1.call-done = f32[64,192]{1,0:T(8,128)} async-done(((f32[512,192]{1,0:T(8,128)}), f32[64,192]{1,0:T(8,128)}) %reduce-scatter.16.cloned.1.call-update) | async-done | bytes 49168 | tf_op jit(solution)/shard_map/reduce_scatter | solution.py:108
  1694.4 32.0 %reduce-scatter.12.cloned.1.call-done = f32[64,192]{1,0:T(8,128)} async-done(((f32[512,192]{1,0:T(8,128)}), f32[64,192]{1,0:T(8,128)}) %reduce-scatter.12.cloned.1.call-update) | async-done | bytes 49168 | tf_op jit(solution)/shard_map/reduce_scatter | solution.py:108
  1726.4 32.0 %reduce-scatter.14.cloned.1.call-done = f32[64,192]{1,0:T(8,128)} async-done(((f32[512,192]{1,0:T(8,128)}), f32[64,192]{1,0:T(8,128)}) %reduce-scatter.14.cloned.1.call-update) | async-done | bytes 49168 | tf_op jit(solution)/shard_map/reduce_scatter | solution.py:108
  (295 shorter events, 511.3 us)
Async XLA Ops:
  7.2 225.8 %copy-start = (bf16[16,192,512]{2,1,0:T(8,128)(2,1)S(1)}, bf16[16,192,512]{2,1,0:T(8,128)(2,1)}, u32[]{:S(2)}) copy-start(bf16[16,192,512]{2,1,0:T(8,128)(2,1)} %param.20) | copy-start | bytes 9437188
  7.2 64.1 %copy-start.65 = (s32[15]{0:T(128)S(1)}, s32[15]{0:T(128)}, u32[]{:S(2)}) copy-start(s32[15]{0:T(128)} %constant.39.clone) | copy-start | bytes 184
  7.2 336.7 %all-reduce.15.cloned.1.call-start = ((), (), s32[]{:S(2)}) async-start(), calls=%async_computation.11 | async-start | bytes 12582912 | tf_op jit(solution)/shard_map/psum | solution.py:104
  194.5 329.2 %all-reduce.17.cloned.1.call-start = ((), (), s32[]{:S(2)}) async-start(), calls=%async_computation.12 | async-start | bytes 12582912 | tf_op jit(solution)/shard_map/psum | solution.py:104
  194.6 158.9 %copy-start.57 = (f32[512]{0:T(512)}, f32[512]{0:T(512)S(1)}, u32[]{:S(2)}) copy-start(f32[512]{0:T(512)S(1)} %convert_element_type.259) | copy-start | bytes 6148
  239.1 115.0 %copy-start.43 = (bf16[512,192]{0,1:T(8,128)(2,1)S(1)}, bf16[512,192]{0,1:T(8,128)(2,1)}, u32[]{:S(2)}) copy-start(bf16[512,192]{0,1:T(8,128)(2,1)} %copy.115) | copy-start | bytes 589828
  374.4 352.9 %all-reduce.19.cloned.1.call-start = ((), (), s32[]{:S(2)}) async-start(), calls=%async_computation.13 | async-start | bytes 12582912 | tf_op jit(solution)/shard_map/psum | solution.py:104
  374.4 361.9 %copy-start.60 = (f32[512]{0:T(512)}, f32[512]{0:T(512)S(1)}, u32[]{:S(2)}) copy-start(f32[512]{0:T(512)S(1)} %convert_element_type.272) | copy-start | bytes 6148
  578.0 347.5 %all-reduce.21.cloned.1.call-start = ((), (), s32[]{:S(2)}) async-start(), calls=%async_computation.14 | async-start | bytes 12582912 | tf_op jit(solution)/shard_map/psum | solution.py:104
  776.1 623.5 %all-reduce.23.cloned.1.call-start = ((), (), s32[]{:S(2)}) async-start(), calls=%async_computation.26 | async-start | bytes 31457280 | tf_op jit(solution)/shard_map/psum | solution.py:104
  801.9 123.6 %copy-start.39 = (f32[16,384]{1,0:T(8,128)S(1)}, f32[16,384]{1,0:T(8,128)}, u32[]{:S(2)}) copy-start(f32[16,384]{1,0:T(8,128)} %copy-done.38) | copy-start | bytes 73732
  801.9 123.6 %copy-start.58 = (f32[512]{0:T(512)S(1)}, f32[512]{0:T(512)}, u32[]{:S(2)}) copy-start(f32[512]{0:T(512)} %copy-done.57) | copy-start | bytes 6148
  1047.8 391.2 %reduce-scatter.28.cloned.1.call-start = ((), (), s32[]{:S(2)}) async-start(), calls=%async_computation.23 | async-start | bytes 1179648 | tf_op jit(solution)/shard_map/reduce_scatter | solution.py:108
  1057.8 409.9 %reduce-scatter.30.cloned.1.call-start = ((), (), s32[]{:S(2)}) async-start(), calls=%async_computation.24 | async-start | bytes 1179648 | tf_op jit(solution)/shard_map/reduce_scatter | solution.py:108
  1070.0 431.7 %reduce-scatter.32.cloned.1.call-start = ((), (), s32[]{:S(2)}) async-start(), calls=%async_computation.25 | async-start | bytes 1179648 | tf_op jit(solution)/shard_map/reduce_scatter | solution.py:108
  1083.8 450.1 %reduce-scatter.26.cloned.1.call-start = ((), (), s32[]{:S(2)}) async-start(), calls=%async_computation.22 | async-start | bytes 589824 | tf_op jit(solution)/shard_map/reduce_scatter | solution.py:108
  1089.9 476.0 %reduce-scatter.24.cloned.1.call-start = ((), (), s32[]{:S(2)}) async-start(), calls=%async_computation.21 | async-start | bytes 589824 | tf_op jit(solution)/shard_map/reduce_scatter | solution.py:108
  1093.4 504.7 %reduce-scatter.20.cloned.1.call-start = ((), (), s32[]{:S(2)}) async-start(), calls=%async_computation.19 | async-start | bytes 589824 | tf_op jit(solution)/shard_map/reduce_scatter | solution.py:108
  1099.8 530.4 %reduce-scatter.22.cloned.1.call-start = ((), (), s32[]{:S(2)}) async-start(), calls=%async_computation.20 | async-start | bytes 589824 | tf_op jit(solution)/shard_map/reduce_scatter | solution.py:108
  1103.1 559.2 %reduce-scatter.18.cloned.1.call-start = ((), (), s32[]{:S(2)}) async-start(), calls=%async_computation.18 | async-start | bytes 589824 | tf_op jit(solution)/shard_map/reduce_scatter | solution.py:108
  1109.7 584.6 %reduce-scatter.16.cloned.1.call-start = ((), (), s32[]{:S(2)}) async-start(), calls=%async_computation.17 | async-start | bytes 589824 | tf_op jit(solution)/shard_map/reduce_scatter | solution.py:108
  1116.2 610.2 %reduce-scatter.12.cloned.1.call-start = ((), (), s32[]{:S(2)}) async-start(), calls=%async_computation.15 | async-start | bytes 589824 | tf_op jit(solution)/shard_map/reduce_scatter | solution.py:108
  1122.6 635.9 %reduce-scatter.14.cloned.1.call-start = ((), (), s32[]{:S(2)}) async-start(), calls=%async_computation.16 | async-start | bytes 589824 | tf_op jit(solution)/shard_map/reduce_scatter | solution.py:108
  1129.2 270.5 %copy-start.37 = (f32[16,384]{1,0:T(8,128)S(1)}, f32[16,384]{1,0:T(8,128)}, u32[]{:S(2)}) copy-start(f32[16,384]{1,0:T(8,128)} %copy-done.36) | copy-start | bytes 73732
  (67 other events, 729.5 us)
Sparse Core Ops, SparseCore 0:
  194.6 149.2 all-reduce.14
  374.5 149.1 all-reduce.16
  578.1 149.1 all-reduce.18
  776.2 149.1 all-reduce.20
  1047.9 351.7 all-reduce.22
  1403.2 30.2 reduce-scatter.27
  1437.2 30.3 reduce-scatter.29
  1471.4 30.2 reduce-scatter.31
  1505.3 28.5 reduce-scatter.25
  1537.3 28.5 reduce-scatter.23
  1569.5 28.5 reduce-scatter.19
  1601.6 28.5 reduce-scatter.21
  1633.8 28.5 reduce-scatter.17
  1665.8 28.5 reduce-scatter.15
  1697.8 28.5 reduce-scatter.11
  1729.9 28.5 reduce-scatter.13
where the time goes:
time: 1780 us; the launch traced here: 1770 us
  waiting for transfers between devices  1070 us (60%)
  matrix products  326 us (18%)
  other arithmetic  150 us (8%)
  blocking collectives  130 us (7%)
  local copies, waits for them, and re-layouts  75.1 us (4%)
    psum x5, waiting for transfers between devices, model_sum(): return lax.psum(partial.astype(jnp.bfloat16), 'model')  751 us
    reduce_scatter x11, waiting for transfers between devices, data_scatter(): lax.psum_scatter(grad_full, 'data', scatter_dimension=dim_idx, tiled=True)  320 us
    all_gather x6, blocking collectives, gather_in(): w_full = lax.all_gather(w_shard, 'data', axis=0, tiled=True)  52 us
  transfers between devices with their start and end apart: 16, of which 15 were waited for; matrix products, arithmetic and copies ran while one was open for 9% of the time, Pallas kernels for 0%

commit v1 on v0

v1 whole, which is shorter than its diff:
```python
import math
import jax
import jax.numpy as jnp
from jax import lax
from jax.sharding import PartitionSpec as P

EPS = 1e-6
NUM_BUCKETS = 32
MASK_VALUE = -1e9
BUCKET_EDGES = tuple(math.ceil(16 * 8.0 ** (bucket_no / 16.0)) for bucket_no in range(1, 16))


def bucket_table(seq_len):
    positions = jnp.arange(seq_len)
    rel_dist = jnp.maximum(positions[:, None] - positions[None, :], 0)
    bucket_edges = jnp.array(BUCKET_EDGES, dtype=jnp.int32)
    bucket_ids = jnp.minimum(rel_dist, 16) + jnp.sum((rel_dist[:, :, None] >= bucket_edges).astype(jnp.int32), axis=-1)
    one_hot = (bucket_ids[:, :, None] == jnp.arange(NUM_BUCKETS)).astype(jnp.bfloat16)
    return one_hot, positions[:, None] >= positions[None, :]


def gelu_tanh(pre_act):
    return jax.nn.gelu(pre_act, approximate=True)


def norm_fwd(act_in, gain_vec):
    act_f = act_in.astype(jnp.float32)
    inv_rms = lax.rsqrt(jnp.mean(act_f * act_f, axis=-1, keepdims=True) + EPS)
    unit_act = act_f * inv_rms
    return (unit_act * gain_vec.astype(jnp.float32)).astype(jnp.bfloat16), unit_act, inv_rms


def norm_bwd(d_norm, unit_act, inv_rms, gain_vec):
    d_norm_f = d_norm.astype(jnp.float32)
    d_unit = d_norm_f * gain_vec.astype(jnp.float32)
    d_act = inv_rms * (d_unit - unit_act * jnp.mean(d_unit * unit_act, axis=-1, keepdims=True))
    return d_act, jnp.sum(d_norm_f * unit_act, axis=(0, 1))


def project(act_in, weight):
    return jnp.einsum("bsd,dhe->bshe", act_in, weight, preferred_element_type=jnp.float32).astype(jnp.bfloat16)


def back_in(d_heads, weight):
    return jnp.einsum("bshe,dhe->bsd", d_heads, weight, preferred_element_type=jnp.float32)


def in_grad(act_in, d_heads):
    grad_w = jnp.einsum("bsd,bshe->dhe", act_in, d_heads, preferred_element_type=jnp.float32)
    return grad_w.reshape(grad_w.shape[0], -1)


def out_proj(context, weight):
    return jnp.einsum("crif,ife->cre", context, weight, preferred_element_type=jnp.float32)


def out_grad(context, d_res):
    grad_w = jnp.einsum("crif,cre->ife", context, d_res, preferred_element_type=jnp.float32)
    return grad_w.reshape(-1, grad_w.shape[2])


def ctx_grad(d_res, weight):
    return jnp.einsum("cre,ife->crif", d_res, weight, preferred_element_type=jnp.float32).astype(jnp.bfloat16)


def attn_fwd(q_heads, k_heads, v_heads, pos_bias, key_mask):
    logits = jnp.einsum("bqhe,bkhe->bhqk", q_heads, k_heads, preferred_element_type=jnp.float32)
    logits = jnp.where(key_mask, logits.astype(jnp.bfloat16).astype(jnp.float32) + pos_bias, MASK_VALUE)
    attn_probs = jax.nn.softmax(logits, axis=-1)
    context = jnp.einsum("bhqk,bkhe->bqhe", attn_probs.astype(jnp.bfloat16), v_heads, preferred_element_type=jnp.float32)
    return attn_probs, context.astype(jnp.bfloat16)


def attn_bwd(d_context, attn_probs, q_heads, k_heads, v_heads):
    d_probs = jnp.einsum("bqhe,bkhe->bhqk", d_context, v_heads, preferred_element_type=jnp.float32)
    d_probs = d_probs.astype(jnp.bfloat16).astype(jnp.float32)
    d_logits = attn_probs * (d_probs - jnp.sum(attn_probs * d_probs, axis=-1, keepdims=True))
    d_logits_b = d_logits.astype(jnp.bfloat16)
    d_query = jnp.einsum("bhqk,bkhe->bqhe", d_logits_b, k_heads, preferred_element_type=jnp.float32)
    d_key = jnp.einsum("bhqk,bqhe->bkhe", d_logits_b, q_heads, preferred_element_type=jnp.float32)
    d_value = jnp.einsum("bhqk,bqhe->bkhe", attn_probs.astype(jnp.bfloat16), d_context, preferred_element_type=jnp.float32)
    return d_logits, d_query.astype(jnp.bfloat16), d_key.astype(jnp.bfloat16), d_value.astype(jnp.bfloat16)


def residual(base_val, delta_val):
    return (base_val.astype(jnp.float32) + delta_val.astype(jnp.float32)).astype(jnp.bfloat16)


IN_HALF = 192
FF_HALF = 512


def pack_local(sq, sk, sv, so, cq, ck, cv, co, wi0, wi1, wo):
    return [sq, sk, sv, so.T, cq, ck, cv, co.T, wi0, wi1, wo.T]


def gather_weights(blocks):
    local = jnp.concatenate(blocks, axis=1)
    pair = lax.all_gather(local, "model", axis=0)
    cols = []
    off = 0
    for blk in blocks:
        width = blk.shape[1]
        cols.append(pair[0, :, off:off + width])
        cols.append(pair[1, :, off:off + width])
        off += width
    both = jnp.concatenate(cols, axis=1)
    return lax.all_gather(both, "data", axis=0, tiled=True)


def scatter_grads(grad_all, widths):
    rows = lax.psum_scatter(grad_all, "data", scatter_dimension=0, tiled=True)
    lo, hi = [], []
    off = 0
    for width in widths:
        lo.append(rows[:, off:off + width])
        hi.append(rows[:, off + width:off + 2 * width])
        off += 2 * width
    pair = jnp.stack([jnp.concatenate(lo, axis=1), jnp.concatenate(hi, axis=1)])
    mine = lax.psum_scatter(pair, "model", scatter_dimension=0)
    outs = []
    off = 0
    for width in widths:
        outs.append(mine[:, off:off + width])
        off += width
    return outs


def layer_shard(dec_in, enc_out, grad_out, rel_bias, self_q, self_k, self_v, self_o, cross_q, cross_k, cross_v, cross_o, mlp_wi_0, mlp_wi_1, mlp_wo, norm_self, norm_cross, norm_mlp):
    model_idx = lax.axis_index("model")
    data_idx = lax.axis_index("data")
    half = dec_in.shape[0] // 2
    dec_in = lax.dynamic_slice_in_dim(dec_in, model_idx * half, half, 0)
    enc_out = lax.dynamic_slice_in_dim(enc_out, model_idx * half, half, 0)
    grad_out = lax.dynamic_slice_in_dim(grad_out, model_idx * half, half, 0)
    blocks = pack_local(self_q, self_k, self_v, self_o, cross_q, cross_k, cross_v, cross_o, mlp_wi_0, mlp_wi_1, mlp_wo)
    widths = [blk.shape[1] for blk in blocks]
    weights = gather_weights(blocks)
    full = []
    off = 0
    for width in widths:
        full.append(weights[:, off:off + 2 * width])
        off += 2 * width
    w_sq, w_sk, w_sv, w_so, w_cq, w_ck, w_cv, w_co, w_i0, w_i1, w_o = full
    gains = lax.all_gather(jnp.stack([norm_self, norm_cross, norm_mlp]), "data", axis=1, tiled=True)
    gain_1, gain_2, gain_3 = gains[0], gains[1], gains[2]
    bias_pair = lax.all_gather(rel_bias, "model", axis=1, tiled=True)

    heads = bias_pair.shape[1]
    one_hot, causal = bucket_table(dec_in.shape[1])
    pos_bias = jnp.einsum("qkr,rh->hqk", one_hot, bias_pair, preferred_element_type=jnp.float32)

    def heads_in(w):
        return w.reshape(w.shape[0], heads, -1)

    normed_1, unit_1, inv_1 = norm_fwd(dec_in, gain_1)
    q_self = project(normed_1, heads_in(w_sq))
    k_self = project(normed_1, heads_in(w_sk))
    v_self = project(normed_1, heads_in(w_sv))
    probs_self, ctx_self = attn_fwd(q_self, k_self, v_self, pos_bias, causal)
    mid_1 = residual(dec_in, back_in(ctx_self, heads_in(w_so)))

    normed_2, unit_2, inv_2 = norm_fwd(mid_1, gain_2)
    q_cross = project(normed_2, heads_in(w_cq))
    k_cross = project(enc_out, heads_in(w_ck))
    v_cross = project(enc_out, heads_in(w_cv))
    probs_cross, ctx_cross = attn_fwd(q_cross, k_cross, v_cross, 0.0, True)
    mid_2 = residual(mid_1, back_in(ctx_cross, heads_in(w_co)))

    normed_3, unit_3, inv_3 = norm_fwd(mid_2, gain_3)
    pre_0 = jnp.einsum("bsd,df->bsf", normed_3, w_i0, preferred_element_type=jnp.float32).astype(jnp.bfloat16)
    pre_1 = jnp.einsum("bsd,df->bsf", normed_3, w_i1, preferred_element_type=jnp.float32).astype(jnp.bfloat16)
    gelu_0, gelu_pull = jax.vjp(gelu_tanh, pre_0.astype(jnp.float32))
    hidden = (gelu_0 * pre_1.astype(jnp.float32)).astype(jnp.bfloat16)
    dec_out = residual(mid_2, jnp.einsum("bsf,df->bsd", hidden, w_o, preferred_element_type=jnp.float32))

    d_hidden = jnp.einsum("bsd,df->bsf", grad_out, w_o, preferred_element_type=jnp.float32)
    d_hidden = d_hidden.astype(jnp.bfloat16).astype(jnp.float32)
    d_pre_0 = gelu_pull(d_hidden * pre_1.astype(jnp.float32))[0].astype(jnp.bfloat16)
    d_pre_1 = (d_hidden * gelu_0).astype(jnp.bfloat16)
    d_norm_3 = (jnp.einsum("bsf,df->bsd", d_pre_0, w_i0, preferred_element_type=jnp.float32) + jnp.einsum("bsf,df->bsd", d_pre_1, w_i1, preferred_element_type=jnp.float32)).astype(jnp.bfloat16)

    def wgrad(act, d_out):
        return jnp.einsum("bsd,bsf->df", act, d_out, preferred_element_type=jnp.float32)

    g_wo = wgrad(grad_out, hidden)
    g_i0 = wgrad(normed_3, d_pre_0)
    g_i1 = wgrad(normed_3, d_pre_1)
    d_act_3, d_gain_3 = norm_bwd(d_norm_3, unit_3, inv_3, gain_3)
    d_mid_2 = residual(grad_out, d_act_3)

    g_co = in_grad(d_mid_2, ctx_cross)
    d_ctx_cross = project(d_mid_2, heads_in(w_co))
    _, dq_cross, dk_cross, dv_cross = attn_bwd(d_ctx_cross, probs_cross, q_cross, k_cross, v_cross)
    d_norm_2 = back_in(dq_cross, heads_in(w_cq)).astype(jnp.bfloat16)
    grad_enc = (back_in(dk_cross, heads_in(w_ck)) + back_in(dv_cross, heads_in(w_cv))).astype(jnp.bfloat16)
    g_cq = in_grad(normed_2, dq_cross)
    g_ck = in_grad(enc_out, dk_cross)
    g_cv = in_grad(enc_out, dv_cross)
    d_act_2, d_gain_2 = norm_bwd(d_norm_2, unit_2, inv_2, gain_2)
    d_mid_1 = residual(d_mid_2, d_act_2)

    g_so = in_grad(d_mid_1, ctx_self)
    d_ctx_self = project(d_mid_1, heads_in(w_so))
    d_logit_self, dq_self, dk_self, dv_self = attn_bwd(d_ctx_self, probs_self, q_self, k_self, v_self)
    bias_part = jnp.einsum("qkr,hqk->rh", one_hot.astype(jnp.float32), jnp.sum(d_logit_self, axis=0))
    d_norm_1 = (back_in(dq_self, heads_in(w_sq)) + back_in(dk_self, heads_in(w_sk)) + back_in(dv_self, heads_in(w_sv))).astype(jnp.bfloat16)
    g_sq = in_grad(normed_1, dq_self)
    g_sk = in_grad(normed_1, dk_self)
    g_sv = in_grad(normed_1, dv_self)
    d_act_1, d_gain_1 = norm_bwd(d_norm_1, unit_1, inv_1, gain_1)
    grad_dec = residual(d_mid_1, d_act_1)

    small = jnp.concatenate([d_gain_1, d_gain_2, d_gain_3, bias_part.reshape(-1)])
    small = lax.psum(small, ("model", "data"))
    gain_sums = small[:3 * gain_1.shape[0]].reshape(3, -1)
    gain_len = norm_self.shape[0]
    gain_mine = lax.dynamic_slice_in_dim(gain_sums, data_idx * gain_len, gain_len, 1)
    bias_sum = small[3 * gain_1.shape[0]:].reshape(bias_part.shape)
    grad_bias = lax.dynamic_slice_in_dim(bias_sum, model_idx * rel_bias.shape[1], rel_bias.shape[1], 1)

    grads = scatter_grads(jnp.concatenate([g_sq, g_sk, g_sv, g_so, g_cq, g_ck, g_cv, g_co, g_i0, g_i1, g_wo], axis=1), widths)
    o_sq, o_sk, o_sv, o_so, o_cq, o_ck, o_cv, o_co, o_i0, o_i1, o_wo = grads

    def both(arr):
        return lax.all_gather(arr, "model", axis=0, tiled=True)

    return (both(dec_out), both(grad_dec), both(grad_enc), grad_bias, o_sq, o_sk, o_sv, o_so.T, o_cq, o_ck, o_cv, o_co.T, o_i0, o_i1, o_wo.T, gain_mine[0], gain_mine[1], gain_mine[2])


def solution(mesh):
    row_spec = P("data", None, None)
    col_in = P("data", "model")
    col_out = P("model", "data")
    gain_spec = P("data")
    bias_spec = P(None, "model")
    arg_specs = (row_spec, row_spec, row_spec, bias_spec, col_in, col_in, col_in, col_out, col_in, col_in, col_in, col_out, col_in, col_in, col_out, gain_spec, gain_spec, gain_spec)
    out_specs = (row_spec, row_spec, row_spec) + arg_specs[3:]
    return jax.shard_map(layer_shard, mesh=mesh, in_specs=arg_specs, out_specs=out_specs, check_vma=False)
```

time: 1780 us -> 805 us (0.45)
  waiting for transfers between devices: 1070 us -> 248 us
  blocking collectives: 130 us -> 59 us
  other arithmetic: 150 us -> 83 us
  matrix products: 326 us -> 274 us
  local copies, waits for them, and re-layouts: 75.1 us -> 114 us
    psum x5 -> x0, waiting for transfers between devices: 751 us -> none  [model_sum(): return lax.psum(partial.astype(jnp.bfloat16), 'model')]
    reduce_scatter x11 -> x2, waiting for transfers between devices: 320 us -> 82.6 us  [the longest x1 56.3 us: scatter_grads(): rows = lax.psum_scatter(grad_all, 'data', scatter_dimension=0, tiled=True)]
    all_gather x0 -> x4, waiting for transfers between devices: none -> 166 us  [the longest x3 166 us: both(): return lax.all_gather(arr, 'model', axis=0, tiled=True)]
    all_gather x11 -> x3, blocking collectives: 100 us -> 26.4 us  [the longest x1 13.1 us: gather_weights(): pair = lax.all_gather(local, 'model', axis=0)]
    dot_general x16 -> x10, matrix products: 129 us -> 93.8 us  [the longest x3 25.6 us: wgrad(): jnp.einsum('bsd,bsf->df', act, d_out, preferred_element_type=jnp.float32)]
    reduce_sum x3 -> x0, other arithmetic: 26 us -> none  [norm_bwd(): return (d_act, jnp.sum(d_norm_f * unit_act, axis=(0, 1)))]
    reduce_sum x3 -> x1, other arithmetic: 23.8 us -> 2.58 us  [norm_fwd(): inv_rms = lax.rsqrt(jnp.mean(act_f * act_f, axis=-1, keepdims=True) + EPS)]
    slice x0 -> x12, local copies, waits for them, and re-layouts: none -> 20.7 us  [the longest x9 17.8 us: layer_shard(): full.append(weights[:, off:off + 2 * width])]
  transfers between devices with their start and end apart: 16 -> 6, of which waited for: 15 -> 5; matrix products, arithmetic and copies ran while one was open for 9% -> 12% of each run, Pallas kernels for 0% -> 0%
where the time goes in v1:
time: 805 us; the launch traced here: 794 us
  matrix products  274 us (34%)
  waiting for transfers between devices  248 us (31%)
  local copies, waits for them, and re-layouts  114 us (14%)
  other arithmetic  83 us (10%)
  blocking collectives  59 us (7%)
  between operations  15.3 us (2%)
    all_gather x3, waiting for transfers between devices, both(): return lax.all_gather(arr, 'model', axis=0, tiled=True)  166 us
    reduce_scatter x1, waiting for transfers between devices, scatter_grads(): rows = lax.psum_scatter(grad_all, 'data', scatter_dimension=0, tiled=True)  56.3 us
    psum x1, blocking collectives, layer_shard(): small = lax.psum(small, ('model', 'data'))  32.6 us
    unnamed x192, local copies, waits for them, and re-layouts  32.2 us
    sub x1, other arithmetic, attn_fwd(): attn_probs = jax.nn.softmax(logits, axis=-1)  29.3 us
    eq x1, local copies, waits for them, and re-layouts, bucket_table(): bucket_ids[:, :, None] == jnp.arange(NUM_BUCKETS)  28 us
    dot_general x2, matrix products, attn_bwd(): jnp.einsum('bqhe,bkhe->bhqk', d_context, v_heads, preferred_element_type=...  27 us
    dot_general x8, matrix products, in_grad(): jnp.einsum('bsd,bshe->dhe', act_in, d_heads, preferred_element_type=jnp.f...  26.5 us
  transfers between devices with their start and end apart: 6, of which 5 were waited for; matrix products, arithmetic and copies ran while one was open for 12% of the time, Pallas kernels for 0%

profile of v1, /device:TPU:0, one launch (start us, length us, event | category | flops | bytes accessed | tf_op | source)
XLA Modules:
  0.0 794.1 jit_solution(14129857300439122554)
XLA Ops:
  8.6 13.1 %all-gather = bf16[128,3072]{1,0:T(8,128)(2,1)S(1)} all-gather(bf16[64,3072]{1,0:T(8,128)(2,1)S(1)} %concatenate.18), channel_id=2, replica_groups=mesh['model'=2,'data'=8] {'model'}, dimensions={0}, use_global_device_ids=true | all-gather | bytes 1179648 | tf_op jit(solution)/shard_map/all_gather | solution.py:99
  29.6 9.1 %all-gather.1 = bf16[8,64,3]{1,2,0:T(4,128)(2,1)S(1)} all-gather(bf16[1,64,3]{1,2,0:T(4,128)(2,1)S(1)} %maximum_bitcast_fusion), channel_id=1, replica_groups=mesh['model'=2,'data'=8] {'data'}, dimensions={0}, use_global_device_ids=true | all-gather | bytes 3456 | tf_op jit(solution)/shard_map/all_gather | solution.py:145
  48.5 28.0 %copy.151 = pred[384,384,32]{1,2,0:T(32,128)(4,1)} copy(pred[384,384,32]{0,2,1:T(32,128)(4,1)} %iota_compare_fusion) | data formatting | bytes 9437184 | tf_op jit(solution)/shard_map/eq | solution.py:18
  128.2 11.3 %convolution_convert_fusion.1 = bf16[8,6,384,384]{2,3,1,0:T(8,128)(2,1)} fusion(bf16[8,384,6,64]{1,3,2,0:T(8,128)(2,1)} %convolution_convert_fusion.12, bf16[8,384,6,64]{1,3,2,0:T(8,128)(2,1)} %convolution_convert_fusion.11), kind=kOutput, calls=%fused_computation.64 | convolution fusion | flops 913047552 | bytes 18874368 | tf_op jit(solution)/shard_map/bqhe,bkhe->bhqk/dot_general | solution.py:67
  139.5 29.3 %fusion.175 = (f32[8,6,384]{2,1,0:T(8,128)}, f32[8,6,384,384]{2,3,1,0:T(8,128)}) fusion(bf16[8,6,384,384]{2,3,1,0:T(8,128)(2,1)} %convolution_convert_fusion.1, f32[6,384,384]{1,2,0:T(8,128)} %copy.152, pred[384,384]{0,1:T(8,128)(4,1)S(1)} %copy-done.43), kind=kOutput, calls=%fused_computation.253 | output fusion | flops 56623488 | bytes 46227456 | tf_op jit(solution)/shard_map/sub | solution.py:69
  168.8 13.5 %fusion.113 = bf16[8,6,64,384]{3,2,1,0:T(8,128)(2,1)} fusion(bf16[8,384,6,64]{1,3,2,0:T(8,128)(2,1)} %convolution_convert_fusion.13, f32[8,6,384,384]{2,3,1,0:T(8,128)} %get-tuple-element.150, f32[8,6,384]{2,1,0:T(8,128)} %get-tuple-element.149), kind=kOutput, calls=%fused_computation.155 | convolution fusion | flops 921305088 | bytes 33103872 | tf_op jit(solution)/shard_map/bhqk,bkhe->bqhe/dot_general | solution.py:70
  201.3 7.6 convolution_convert_fusion.4
  215.8 16.1 %fusion.19 = (bf16[8,384,1024]{2,1,0:T(8,128)(2,1)}, bf16[8,384,1024]{2,1,0:T(8,128)(2,1)}) fusion(bf16[8,384,1024]{2,1,0:T(8,128)(2,1)} %convolution_convert_fusion.5, bf16[8,384,1024]{2,1,0:T(8,128)(2,1)} %convolution_convert_fusion.4, bf16[512,6144]{1,0:T(8,128)(2,1)S(1)} %bitcast.367, bf16[8,384,512]{2,1,0:T(8,128)(2,1)S(1)} %get-tuple-element.156, ...), kind=kOutput, calls=%fused_computation.36 | convolution fusion | flops 3306160128 | bytes 29374464 | tf_op jit(solution)/shard_map/bsd,df->bsf/dot_general | solution.py:171
  231.9 8.3 %fusion.151 = f32[8,384,512]{2,1,0:T(8,128)} fusion(bf16[8,384,1024]{2,1,0:T(8,128)(2,1)} %get-tuple-element.157, bf16[512,6144]{1,0:T(8,128)(2,1)S(1)} %bitcast.367), kind=kOutput, calls=%fused_computation.189 | convolution fusion | flops 3221225472 | bytes 13631488 | tf_op jit(solution)/shard_map/bsf,df->bsd/dot_general | solution.py:181
  240.2 12.0 %fusion.65 = (f32[512]{0:T(512)}, f32[8,384]{1,0:T(8,128)S(1)}, bf16[8,384,512]{2,1,0:T(8,128)(2,1)S(1)}) fusion(bf16[8,384,512]{2,1,0:T(8,128)(2,1)S(1)} %get-tuple-element.156, f32[8,384]{1,0:T(8,128)S(1)} %add_rsqrt_fusion, f32[512]{0:T(512)S(1)} %bitcast.413, f32[8,384,512]{2,1,0:T(8,128)} %fusion.151, bf16[512,6144]{1,0:T(8,128)(2,1)S(1)} %bitcast.367, ...), kind=kOutput, calls=%fused_computation.99 | convolution fusion | flops 3274699264 | bytes 26243072 | tf_op jit(solution)/shard_map/bsf,df->bsd/dot_general | solution.py:181
  266.0 9.0 %fusion.7 = (f32[8,6,384]{2,1,0:T(8,128)S(1)}, bf16[8,6,384,192]{2,3,1,0:T(8,128)(2,1)}) fusion(f32[8,6,384]{2,1,0:T(8,128)S(1)} %copy-done.28, f32[8,6,384]{2,1,0:T(8,128)S(1)} %copy-done.26, bf16[8,6,384,192]{2,3,1,0:T(8,128)(2,1)S(1)} %bitcast.355, bf16[8,384,6,64]{1,3,2,0:T(8,128)(2,1)} %copy-done.64, bf16[8,192,6,64]{1,3,2,0:T(8,128)(2,1)} %convolution_convert_fusion.15), kind=kOutput, calls=%fused_computation.22 | convolution fusion | flops 477739008 | bytes 17915904 | tf_op jit(solution)/shard_map/bqhe,bkhe->bhqk/dot_general | solution.py:75
  301.5 13.2 %fusion.116 = bf16[8,6,64,384]{3,2,1,0:T(8,128)(2,1)} fusion(bf16[8,384,6,64]{1,3,2,0:T(8,128)(2,1)S(1)} %fusion.110, f32[8,6,384,384]{2,3,1,0:T(8,128)} %get-tuple-element.150, f32[8,6,384]{2,1,0:T(8,128)S(1)} %copy-done.44), kind=kOutput, calls=%fused_computation.156 | convolution fusion | flops 921305088 | bytes 33103872 | tf_op jit(solution)/shard_map/bhqk,bqhe->bkhe/dot_general | solution.py:81
  314.7 18.0 %fusion.1 = (f32[8,6,384]{2,1,0:T(8,128)S(1)}, bf16[8,6,384,384]{2,3,1,0:T(8,128)(2,1)}) fusion(f32[8,6,384,384]{2,3,1,0:T(8,128)} %get-tuple-element.150, f32[8,6,384]{2,1,0:T(8,128)S(1)} %copy-done.44, bf16[8,384,6,64]{1,3,2,0:T(8,128)(2,1)} %copy-done.65, bf16[8,384,6,64]{1,3,2,0:T(8,128)(2,1)} %convolution_convert_fusion.13), kind=kOutput, calls=%fused_computation.3 | convolution fusion | flops 941340672 | bytes 47333376 | tf_op jit(solution)/shard_map/bqhe,bkhe->bhqk/dot_general | solution.py:75
  332.7 21.1 %fusion.5 = (bf16[6,384,384]{1,2,0:T(8,128)(2,1)}, bf16[8,6,384,384]{2,3,1,0:T(8,128)(2,1)}) fusion(bf16[8,6,384,384]{2,3,1,0:T(8,128)(2,1)} %get-tuple-element.164, f32[8,6,384]{2,1,0:T(8,128)S(1)} %get-tuple-element.163, f32[8,6,384,384]{2,3,1,0:T(8,128)} %get-tuple-element.150, f32[8,6,384]{2,1,0:T(8,128)S(1)} %copy-done.44), kind=kLoop, calls=%fused_computation.15 | loop fusion | flops 41582592 | bytes 58540032 | tf_op jit(solution)/shard_map/reduce_sum | solution.py:206
  353.8 12.3 %convolution_convert_fusion.7 = bf16[8,6,64,384]{3,2,1,0:T(8,128)(2,1)} fusion(bf16[8,384,6,64]{1,3,2,0:T(8,128)(2,1)} %convolution_convert_fusion.12, bf16[8,6,384,384]{2,3,1,0:T(8,128)(2,1)} %get-tuple-element.79), kind=kOutput, calls=%fused_computation.157 | convolution fusion | flops 907149312 | bytes 18874368 | tf_op jit(solution)/shard_map/bhqk,bqhe->bkhe/dot_general | solution.py:80
  366.0 9.5 %convolution_convert_fusion.8 = bf16[8,6,64,384]{3,2,1,0:T(8,128)(2,1)} fusion(bf16[8,384,6,64]{1,3,2,0:T(8,128)(2,1)} %convolution_convert_fusion.11, bf16[8,6,384,384]{2,3,1,0:T(8,128)(2,1)} %get-tuple-element.79), kind=kOutput, calls=%fused_computation.158 | convolution fusion | flops 907149312 | bytes 18874368 | tf_op jit(solution)/shard_map/bhqk,bkhe->bqhe/dot_general | solution.py:79
  429.6 11.1 %bitcast_dynamic-update-slice_fusion.1 = f32[512,6144]{1,0:T(8,128)} fusion(f32[512,6144]{1,0:T(8,128)} %bitcast_dynamic-update-slice_fusion.2, bf16[8,384,512]{2,1,0:T(8,128)(2,1)S(1)} %copy-done.17, f32[512]{0:T(512)S(1)} %bitcast.416, f32[8,384]{1,0:T(8,128)S(1)} %copy-done.48, bf16[8,384,1024]{2,1,0:T(8,128)(2,1)S(1)} %copy-done.69, ...), kind=kOutput, calls=%fused_computation.151 | convolution fusion | flops 3265265664 | bytes 17840128 | tf_op jit(solution)/shard_map/bsd,bsf->df/dot_general | solution.py:184
  440.7 9.6 %bitcast_dynamic-update-slice_fusion = f32[512,6144]{1,0:T(8,128)} fusion(f32[512,6144]{1,0:T(8,128)} %bitcast_dynamic-update-slice_fusion.1, bf16[16,384,512]{2,1,0:T(8,128)(2,1)S(1)} %bitcast.371, s32[]{:T(128)S(6)} %select_n.19, bf16[8,384,1024]{2,1,0:T(8,128)(2,1)S(1)} %bitcast.426, bf16[8,384,1024]{2,1,0:T(8,128)(2,1)} %get-tuple-element.158), kind=kOutput, calls=%fused_computation.150 | convolution fusion | flops 3258974208 | bytes 17825796 | tf_op jit(solution)/shard_map/bsd,bsf->df/dot_general | solution.py:184
  455.5 10.5 %fusion.67 = bf16[8,384,512]{2,1,0:T(8,128)(2,1)} fusion(bf16[8,384,512]{2,1,0:T(8,128)(2,1)S(1)} %copy-done.18, bf16[512,6144]{1,0:T(8,128)(2,1)} %all-gather.8.cloned.1.call-done, bf16[8,384,1024]{2,1,0:T(8,128)(2,1)} %convolution_convert_fusion.5, bf16[8,384,1024]{2,1,0:T(8,128)(2,1)} %get-tuple-element.158), kind=kOutput, calls=%fused_computation.101 | convolution fusion | flops 3263692800 | bytes 19922944 | tf_op jit(solution)/shard_map/bsf,df->bsd/dot_general | solution.py:175
  479.5 56.3 %reduce-scatter.3.cloned.1.call-done = f32[64,6144]{1,0:T(8,128)} async-done(((f32[512,6144]{1,0:T(8,128)}), f32[64,6144]{1,0:T(8,128)}) %reduce-scatter.3.cloned.1.call-update) | async-done | bytes 1572880 | tf_op jit(solution)/shard_map/reduce_scatter | solution.py:112
  545.0 32.6 %psum.7 = f32[1728]{0:T(1024)S(1)} all-reduce(f32[1728]{0:T(1024)S(1)} %pad_maximum_fusion.1), channel_id=1, replica_groups=mesh['model'=2,'data'=8] {'model','data'}, use_global_device_ids=true, to_apply=%region_17.18 | all-reduce | flops 1728 | bytes 13824 | tf_op jit(solution)/shard_map/psum | solution.py:215
  582.6 81.1 %all-gather.10.cloned.1.call-done = bf16[16,384,512]{2,1,0:T(8,128)(2,1)} async-done(((bf16[8,384,512]{2,1,0:T(8,128)(2,1)}), bf16[16,384,512]{2,1,0:T(8,128)(2,1)}) %all-gather.10.cloned.1.call-update) | async-done | bytes 6291472 | tf_op jit(solution)/shard_map/all_gather | solution.py:226
  663.7 81.1 %all-gather.12.cloned.1.call-done = bf16[16,384,512]{2,1,0:T(8,128)(2,1)} async-done(((bf16[8,384,512]{2,1,0:T(8,128)(2,1)}), bf16[16,384,512]{2,1,0:T(8,128)(2,1)}) %all-gather.12.cloned.1.call-update) | async-done | bytes 6291472 | tf_op jit(solution)/shard_map/all_gather | solution.py:226
  744.8 26.3 %reduce-scatter.5.cloned.1.call-done = f32[1,64,3072]{2,1,0:T(8,128)} async-done(((f32[2,64,3072]{2,1,0:T(8,128)}), f32[1,64,3072]{2,1,0:T(8,128)}) %reduce-scatter.5.cloned.1.call-update) | async-done | bytes 786448 | tf_op jit(solution)/shard_map/reduce_scatter | solution.py:120
  (307 shorter events, 238.8 us)
Async XLA Ops:
  7.2 103.4 %copy-start = (bf16[16,192,512]{2,1,0:T(8,128)(2,1)S(1)}, bf16[16,192,512]{2,1,0:T(8,128)(2,1)}, u32[]{:S(2)}) copy-start(bf16[16,192,512]{2,1,0:T(8,128)(2,1)} %param.20) | copy-start | bytes 9437188
  7.2 31.6 %copy-start.60 = (s32[15]{0:T(128)S(1)}, s32[15]{0:T(128)}, u32[]{:S(2)}) copy-start(s32[15]{0:T(128)} %constant.59.clone) | copy-start | bytes 184
  7.2 17.5 %copy-start.59 = (bf16[32,3]{0,1:T(4,128)(2,1)S(1)}, bf16[32,3]{0,1:T(4,128)(2,1)}, u32[]{:S(2)}) copy-start(bf16[32,3]{0,1:T(4,128)(2,1)} %param.22) | copy-start | bytes 580
  7.2 21.7 %copy-start.61 = (bf16[64]{0:T(256)(128)(2,1)S(1)}, bf16[64]{0:T(256)(128)(2,1)}, u32[]{:S(2)}) copy-start(bf16[64]{0:T(256)(128)(2,1)} %param.36) | copy-start | bytes 388
  7.2 21.7 %copy-start.62 = (bf16[64]{0:T(256)(128)(2,1)S(1)}, bf16[64]{0:T(256)(128)(2,1)}, u32[]{:S(2)}) copy-start(bf16[64]{0:T(256)(128)(2,1)} %param.35) | copy-start | bytes 388
  7.3 85.5 %all-gather.8.cloned.1.call-start = ((), (), s32[]{:S(2)}) async-start(), calls=%async_computation.2 | async-start | bytes 7077888 | tf_op jit(solution)/shard_map/all_gather | solution.py:108
  24.6 511.2 %reduce-scatter.3.cloned.1.call-start = ((), (), s32[]{:S(2)}) async-start(), calls=%async_computation.6 | async-start | bytes 14155776 | tf_op jit(solution)/shard_map/reduce_scatter | solution.py:112
  92.7 32.5 %copy-start.51 = (f32[1,512]{1,0:T(1,128)}, f32[1,512]{1,0:T(1,128)S(1)}, u32[]{:S(2)}) copy-start(f32[1,512]{1,0:T(1,128)S(1)} %get-tuple-element.145) | copy-start | bytes 6148
  92.7 32.5 %copy-start.45 = (f32[8,384]{1,0:T(8,128)}, f32[8,384]{1,0:T(8,128)S(1)}, u32[]{:S(2)}) copy-start(f32[8,384]{1,0:T(8,128)S(1)} %add_rsqrt_fusion.2) | copy-start | bytes 36868
  168.8 13.5 %copy-start.37 = (bf16[512,384]{0,1:T(8,128)(2,1)S(1)}, bf16[512,384]{0,1:T(8,128)(2,1)}, u32[]{:S(2)}) copy-start(bf16[512,384]{0,1:T(8,128)(2,1)} %copy.154) | copy-start | bytes 1179652
  201.2 51.0 %copy-start.16 = (bf16[8,384,512]{2,1,0:T(8,128)(2,1)}, bf16[8,384,512]{2,1,0:T(8,128)(2,1)S(1)}, u32[]{:S(2)}) copy-start(bf16[8,384,512]{2,1,0:T(8,128)(2,1)S(1)} %get-tuple-element.156) | copy-start | bytes 9437188
  201.3 51.0 %copy-start.47 = (f32[8,384]{1,0:T(8,128)}, f32[8,384]{1,0:T(8,128)S(1)}, u32[]{:S(2)}) copy-start(f32[8,384]{1,0:T(8,128)S(1)} %add_rsqrt_fusion) | copy-start | bytes 36868
  201.3 14.5 %slice-start.8 = ((s8[6291456]{0:T(1024)(128)(4,1)}), s8[4194304]{0:T(1024)(128)(4,1)S(1)}, s32[]{:S(2)}) async-start(s8[6291456]{0:T(1024)(128)(4,1)} %bitcast.366), calls=%async_computation.16 | async-start | bytes 8388608
  408.8 13.8 %copy-start.13 = (f32[512,384]{1,0:T(8,128)S(1)}, f32[512,384]{1,0:T(8,128)}, u32[]{:S(2)}) copy-start(f32[512,384]{1,0:T(8,128)} %copy.181) | copy-start | bytes 2359300
  408.8 14.8 %copy-start.12 = (f32[512,384]{1,0:T(8,128)S(1)}, f32[512,384]{1,0:T(8,128)}, u32[]{:S(2)}) copy-start(f32[512,384]{1,0:T(8,128)} %copy.182) | copy-start | bytes 2359300
  411.3 13.3 %copy-start.54 = (f32[1,512]{1,0:T(1,128)S(1)}, f32[1,512]{1,0:T(1,128)}, u32[]{:S(2)}) copy-start(f32[1,512]{1,0:T(1,128)} %get-tuple-element.143) | copy-start | bytes 6148
  411.3 13.3 %copy-start.66 = (bf16[8,384,1024]{2,1,0:T(8,128)(2,1)S(1)}, bf16[8,384,1024]{2,1,0:T(8,128)(2,1)}, u32[]{:S(2)}) copy-start(bf16[8,384,1024]{2,1,0:T(8,128)(2,1)} %get-tuple-element.157) | copy-start | bytes 18874372
  424.6 16.1 %slice-start.12 = ((s8[6291456]{0:T(1024)(128)(4,1)}), s8[4194304]{0:T(1024)(128)(4,1)S(1)}, s32[]{:S(2)}) async-start(s8[6291456]{0:T(1024)(128)(4,1)} %bitcast.370), calls=%async_computation.20 | async-start | bytes 8388608
  424.6 16.1 %slice-start.14 = ((s8[6291456]{0:T(1024)(128)(4,1)}), s8[4194304]{0:T(1024)(128)(4,1)S(1)}, s32[]{:S(2)}) async-start(s8[6291456]{0:T(1024)(128)(4,1)} %bitcast.425), calls=%async_computation.22 | async-start | bytes 8388608
  450.3 132.3 %all-gather.14.cloned.1.call-start = ((), (), s32[]{:S(2)}) async-start(), calls=%async_computation.5 | async-start | bytes 4718592 | tf_op jit(solution)/shard_map/all_gather | solution.py:226
  455.4 208.3 %all-gather.10.cloned.1.call-start = ((), (), s32[]{:S(2)}) async-start(), calls=%async_computation.3 | async-start | bytes 9437184 | tf_op jit(solution)/shard_map/all_gather | solution.py:226
  466.0 278.8 %all-gather.12.cloned.1.call-start = ((), (), s32[]{:S(2)}) async-start(), calls=%async_computation.4 | async-start | bytes 9437184 | tf_op jit(solution)/shard_map/all_gather | solution.py:226
  479.4 60.9 %copy-start.23 = (s32[384,384]{0,1:T(8,128)S(1)}, s32[384,384]{0,1:T(8,128)}, u32[]{:S(2)}) copy-start(s32[384,384]{0,1:T(8,128)} %copy.150) | copy-start | bytes 1769476
  479.4 291.7 %reduce-scatter.5.cloned.1.call-start = ((), (), s32[]{:S(2)}) async-start(), calls=%async_computation.7 | async-start | bytes 2359296 | tf_op jit(solution)/shard_map/reduce_scatter | solution.py:120
  (71 other events, 361.5 us)
Sparse Core Ops, SparseCore 0:
  24.8 42.6 all-gather.7
  450.4 85.3 reduce-scatter.2
  537.9 44.6 all-gather.13
  584.5 79.1 all-gather.9
  665.6 79.1 all-gather.11
  746.9 24.1 reduce-scatter.4

commit v2 on v1

v2 whole, which is shorter than its diff:
```python
import math
import jax
import jax.numpy as jnp
from jax import lax
from jax.experimental import pallas as pl
from jax.experimental.pallas import tpu as pltpu
from jax.sharding import PartitionSpec as P

EPS = 1e-6
NUM_BUCKETS = 32
MASK_VALUE = -1e9
BUCKET_EDGES = tuple(math.ceil(16 * 8.0 ** (bucket_no / 16.0)) for bucket_no in range(1, 16))


SEQ = 384
ENC = 192
DIM = 512
INNER = 384
FF = 1024
HEADS = 6
PAIRS = 3
QB = 128
CHUNK = 64
SEQS_STEP = 2
C_SQ, C_SO, C_CQ, C_CK, C_CO, C_I0, C_I1, C_WO, C_END = 0, 1152, 1536, 1920, 2688, 3072, 4096, 5120, 6144
BF = jnp.bfloat16
F32 = jnp.float32
GELU_C = math.sqrt(2.0 / math.pi)
GELU_K = 0.044715


def nn(a, b):
    return lax.dot_general(a, b, (((1,), (0,)), ((), ())), preferred_element_type=F32)


def nt(a, b):
    return lax.dot_general(a, b, (((1,), (1,)), ((), ())), preferred_element_type=F32)


def tn(a, b):
    return lax.dot_general(a, b, (((0,), (0,)), ((), ())), preferred_element_type=F32)


def unit_of(act_f):
    inv = lax.rsqrt(jnp.mean(act_f * act_f, axis=-1, keepdims=True) + EPS)
    return act_f * inv, inv


def head_mask(value, head, lane_idx):
    keep = (lane_idx < 64) if head == 0 else (lane_idx >= 64)
    return jnp.where(keep, value.astype(F32), 0.0).astype(BF)


def softmax_t(logits):
    top = jnp.max(logits, axis=0, keepdims=True)
    expd = jnp.exp(logits - top)
    return expd * (1.0 / jnp.sum(expd, axis=0, keepdims=True))


def seq_body(s, x_ref, e_ref, dy_ref, w_ref, gain_ref, bias_ref, y_ref, dx_ref, de_ref, dg_ref, db_ref,
             n1_s, n2_s, n3_s, dm1_s, dm2_s, qkv_s, dqkv_s, ctx_s, cq_s, ckv_s, dcq_s, dckv_s, cctx_s,
             hid_s, d01_s, x1_s, x2_s, dctx_s, pf_s, pt_s, cpf_s, cpt_s, ds_s, cds_s, km_s, vm_s):
    r0 = pl.multiple_of(s * SEQ, SEQ)
    e0 = pl.multiple_of(s * ENC, ENC)
    rows = pl.ds(r0, SEQ)
    erows = pl.ds(e0, ENC)

    def chunk_rows(off):
        return pl.ds(pl.multiple_of(r0 + off, CHUNK), CHUNK)

    chunks = range(0, SEQ, CHUNK)
    lane_idx = lax.broadcasted_iota(jnp.int32, (SEQ, QB), 1)
    tri = lax.broadcasted_iota(jnp.int32, (QB, QB), 0) <= lax.broadcasted_iota(jnp.int32, (QB, QB), 1)

    for off in chunks:
        unit, _ = unit_of(x_ref[chunk_rows(off), :].astype(F32))
        n1_s[chunk_rows(off), :] = (unit * gain_ref[0:1, :]).astype(BF)
    for col in range(0, 3 * INNER, INNER):
        qkv_s[:, col:col + INNER] = nn(n1_s[rows, :], w_ref[:, C_SQ + col:C_SQ + col + INNER]).astype(BF)

    def self_pair(hp, carry):
        o = pl.multiple_of(hp * QB, QB)
        k_pair = qkv_s[:, pl.ds(pl.multiple_of(INNER + o, QB), QB)]
        v_pair = qkv_s[:, pl.ds(pl.multiple_of(2 * INNER + o, QB), QB)]
        for head in range(2):
            km_s[head * SEQ:(head + 1) * SEQ, :] = head_mask(k_pair, head, lane_idx)
            vm_s[head * SEQ:(head + 1) * SEQ, :] = head_mask(v_pair, head, lane_idx)
        for head in range(2):
            for qb in range(3):
                n = QB * (qb + 1)
                logits = nt(km_s[head * SEQ:head * SEQ + n, :], qkv_s[qb * QB:(qb + 1) * QB, pl.ds(o, QB)])
                logits = logits.astype(BF).astype(F32) + bias_ref[2 * hp + head, SEQ - n:SEQ, :]
                diag = jnp.where(tri, logits[n - QB:n], MASK_VALUE)
                logits = diag if qb == 0 else jnp.concatenate([logits[:n - QB], diag], axis=0)
                probs = softmax_t(logits)
                pf_s[2 * hp + head, 0:n, qb * QB:(qb + 1) * QB] = probs
                pt_s[hp, head * SEQ:head * SEQ + n, qb * QB:(qb + 1) * QB] = probs.astype(BF)
        ctx_s[rows, pl.ds(o, QB)] = tn(pt_s[hp], vm_s[...]).astype(BF)
        return carry

    lax.fori_loop(0, PAIRS, self_pair, 0)

    delta = nt(ctx_s[rows, :], w_ref[:, C_SO:C_SO + INNER])
    for off in chunks:
        mid = (x_ref[chunk_rows(off), :].astype(F32) + delta[off:off + CHUNK]).astype(BF)
        x1_s[off:off + CHUNK, :] = mid
        unit, _ = unit_of(mid.astype(F32))
        n2_s[chunk_rows(off), :] = (unit * gain_ref[1:2, :]).astype(BF)
    cq_s[...] = nn(n2_s[rows, :], w_ref[:, C_CQ:C_CQ + INNER]).astype(BF)
    ckv_s[...] = nn(e_ref[erows, :], w_ref[:, C_CK:C_CK + 2 * INNER]).astype(BF)

    def cross_masks(o):
        k_pair = ckv_s[:, pl.ds(o, QB)]
        v_pair = ckv_s[:, pl.ds(pl.multiple_of(INNER + o, QB), QB)]
        for head in range(2):
            km_s[head * ENC:(head + 1) * ENC, :] = head_mask(k_pair, head, lane_idx[:ENC])
            vm_s[head * ENC:(head + 1) * ENC, :] = head_mask(v_pair, head, lane_idx[:ENC])

    def cross_pair(hp, carry):
        o = pl.multiple_of(hp * QB, QB)
        cross_masks(o)
        for head in range(2):
            for qb in range(3):
                cols = slice(qb * QB, (qb + 1) * QB)
                logits = nt(km_s[head * ENC:(head + 1) * ENC, :], cq_s[cols, pl.ds(o, QB)])
                probs = softmax_t(logits.astype(BF).astype(F32))
                cpf_s[2 * hp + head, :, cols] = probs
                cpt_s[hp, head * ENC:(head + 1) * ENC, cols] = probs.astype(BF)
        cctx_s[rows, pl.ds(o, QB)] = tn(cpt_s[hp], vm_s[0:2 * ENC, :]).astype(BF)
        return carry

    lax.fori_loop(0, PAIRS, cross_pair, 0)

    delta = nt(cctx_s[rows, :], w_ref[:, C_CO:C_CO + INNER])
    for off in chunks:
        mid = (x1_s[off:off + CHUNK, :].astype(F32) + delta[off:off + CHUNK]).astype(BF)
        x2_s[off:off + CHUNK, :] = mid
        unit, _ = unit_of(mid.astype(F32))
        n3_s[chunk_rows(off), :] = (unit * gain_ref[2:3, :]).astype(BF)
    step = 256
    for col in range(0, FF, step):
        pre_0 = nn(n3_s[rows, :], w_ref[:, C_I0 + col:C_I0 + col + step])
        pre_1 = nn(n3_s[rows, :], w_ref[:, C_I1 + col:C_I1 + col + step])
        d_hid = nn(dy_ref[rows, :], w_ref[:, C_WO + col:C_WO + col + step])
        for off in chunks:
            a0 = pre_0[off:off + CHUNK].astype(BF).astype(F32)
            a1 = pre_1[off:off + CHUNK].astype(BF).astype(F32)
            dh = d_hid[off:off + CHUNK].astype(BF).astype(F32)
            sq = a0 * a0
            half = 0.5 * jnp.tanh(a0 * (GELU_C + (GELU_C * GELU_K) * sq)) + 0.5
            gelu = a0 * half
            slope = half * (1.0 + (a0 - gelu) * (2.0 * GELU_C + (6.0 * GELU_C * GELU_K) * sq))
            hid_s[chunk_rows(off), col:col + step] = (gelu * a1).astype(BF)
            d01_s[chunk_rows(off), col:col + step] = (slope * (dh * a1)).astype(BF)
            d01_s[chunk_rows(off), FF + col:FF + col + step] = (dh * gelu).astype(BF)
    delta = nt(hid_s[rows, :], w_ref[:, C_WO:C_WO + FF])
    for off in chunks:
        y_ref[chunk_rows(off), :] = (x2_s[off:off + CHUNK, :].astype(F32) + delta[off:off + CHUNK]).astype(BF)

    def norm_back(d_norm, base, d_res, out, idx):
        total = dg_ref[8 * idx:8 * idx + 8, :]
        for off in chunks:
            d_n = d_norm[off:off + CHUNK].astype(BF).astype(F32)
            unit, inv = unit_of(base(off).astype(F32))
            total = total + jnp.sum((d_n * unit).reshape(CHUNK // 8, 8, DIM), axis=0)
            d_unit = d_n * gain_ref[idx:idx + 1, :]
            d_act = inv * (d_unit - unit * jnp.mean(d_unit * unit, axis=-1, keepdims=True))
            out[chunk_rows(off), :] = (d_res[chunk_rows(off), :].astype(F32) + d_act).astype(BF)
        dg_ref[8 * idx:8 * idx + 8, :] = total

    d_norm = nt(d01_s[rows, :], w_ref[:, C_I0:C_I0 + 2 * FF])
    norm_back(d_norm, lambda off: x2_s[off:off + CHUNK, :], dy_ref, dm2_s, 2)

    dctx_s[...] = nn(dm2_s[rows, :], w_ref[:, C_CO:C_CO + INNER]).astype(BF)

    def cross_pair_back(hp, carry):
        o = pl.multiple_of(hp * QB, QB)
        cross_masks(o)
        for head in range(2):
            for qb in range(3):
                cols = slice(qb * QB, (qb + 1) * QB)
                d_p = nt(vm_s[head * ENC:(head + 1) * ENC, :], dctx_s[cols, pl.ds(o, QB)]).astype(BF).astype(F32)
                probs = cpf_s[2 * hp + head, :, cols]
                d_l = probs * (d_p - jnp.sum(probs * d_p, axis=0, keepdims=True))
                cds_s[head * ENC:(head + 1) * ENC, cols] = d_l.astype(BF)
        dcq_s[rows, pl.ds(o, QB)] = tn(cds_s[...], km_s[0:2 * ENC, :]).astype(BF)
        d_k = nn(cds_s[...], cq_s[:, pl.ds(o, QB)])
        d_v = nn(cpt_s[hp], dctx_s[:, pl.ds(o, QB)])
        low = lane_idx[:ENC] < 64
        dckv_s[erows, pl.ds(o, QB)] = jnp.where(low, d_k[:ENC], d_k[ENC:]).astype(BF)
        dckv_s[erows, pl.ds(pl.multiple_of(INNER + o, QB), QB)] = jnp.where(low, d_v[:ENC], d_v[ENC:]).astype(BF)
        return carry

    lax.fori_loop(0, PAIRS, cross_pair_back, 0)
    d_norm = nt(dcq_s[rows, :], w_ref[:, C_CQ:C_CQ + INNER])
    de_ref[erows, :] = nt(dckv_s[erows, :], w_ref[:, C_CK:C_CK + 2 * INNER]).astype(BF)
    norm_back(d_norm, lambda off: x1_s[off:off + CHUNK, :], dm2_s, dm1_s, 1)

    dctx_s[...] = nn(dm1_s[rows, :], w_ref[:, C_SO:C_SO + INNER]).astype(BF)

    def self_pair_back(hp, carry):
        o = pl.multiple_of(hp * QB, QB)
        k_pair = qkv_s[:, pl.ds(pl.multiple_of(INNER + o, QB), QB)]
        v_pair = qkv_s[:, pl.ds(pl.multiple_of(2 * INNER + o, QB), QB)]
        for head in range(2):
            km_s[head * SEQ:(head + 1) * SEQ, :] = head_mask(k_pair, head, lane_idx)
            vm_s[head * SEQ:(head + 1) * SEQ, :] = head_mask(v_pair, head, lane_idx)
        for head in range(2):
            for qb in range(3):
                n = QB * (qb + 1)
                cols = slice(qb * QB, (qb + 1) * QB)
                d_p = nt(vm_s[head * SEQ:head * SEQ + n, :], dctx_s[cols, pl.ds(o, QB)]).astype(BF).astype(F32)
                probs = pf_s[2 * hp + head, 0:n, cols]
                d_l = probs * (d_p - jnp.sum(probs * d_p, axis=0, keepdims=True))
                db_ref[2 * hp + head, SEQ - n:SEQ, :] += d_l
                ds_s[head * SEQ:head * SEQ + n, cols] = d_l.astype(BF)
        dqkv_s[rows, pl.ds(o, QB)] = tn(ds_s[...], km_s[...]).astype(BF)
        d_k = nn(ds_s[...], qkv_s[:, pl.ds(o, QB)])
        d_v = nn(pt_s[hp], dctx_s[:, pl.ds(o, QB)])
        low = lane_idx < 64
        dqkv_s[rows, pl.ds(pl.multiple_of(INNER + o, QB), QB)] = jnp.where(low, d_k[:SEQ], d_k[SEQ:]).astype(BF)
        dqkv_s[rows, pl.ds(pl.multiple_of(2 * INNER + o, QB), QB)] = jnp.where(low, d_v[:SEQ], d_v[SEQ:]).astype(BF)
        return carry

    lax.fori_loop(0, PAIRS, self_pair_back, 0)
    d_norm = nt(dqkv_s[rows, :], w_ref[:, C_SQ:C_SQ + 3 * INNER])
    norm_back(d_norm, lambda off: x_ref[chunk_rows(off), :], dm1_s, dx_ref, 0)


SCRATCH = [
    ((2 * SEQ, DIM), BF),
    ((2 * SEQ, DIM), BF),
    ((2 * SEQ, DIM), BF),
    ((2 * SEQ, DIM), BF),
    ((2 * SEQ, DIM), BF),
    ((SEQ, 3 * INNER), BF),
    ((2 * SEQ, 3 * INNER), BF),
    ((2 * SEQ, INNER), BF),
    ((SEQ, INNER), BF),
    ((ENC, 2 * INNER), BF),
    ((2 * SEQ, INNER), BF),
    ((2 * ENC, 2 * INNER), BF),
    ((2 * SEQ, INNER), BF),
    ((2 * SEQ, FF), BF),
    ((2 * SEQ, 2 * FF), BF),
    ((SEQ, DIM), BF),
    ((SEQ, DIM), BF),
    ((SEQ, INNER), BF),
    ((HEADS, SEQ, SEQ), F32),
    ((PAIRS, 2 * SEQ, SEQ), BF),
    ((HEADS, ENC, SEQ), F32),
    ((PAIRS, 2 * ENC, SEQ), BF),
    ((2 * SEQ, SEQ), BF),
    ((2 * ENC, SEQ), BF),
    ((2 * SEQ, QB), BF),
    ((2 * SEQ, QB), BF),
]


def weight_grads(g_ref, e_ref, dy_ref, n1_s, n2_s, n3_s, dm1_s, dm2_s, dqkv_s, ctx_s, dcq_s, dckv_s, cctx_s, hid_s, d01_s):
    def add(act, d_out, col, width):
        for off in range(0, width, 384 if width % 384 == 0 else 512):
            size = 384 if width % 384 == 0 else 512
            g_ref[:, col + off:col + off + size] += tn(act[...], d_out[:, off:off + size])

    add(n3_s, d01_s, C_I0, 2 * FF)
    add(dy_ref, hid_s, C_WO, FF)
    add(dm2_s, cctx_s, C_CO, INNER)
    add(n2_s, dcq_s, C_CQ, INNER)
    add(e_ref, dckv_s, C_CK, 2 * INNER)
    add(dm1_s, ctx_s, C_SO, INNER)
    add(n1_s, dqkv_s, C_SQ, 3 * INNER)


def layer_kernel(x_ref, e_ref, dy_ref, w_ref, gain_ref, bias_ref, y_ref, dx_ref, de_ref, g_ref, dg_ref, db_ref, *scratch):
    (n1_s, n2_s, n3_s, dm1_s, dm2_s, qkv_s, dqkv_s, ctx_s, cq_s, ckv_s, dcq_s, dckv_s, cctx_s,
     hid_s, d01_s, x1_s, x2_s, dctx_s, pf_s, pt_s, cpf_s, cpt_s, ds_s, cds_s, km_s, vm_s) = scratch

    @pl.when(pl.program_id(0) == 0)
    def _():
        pt_s[...] = jnp.zeros_like(pt_s)
        ds_s[...] = jnp.zeros_like(ds_s)
        dg_ref[...] = jnp.zeros_like(dg_ref)
        db_ref[...] = jnp.zeros_like(db_ref)
        g_ref[...] = jnp.zeros_like(g_ref)

    def body(s, carry):
        seq_body(s, x_ref, e_ref, dy_ref, w_ref, gain_ref, bias_ref, y_ref, dx_ref, de_ref, dg_ref, db_ref, *scratch)
        return carry

    lax.fori_loop(0, SEQS_STEP, body, 0)
    weight_grads(g_ref, e_ref, dy_ref, n1_s, n2_s, n3_s, dm1_s, dm2_s, dqkv_s, ctx_s, dcq_s, dckv_s, cctx_s, hid_s, d01_s)


def pack_local(sq, sk, sv, so, cq, ck, cv, co, wi0, wi1, wo):
    return [sq, sk, sv, so.T, cq, ck, cv, co.T, wi0, wi1, wo.T]


def gather_weights(blocks):
    local = jnp.concatenate(blocks, axis=1)
    pair = lax.all_gather(local, "model", axis=0)
    cols = []
    off = 0
    for blk in blocks:
        width = blk.shape[1]
        cols.append(pair[0, :, off:off + width])
        cols.append(pair[1, :, off:off + width])
        off += width
    both = jnp.concatenate(cols, axis=1)
    return lax.all_gather(both, "data", axis=0, tiled=True)


def scatter_grads(grad_all, widths):
    rows = lax.psum_scatter(grad_all, "data", scatter_dimension=0, tiled=True)
    lo, hi = [], []
    off = 0
    for width in widths:
        lo.append(rows[:, off:off + width])
        hi.append(rows[:, off + width:off + 2 * width])
        off += 2 * width
    pair = jnp.stack([jnp.concatenate(lo, axis=1), jnp.concatenate(hi, axis=1)])
    mine = lax.psum_scatter(pair, "model", scatter_dimension=0)
    outs = []
    off = 0
    for width in widths:
        outs.append(mine[:, off:off + width])
        off += width
    return outs


def layer_call(x, e, dy, weights, gains, bias_t):
    steps = x.shape[0] // (SEQS_STEP * SEQ)
    blk = lambda rows: pl.BlockSpec((rows, DIM), lambda i: (i, 0))
    fixed = lambda arr_shape: pl.BlockSpec(arr_shape, lambda i: (0,) * len(arr_shape), pipeline_mode=pl.Buffered(1))
    rows, erows = SEQS_STEP * SEQ, SEQS_STEP * ENC
    outs = [jax.ShapeDtypeStruct(x.shape, BF), jax.ShapeDtypeStruct(x.shape, BF), jax.ShapeDtypeStruct(e.shape, BF),
            jax.ShapeDtypeStruct((DIM, C_END), F32), jax.ShapeDtypeStruct((24, DIM), F32), jax.ShapeDtypeStruct((HEADS, SEQ, QB), F32)]
    return pl.pallas_call(
        layer_kernel,
        out_shape=outs,
        grid=(steps,),
        in_specs=[blk(rows), blk(erows), blk(rows), fixed(weights.shape), fixed(gains.shape), fixed(bias_t.shape)],
        out_specs=[blk(rows), blk(rows), blk(erows), fixed((DIM, C_END)), fixed((24, DIM)), fixed((HEADS, SEQ, QB))],
        scratch_shapes=[pltpu.VMEM(*item) for item in SCRATCH],
        compiler_params=pltpu.CompilerParams(dimension_semantics=("arbitrary",), vmem_limit_bytes=67043328),
        name="layer",
    )(x, e, dy, weights, gains, bias_t)


def bias_table():
    dist = (SEQ - QB + jnp.arange(QB))[None, :] - jnp.arange(SEQ)[:, None]
    dist = jnp.maximum(dist, 0)
    edges = jnp.array(BUCKET_EDGES, dtype=jnp.int32)
    ids = jnp.minimum(dist, 16) + jnp.sum((dist[:, :, None] >= edges).astype(jnp.int32), axis=-1)
    return ids


def layer_shard(dec_in, enc_out, grad_out, rel_bias, self_q, self_k, self_v, self_o, cross_q, cross_k, cross_v, cross_o, mlp_wi_0, mlp_wi_1, mlp_wo, norm_self, norm_cross, norm_mlp):
    model_idx = lax.axis_index("model")
    data_idx = lax.axis_index("data")
    half = dec_in.shape[0] // 2

    def mine(arr):
        part = lax.dynamic_slice_in_dim(arr, model_idx * half, half, 0)
        return part.reshape(-1, arr.shape[2])

    blocks = pack_local(self_q, self_k, self_v, self_o, cross_q, cross_k, cross_v, cross_o, mlp_wi_0, mlp_wi_1, mlp_wo)
    widths = [blk.shape[1] for blk in blocks]
    weights = gather_weights(blocks)
    gains = lax.all_gather(jnp.stack([norm_self, norm_cross, norm_mlp]), "data", axis=1, tiled=True).astype(F32)
    bias_pair = lax.all_gather(rel_bias, "model", axis=1, tiled=True).astype(F32)
    ids = bias_table()
    hot = (ids[:, :, None] == jnp.arange(NUM_BUCKETS)).astype(F32)
    bias_t = jnp.einsum("car,rh->hca", hot, bias_pair, precision=lax.Precision.HIGHEST)
    dec_out, grad_dec, grad_enc, grad_all, gain_part, bias_rows = layer_call(mine(dec_in), mine(enc_out), mine(grad_out), weights, gains, bias_t)
    bias_part = jnp.einsum("car,hca->rh", hot, bias_rows, precision=lax.Precision.HIGHEST)
    gain_part = jnp.sum(gain_part.reshape(3, 8, DIM), axis=1)

    small = jnp.concatenate([gain_part.reshape(-1), bias_part.reshape(-1)])
    small = lax.psum(small, ("model", "data"))
    gain_sums = small[:3 * DIM].reshape(3, DIM)
    gain_len = norm_self.shape[0]
    gain_mine = lax.dynamic_slice_in_dim(gain_sums, data_idx * gain_len, gain_len, 1)
    bias_sum = small[3 * DIM:].reshape(bias_part.shape)
    grad_bias = lax.dynamic_slice_in_dim(bias_sum, model_idx * rel_bias.shape[1], rel_bias.shape[1], 1)

    o_sq, o_sk, o_sv, o_so, o_cq, o_ck, o_cv, o_co, o_i0, o_i1, o_wo = scatter_grads(grad_all, widths)

    def both(arr, length):
        return lax.all_gather(arr.reshape(half, length, DIM), "model", axis=0, tiled=True)

    return (both(dec_out, SEQ), both(grad_dec, SEQ), both(grad_enc, ENC), grad_bias, o_sq, o_sk, o_sv, o_so.T, o_cq, o_ck, o_cv, o_co.T, o_i0, o_i1, o_wo.T, gain_mine[0], gain_mine[1], gain_mine[2])


def solution(mesh):
    row_spec = P("data", None, None)
    col_in = P("data", "model")
    col_out = P("model", "data")
    gain_spec = P("data")
    bias_spec = P(None, "model")
    arg_specs = (row_spec, row_spec, row_spec, bias_spec, col_in, col_in, col_in, col_out, col_in, col_in, col_in, col_out, col_in, col_in, col_out, gain_spec, gain_spec, gain_spec)
    out_specs = (row_spec, row_spec, row_spec) + arg_specs[3:]
    return jax.shard_map(layer_shard, mesh=mesh, in_specs=arg_specs, out_specs=out_specs, check_vma=False)
```

time: 805 us -> 592 us (0.74); the launches traced: 794 us -> 591 us
  matrix products: 274 us -> 3.98 us
  Pallas kernels: 0 us -> 182 us
  other arithmetic: 83 us -> 1.76 us
  local copies, waits for them, and re-layouts: 114 us -> 36.7 us
  waiting for transfers between devices: 248 us -> 293 us
    dot_general x47 -> x2, matrix products: 274 us -> 3.98 us  [the longest x1 2.95 us: layer_shard(): jnp.einsum('car,hca->rh', hot, bias_rows, precision=lax.Precision.HIGHEST)]
    pallas_call x0 -> x1, Pallas kernels: none -> 182 us  [layer_call(): pl.pallas_call(layer_kernel, out_shape=outs, grid=(steps,), in_specs=[blk...]
    sub x1 -> x0, other arithmetic: 29.3 us -> none  [attn_fwd(): attn_probs = jax.nn.softmax(logits, axis=-1)]
    eq x1 -> x0, local copies, waits for them, and re-layouts: 28 us -> none  [bucket_table(): bucket_ids[:, :, None] == jnp.arange(NUM_BUCKETS)]
    reduce_scatter x1, waiting for transfers between devices: 56.3 us -> 83.4 us  [scatter_grads(): rows = lax.psum_scatter(grad_all, 'data', scatter_dimension=0, tiled=True)]
    reduce_sum x4 -> x2, other arithmetic: 27.4 us -> 0.4 us  [the longest x1 0.37 us: bias_table(): jnp.sum((dist[:, :, None] >= edges).astype(jnp.int32), axis=-1)]
    unnamed x192 -> x29, local copies, waits for them, and re-layouts: 32.2 us -> 13 us
    slice x10 -> x1, local copies, waits for them, and re-layouts: 17.8 us -> 0.01 us  [layer_shard(): bias_sum = small[3 * DIM:].reshape(bias_part.shape)]
  transfers between devices with their start and end apart: 6 -> 6, of which waited for: 5 -> 6; matrix products, arithmetic and copies ran while one was open for 12% -> 4% of each run, Pallas kernels for 0% -> 0%
where the time goes in v2:
time: 592 us; the launch traced here: 591 us
  waiting for transfers between devices  293 us (49%)
  Pallas kernels  182 us (31%)
  blocking collectives  59.2 us (10%)
  local copies, waits for them, and re-layouts  36.7 us (6%)
  between operations  14.4 us (2%)
    pallas_call x1, Pallas kernels, layer_call(): pl.pallas_call(layer_kernel, out_shape=outs, grid=(steps,), in_specs=[blk...  182 us
    all_gather x3, waiting for transfers between devices, both(): lax.all_gather(arr.reshape(half, length, DIM), 'model', axis=0, tiled=True)  164 us
    reduce_scatter x1, waiting for transfers between devices, scatter_grads(): rows = lax.psum_scatter(grad_all, 'data', scatter_dimension=0, tiled=True)  83.4 us
    psum x1, blocking collectives, layer_shard(): small = lax.psum(small, ('model', 'data'))  32.6 us
    reduce_scatter x1, waiting for transfers between devices, scatter_grads(): mine = lax.psum_scatter(pair, 'model', scatter_dimension=0)  26.9 us
    all_gather x1, waiting for transfers between devices, gather_weights(): return lax.all_gather(both, 'data', axis=0, tiled=True)  16.7 us
    all_gather x1, blocking collectives, gather_weights(): pair = lax.all_gather(local, 'model', axis=0)  13.2 us
    unnamed x29, local copies, waits for them, and re-layouts  13 us
  transfers between devices with their start and end apart: 6, of which 6 were waited for; matrix products, arithmetic and copies ran while one was open for 4% of the time, Pallas kernels for 0%

profile of v2, /device:TPU:0, one launch (start us, length us, event | category | flops | bytes accessed | tf_op | source)
XLA Modules:
  0.0 591.1 jit_solution(4936800570350859645)
XLA Ops:
  7.2 1.2 concatenate.15
  8.5 13.2 %all-gather = bf16[128,3072]{1,0:T(8,128)(2,1)S(1)} all-gather(bf16[64,3072]{1,0:T(8,128)(2,1)S(1)} %concatenate.15), channel_id=2, replica_groups=mesh['model'=2,'data'=8] {'model'}, dimensions={0}, use_global_device_ids=true | all-gather | bytes 1179648 | tf_op jit(solution)/shard_map/all_gather | solution.py:301
  23.2 4.2 all-gather.2
  27.5 9.1 %all-gather.1 = bf16[8,64,3]{1,2,0:T(4,128)(2,1)S(1)} all-gather(bf16[1,64,3]{1,2,0:T(4,128)(2,1)S(1)} %maximum_bitcast_fusion), channel_id=1, replica_groups=mesh['model'=2,'data'=8] {'data'}, dimensions={0}, use_global_device_ids=true | all-gather | bytes 3456 | tf_op jit(solution)/shard_map/all_gather | solution.py:370
  38.9 1.5 copy.63
  40.3 2.7 constant_dynamic-slice_fusion.3
  43.1 6.1 %constant_dynamic-slice_fusion.2 = (bf16[8,384,512]{2,1,0:T(8,128)(2,1)}, bf16[8,384,512]{2,1,0:T(8,128)(2,1)}) fusion(bf16[16,384,512]{2,1,0:T(8,128)(2,1)} %param.21, s32[]{:T(128)S(6)} %select_n.11, bf16[16,384,512]{2,1,0:T(8,128)(2,1)} %param.19), kind=kLoop, calls=%fused_computation.41 | loop fusion | bytes 12582916 | tf_op jit(solution)/shard_map/dynamic_slice | solution.py:364
  49.2 16.7 %all-gather.8.cloned.1.call-done.w_ref = bf16[512,6144]{1,0:T(8,128)(2,1)} async-done(((bf16[64,6144]{1,0:T(8,128)(2,1)}), bf16[512,6144]{1,0:T(8,128)(2,1)}) %all-gather.8.cloned.1.call-update) | async-done | bytes 6291472 | tf_op jit(solution)/shard_map/all_gather | solution.py:310
  65.9 182.3 %layer.1 = (bf16[3072,512]{1,0:T(8,128)(2,1)}, bf16[3072,512]{1,0:T(8,128)(2,1)}, bf16[1536,512]{1,0:T(8,128)(2,1)}, f32[512,6144]{1,0:T(8,128)}, f32[24,512]{1,0:T(8,128)}, /*index=5*/f32[6,384,128]{2,1,0:T(8,128)}) custom-call(bf16[3072,512]{1,0:T(8,128)(2,1)} %bitcast.91, bf16[1536,512]{1,0:T(8,128)(2,1)} %bitcast.94, bf16[3072,512]{1,0:T(8,128)(2,1)} %bitcast.90, ...), custom_call_target="tpu_custom_call" | custom-call | tf_op jit(solution)/shard_map/layer/pallas_call | solution.py:338
  250.2 83.4 %reduce-scatter.3.cloned.1.call-done = f32[64,6144]{1,0:T(8,128)} async-done(((f32[512,6144]{1,0:T(8,128)}), f32[64,6144]{1,0:T(8,128)}) %reduce-scatter.3.cloned.1.call-update) | async-done | bytes 1572880 | tf_op jit(solution)/shard_map/reduce_scatter | solution.py:314
  333.6 1.3 fusion.6
  334.9 2.2 fusion.7
  338.4 1.3 pad_maximum_fusion
  340.6 3.0 fusion.4
  343.6 32.6 %psum.7 = f32[1728]{0:T(1024)S(1)} all-reduce(f32[1728]{0:T(1024)S(1)} %pad_maximum_fusion.1), channel_id=1, replica_groups=mesh['model'=2,'data'=8] {'model','data'}, use_global_device_ids=true, to_apply=%region_2.0 | all-reduce | flops 1728 | bytes 13824 | tf_op jit(solution)/shard_map/psum | solution.py:380
  377.7 2.1 all-gather.14.cloned.1.call-done
  379.8 80.5 %all-gather.12.cloned.1.call-done = bf16[16,384,512]{2,1,0:T(8,128)(2,1)} async-done(((bf16[8,384,512]{2,1,0:T(8,128)(2,1)}), bf16[16,384,512]{2,1,0:T(8,128)(2,1)}) %all-gather.12.cloned.1.call-update) | async-done | bytes 6291472 | tf_op jit(solution)/shard_map/all_gather | solution.py:390
  460.4 81.1 %all-gather.10.cloned.1.call-done = bf16[16,384,512]{2,1,0:T(8,128)(2,1)} async-done(((bf16[8,384,512]{2,1,0:T(8,128)(2,1)}), bf16[16,384,512]{2,1,0:T(8,128)(2,1)}) %all-gather.10.cloned.1.call-update) | async-done | bytes 6291472 | tf_op jit(solution)/shard_map/all_gather | solution.py:390
  541.5 26.9 %reduce-scatter.5.cloned.1.call-done = f32[1,64,3072]{2,1,0:T(8,128)} async-done(((f32[2,64,3072]{2,1,0:T(8,128)}), f32[1,64,3072]{2,1,0:T(8,128)}) %reduce-scatter.5.cloned.1.call-update) | async-done | bytes 786448 | tf_op jit(solution)/shard_map/reduce_scatter | solution.py:322
  568.3 1.8 slice_bitcast_fusion
  570.1 2.1 slice_bitcast_fusion.1
  572.2 6.2 %copy.73 = bf16[16,384,512]{2,1,0:T(8,128)(2,1)} copy(bf16[16,384,512]{2,1,0:T(8,128)(2,1)} %all-gather.10.cloned.1.call-done) | data formatting | bytes 12582912
  578.4 3.2 copy.74
  582.6 1.7 copy.75
  (64 shorter events, 10.4 us)
Async XLA Ops:
  7.2 58.7 %all-gather.8.cloned.1.call-start = ((), (), s32[]{:S(2)}) async-start(), calls=%async_computation.2 | async-start | bytes 7077888 | tf_op jit(solution)/shard_map/all_gather | solution.py:310
  8.4 14.7 %copy-start.5 = (bf16[32,3]{0,1:T(4,128)(2,1)S(1)}, bf16[32,3]{0,1:T(4,128)(2,1)}, u32[]{:S(2)}) copy-start(bf16[32,3]{0,1:T(4,128)(2,1)} %param.22) | copy-start | bytes 580
  8.4 19.0 %copy-start.7 = (bf16[64]{0:T(256)(128)(2,1)S(1)}, bf16[64]{0:T(256)(128)(2,1)}, u32[]{:S(2)}) copy-start(bf16[64]{0:T(256)(128)(2,1)} %param.36) | copy-start | bytes 388
  8.5 19.0 %copy-start.8 = (bf16[64]{0:T(256)(128)(2,1)S(1)}, bf16[64]{0:T(256)(128)(2,1)}, u32[]{:S(2)}) copy-start(bf16[64]{0:T(256)(128)(2,1)} %param.35) | copy-start | bytes 388
  8.5 19.0 %copy-start.9 = (bf16[64]{0:T(256)(128)(2,1)S(1)}, bf16[64]{0:T(256)(128)(2,1)}, u32[]{:S(2)}) copy-start(bf16[64]{0:T(256)(128)(2,1)} %param.34) | copy-start | bytes 388
  8.5 28.8 %copy-start.6 = (s32[15]{0:T(128)S(1)}, s32[15]{0:T(128)}, u32[]{:S(2)}) copy-start(s32[15]{0:T(128)} %constant.31.clone) | copy-start | bytes 184
  23.1 310.5 %reduce-scatter.3.cloned.1.call-start = ((), (), s32[]{:S(2)}) async-start(), calls=%async_computation.6 | async-start | bytes 14155776 | tf_op jit(solution)/shard_map/reduce_scatter | solution.py:314
  37.8 5.2 copy-start.2
  248.2 131.6 %all-gather.14.cloned.1.call-start = ((), (), s32[]{:S(2)}) async-start(), calls=%async_computation.5 | async-start | bytes 4718592 | tf_op jit(solution)/shard_map/all_gather | solution.py:390
  249.0 211.4 %all-gather.12.cloned.1.call-start = ((), (), s32[]{:S(2)}) async-start(), calls=%async_computation.4 | async-start | bytes 9437184 | tf_op jit(solution)/shard_map/all_gather | solution.py:390
  249.5 291.9 %all-gather.10.cloned.1.call-start = ((), (), s32[]{:S(2)}) async-start(), calls=%async_computation.3 | async-start | bytes 9437184 | tf_op jit(solution)/shard_map/all_gather | solution.py:390
  250.1 318.2 %reduce-scatter.5.cloned.1.call-start = ((), (), s32[]{:S(2)}) async-start(), calls=%async_computation.7 | async-start | bytes 2359296 | tf_op jit(solution)/shard_map/reduce_scatter | solution.py:322
  337.2 2.5 copy-start.1
  338.4 1.3 copy-start.4
  339.6 0.9 copy-start.3
  570.1 8.3 %slice-start = ((s8[6291456]{0:T(1024)(128)(4,1)}), s8[4194304]{0:T(1024)(128)(4,1)S(1)}, s32[]{:S(2)}) async-start(s8[6291456]{0:T(1024)(128)(4,1)} %bitcast.92), calls=%async_computation.8 | async-start | bytes 8388608
  572.2 6.2 %slice-start.1 = ((s8[6291456]{0:T(1024)(128)(4,1)}), s8[2097152]{0:T(1024)(128)(4,1)S(1)}, s32[]{:S(2)}) async-start(s8[6291456]{0:T(1024)(128)(4,1)} %bitcast.92), calls=%async_computation.9 | async-start | bytes 4194304
  578.4 4.2 copy-start
Sparse Core Ops, SparseCore 0:
  23.2 42.6 all-gather.7
  248.4 85.2 reduce-scatter.2
  335.1 44.6 all-gather.13
  381.2 79.1 all-gather.11
  462.3 79.1 all-gather.9
  544.1 24.1 reduce-scatter.4

commit v3 on v2

--- a/solution.py
+++ b/solution.py
@@ -27,6 +27,7 @@
 F32 = jnp.float32
 GELU_C = math.sqrt(2.0 / math.pi)
 GELU_K = 0.044715
+MESH = pl.DeviceIdType.MESH
 
 
 def nn(a, b):
@@ -57,7 +58,7 @@
     return expd * (1.0 / jnp.sum(expd, axis=0, keepdims=True))
 
 
-def seq_body(s, x_ref, e_ref, dy_ref, w_ref, gain_ref, bias_ref, y_ref, dx_ref, de_ref, dg_ref, db_ref,
+def seq_body(s, exchange, x_ref, e_ref, dy_ref, w_ref, gain_ref, bias_ref, y_buf, dx_buf, de_buf, dg_ref, db_ref,
              n1_s, n2_s, n3_s, dm1_s, dm2_s, qkv_s, dqkv_s, ctx_s, cq_s, ckv_s, dcq_s, dckv_s, cctx_s,
              hid_s, d01_s, x1_s, x2_s, dctx_s, pf_s, pt_s, cpf_s, cpt_s, ds_s, cds_s, km_s, vm_s):
     r0 = pl.multiple_of(s * SEQ, SEQ)
@@ -69,6 +70,7 @@
         return pl.ds(pl.multiple_of(r0 + off, CHUNK), CHUNK)
 
     chunks = range(0, SEQ, CHUNK)
+    slot, wait_slot, send = exchange
     lane_idx = lax.broadcasted_iota(jnp.int32, (SEQ, QB), 1)
     tri = lax.broadcasted_iota(jnp.int32, (QB, QB), 0) <= lax.broadcasted_iota(jnp.int32, (QB, QB), 1)
 
@@ -154,8 +156,10 @@
             d01_s[chunk_rows(off), col:col + step] = (slope * (dh * a1)).astype(BF)
             d01_s[chunk_rows(off), FF + col:FF + col + step] = (dh * gelu).astype(BF)
     delta = nt(hid_s[rows, :], w_ref[:, C_WO:C_WO + FF])
+    wait_slot(0)
     for off in chunks:
-        y_ref[chunk_rows(off), :] = (x2_s[off:off + CHUNK, :].astype(F32) + delta[off:off + CHUNK]).astype(BF)
+        y_buf[slot, off:off + CHUNK, :] = (x2_s[off:off + CHUNK, :].astype(F32) + delta[off:off + CHUNK]).astype(BF)
+    send(0)
 
     def norm_back(d_norm, base, d_res, out, idx):
         total = dg_ref[8 * idx:8 * idx + 8, :]
@@ -165,11 +169,11 @@
             total = total + jnp.sum((d_n * unit).reshape(CHUNK // 8, 8, DIM), axis=0)
             d_unit = d_n * gain_ref[idx:idx + 1, :]
             d_act = inv * (d_unit - unit * jnp.mean(d_unit * unit, axis=-1, keepdims=True))
-            out[chunk_rows(off), :] = (d_res[chunk_rows(off), :].astype(F32) + d_act).astype(BF)
+            out(off)[...] = (d_res[chunk_rows(off), :].astype(F32) + d_act).astype(BF)
         dg_ref[8 * idx:8 * idx + 8, :] = total
 
     d_norm = nt(d01_s[rows, :], w_ref[:, C_I0:C_I0 + 2 * FF])
-    norm_back(d_norm, lambda off: x2_s[off:off + CHUNK, :], dy_ref, dm2_s, 2)
+    norm_back(d_norm, lambda off: x2_s[off:off + CHUNK, :], dy_ref, lambda off: dm2_s.at[chunk_rows(off), :], 2)
 
     dctx_s[...] = nn(dm2_s[rows, :], w_ref[:, C_CO:C_CO + INNER]).astype(BF)
 
@@ -193,8 +197,10 @@
 
     lax.fori_loop(0, PAIRS, cross_pair_back, 0)
     d_norm = nt(dcq_s[rows, :], w_ref[:, C_CQ:C_CQ + INNER])
-    de_ref[erows, :] = nt(dckv_s[erows, :], w_ref[:, C_CK:C_CK + 2 * INNER]).astype(BF)
-    norm_back(d_norm, lambda off: x1_s[off:off + CHUNK, :], dm2_s, dm1_s, 1)
+    wait_slot(2)
+    de_buf[slot] = nt(dckv_s[erows, :], w_ref[:, C_CK:C_CK + 2 * INNER]).astype(BF)
+    send(2)
+    norm_back(d_norm, lambda off: x1_s[off:off + CHUNK, :], dm2_s, lambda off: dm1_s.at[chunk_rows(off), :], 1)
 
     dctx_s[...] = nn(dm1_s[rows, :], w_ref[:, C_SO:C_SO + INNER]).astype(BF)
 
@@ -224,7 +230,9 @@
 
     lax.fori_loop(0, PAIRS, self_pair_back, 0)
     d_norm = nt(dqkv_s[rows, :], w_ref[:, C_SQ:C_SQ + 3 * INNER])
-    norm_back(d_norm, lambda off: x_ref[chunk_rows(off), :], dm1_s, dx_ref, 0)
+    wait_slot(1)
+    norm_back(d_norm, lambda off: x_ref[chunk_rows(off), :], dm1_s, lambda off: dx_buf.at[slot, off:off + CHUNK, :], 0)
+    send(1)
 
 
 SCRATCH = [
@@ -272,32 +280,82 @@
     add(n1_s, dqkv_s, C_SQ, 3 * INNER)
 
 
-def layer_kernel(x_ref, e_ref, dy_ref, w_ref, gain_ref, bias_ref, y_ref, dx_ref, de_ref, g_ref, dg_ref, db_ref, *scratch):
+def layer_kernel(x_ref, e_ref, dy_ref, w_ref, gain_ref, bias_ref, y_hbm, dx_hbm, de_hbm, g_ref, dg_ref, db_ref, *scratch):
+    *scratch, y_buf, dx_buf, de_buf, local_sem, send_sem, recv_sem = scratch
     (n1_s, n2_s, n3_s, dm1_s, dm2_s, qkv_s, dqkv_s, ctx_s, cq_s, ckv_s, dcq_s, dckv_s, cctx_s,
      hid_s, d01_s, x1_s, x2_s, dctx_s, pf_s, pt_s, cpf_s, cpt_s, ds_s, cds_s, km_s, vm_s) = scratch
-
-    @pl.when(pl.program_id(0) == 0)
+    me = lax.axis_index("model")
+    other = 1 - me
+    step = pl.program_id(0)
+    seqs = SEQS_STEP * pl.num_programs(0)
+    bufs = ((y_buf, y_hbm, SEQ), (dx_buf, dx_hbm, SEQ), (de_buf, de_hbm, ENC))
+
+    @pl.when(step == 0)
     def _():
+        barrier = pltpu.get_barrier_semaphore()
+        pl.semaphore_signal(barrier, inc=1, device_id={"model": other}, device_id_type=MESH)
+        pl.semaphore_wait(barrier, 1)
         pt_s[...] = jnp.zeros_like(pt_s)
         ds_s[...] = jnp.zeros_like(ds_s)
         dg_ref[...] = jnp.zeros_like(dg_ref)
         db_ref[...] = jnp.zeros_like(db_ref)
         g_ref[...] = jnp.zeros_like(g_ref)
 
+    def copies(which, number):
+        buf, hbm, length = bufs[which]
+        slot = lax.rem(number, 2)
+        rows = pl.ds(pl.multiple_of((me * seqs + number) * length, length), length)
+        local = pltpu.make_async_copy(buf.at[slot], hbm.at[rows, :], local_sem.at[which, slot])
+        remote = pltpu.make_async_remote_copy(
+            src_ref=buf.at[slot], dst_ref=hbm.at[rows, :], send_sem=send_sem.at[which, slot],
+            recv_sem=recv_sem.at[which, number], device_id={"model": other}, device_id_type=MESH)
+        return local, remote
+
     def body(s, carry):
-        seq_body(s, x_ref, e_ref, dy_ref, w_ref, gain_ref, bias_ref, y_ref, dx_ref, de_ref, dg_ref, db_ref, *scratch)
+        number = step * SEQS_STEP + s
+
+        def wait_slot(which):
+            @pl.when(number >= 2)
+            def _():
+                local, remote = copies(which, number - 2)
+                local.wait()
+                remote.wait_send()
+
+        def send(which):
+            local, remote = copies(which, number)
+            remote.start()
+            local.start()
+
+        seq_body(s, (lax.rem(number, 2), wait_slot, send), x_ref, e_ref, dy_ref, w_ref, gain_ref, bias_ref, y_buf, dx_buf, de_buf, dg_ref, db_ref, *scratch)
         return carry
 
     lax.fori_loop(0, SEQS_STEP, body, 0)
     weight_grads(g_ref, e_ref, dy_ref, n1_s, n2_s, n3_s, dm1_s, dm2_s, dqkv_s, ctx_s, dcq_s, dckv_s, cctx_s, hid_s, d01_s)
 
+    @pl.when(step == pl.num_programs(0) - 1)
+    def _():
+        for which in range(3):
+            for back in (2, 1):
+                local, remote = copies(which, seqs - back)
+                local.wait()
+                remote.wait_send()
+
+            def arrived(number, carry):
+                copies(which, number)[1].wait_recv()
+                return carry
+
+            lax.fori_loop(0, seqs, arrived, 0)
+
 
 def pack_local(sq, sk, sv, so, cq, ck, cv, co, wi0, wi1, wo):
     return [sq, sk, sv, so.T, cq, ck, cv, co.T, wi0, wi1, wo.T]
 
 
-def gather_weights(blocks):
-    local = jnp.concatenate(blocks, axis=1)
+def gather_weights(blocks, gains, rel_bias):
+    rows, heads_dev = gains.shape[1], rel_bias.shape[1]
+    extra = jnp.concatenate([gains.T, jnp.pad(rel_bias, ((0, rows - rel_bias.shape[0]), (0, 0)))], axis=1)
+    extra = jnp.pad(extra, ((0, 0), (0, QB - extra.shape[1])))
+    local = jnp.concatenate(blocks + [extra], axis=1)
     pair = lax.all_gather(local, "model", axis=0)
     cols = []
     off = 0
@@ -306,18 +364,27 @@
         cols.append(pair[0, :, off:off + width])
         cols.append(pair[1, :, off:off + width])
         off += width
+    cols += [pair[0, :, off:off + 3 + heads_dev], pair[1, :, off + 3:off + QB - heads_dev]]
     both = jnp.concatenate(cols, axis=1)
-    return lax.all_gather(both, "data", axis=0, tiled=True)
-
-
-def scatter_grads(grad_all, widths):
-    rows = lax.psum_scatter(grad_all, "data", scatter_dimension=0, tiled=True)
+    full = lax.all_gather(both, "data", axis=0, tiled=True)
+    return full, full[:, 2 * off:2 * off + 3].T, full[:NUM_BUCKETS, 2 * off + 3:2 * off + 3 + 2 * heads_dev]
+
+
+def scatter_grads(grad_all, gain_part, bias_part, widths):
+    blocks = grad_all.shape[0] // 64
+    rep_bias = jnp.tile(jnp.pad(bias_part, ((0, 64 - bias_part.shape[0]), (0, 0))), (blocks, 1))
+    extra = jnp.concatenate([gain_part.T, rep_bias], axis=1)
+    extra = jnp.pad(extra, ((0, 0), (0, QB - extra.shape[1])))
+    heads_dev = bias_part.shape[1] // 2
+    rows = lax.psum_scatter(jnp.concatenate([grad_all, extra], axis=1), "data", scatter_dimension=0, tiled=True)
     lo, hi = [], []
     off = 0
     for width in widths:
         lo.append(rows[:, off:off + width])
         hi.append(rows[:, off + width:off + 2 * width])
         off += 2 * width
+    lo.append(rows[:, off:off + QB])
+    hi += [rows[:, off:off + 3], rows[:, off + 3 + heads_dev:off + QB], rows[:, :heads_dev]]
     pair = jnp.stack([jnp.concatenate(lo, axis=1), jnp.concatenate(hi, axis=1)])
     mine = lax.psum_scatter(pair, "model", scatter_dimension=0)
     outs = []
@@ -325,24 +392,28 @@
     for width in widths:
         outs.append(mine[:, off:off + width])
         off += width
-    return outs
+    return outs, mine[:, off:off + 3], mine[:NUM_BUCKETS, off + 3:off + 3 + heads_dev]
 
 
 def layer_call(x, e, dy, weights, gains, bias_t):
-    steps = x.shape[0] // (SEQS_STEP * SEQ)
-    blk = lambda rows: pl.BlockSpec((rows, DIM), lambda i: (i, 0))
+    steps = x.shape[0] // (2 * SEQS_STEP * SEQ)
+    part = lambda rows: pl.BlockSpec((rows, DIM), lambda i: (lax.axis_index("model") * steps + i, 0))
     fixed = lambda arr_shape: pl.BlockSpec(arr_shape, lambda i: (0,) * len(arr_shape), pipeline_mode=pl.Buffered(1))
+    anywhere = pl.BlockSpec(memory_space=pl.ANY)
     rows, erows = SEQS_STEP * SEQ, SEQS_STEP * ENC
+    seqs = SEQS_STEP * steps
     outs = [jax.ShapeDtypeStruct(x.shape, BF), jax.ShapeDtypeStruct(x.shape, BF), jax.ShapeDtypeStruct(e.shape, BF),
             jax.ShapeDtypeStruct((DIM, C_END), F32), jax.ShapeDtypeStruct((24, DIM), F32), jax.ShapeDtypeStruct((HEADS, SEQ, QB), F32)]
     return pl.pallas_call(
         layer_kernel,
         out_shape=outs,
         grid=(steps,),
-        in_specs=[blk(rows), blk(erows), blk(rows), fixed(weights.shape), fixed(gains.shape), fixed(bias_t.shape)],
-        out_specs=[blk(rows), blk(rows), blk(erows), fixed((DIM, C_END)), fixed((24, DIM)), fixed((HEADS, SEQ, QB))],
-        scratch_shapes=[pltpu.VMEM(*item) for item in SCRATCH],
-        compiler_params=pltpu.CompilerParams(dimension_semantics=("arbitrary",), vmem_limit_bytes=67043328),
+        in_specs=[part(rows), part(erows), part(rows), pl.BlockSpec((DIM, C_END), lambda i: (0, 0), pipeline_mode=pl.Buffered(1)), fixed(gains.shape), fixed(bias_t.shape)],
+        out_specs=[anywhere, anywhere, anywhere, fixed((DIM, C_END)), fixed((24, DIM)), fixed((HEADS, SEQ, QB))],
+        scratch_shapes=[pltpu.VMEM(*item) for item in SCRATCH] + [
+            pltpu.VMEM((2, SEQ, DIM), BF), pltpu.VMEM((2, SEQ, DIM), BF), pltpu.VMEM((2, ENC, DIM), BF),
+            pltpu.SemaphoreType.DMA((3, 2)), pltpu.SemaphoreType.DMA((3, 2)), pltpu.SemaphoreType.DMA((3, seqs))],
+        compiler_params=pltpu.CompilerParams(dimension_semantics=("arbitrary",), vmem_limit_bytes=67043328, collective_id=0, has_side_effects=True),
         name="layer",
     )(x, e, dy, weights, gains, bias_t)
 
@@ -356,40 +427,22 @@
 
 
 def layer_shard(dec_in, enc_out, grad_out, rel_bias, self_q, self_k, self_v, self_o, cross_q, cross_k, cross_v, cross_o, mlp_wi_0, mlp_wi_1, mlp_wo, norm_self, norm_cross, norm_mlp):
-    model_idx = lax.axis_index("model")
-    data_idx = lax.axis_index("data")
-    half = dec_in.shape[0] // 2
-
-    def mine(arr):
-        part = lax.dynamic_slice_in_dim(arr, model_idx * half, half, 0)
-        return part.reshape(-1, arr.shape[2])
-
     blocks = pack_local(self_q, self_k, self_v, self_o, cross_q, cross_k, cross_v, cross_o, mlp_wi_0, mlp_wi_1, mlp_wo)
     widths = [blk.shape[1] for blk in blocks]
-    weights = gather_weights(blocks)
-    gains = lax.all_gather(jnp.stack([norm_self, norm_cross, norm_mlp]), "data", axis=1, tiled=True).astype(F32)
-    bias_pair = lax.all_gather(rel_bias, "model", axis=1, tiled=True).astype(F32)
+    weights, gains, bias_pair = gather_weights(blocks, jnp.stack([norm_self, norm_cross, norm_mlp]), rel_bias)
     ids = bias_table()
     hot = (ids[:, :, None] == jnp.arange(NUM_BUCKETS)).astype(F32)
-    bias_t = jnp.einsum("car,rh->hca", hot, bias_pair, precision=lax.Precision.HIGHEST)
-    dec_out, grad_dec, grad_enc, grad_all, gain_part, bias_rows = layer_call(mine(dec_in), mine(enc_out), mine(grad_out), weights, gains, bias_t)
+    bias_t = jnp.einsum("car,rh->hca", hot, bias_pair.astype(F32), precision=lax.Precision.HIGHEST)
+
+    def flat(arr):
+        return arr.reshape(-1, DIM)
+
+    dec_out, grad_dec, grad_enc, grad_all, gain_part, bias_rows = layer_call(flat(dec_in), flat(enc_out), flat(grad_out), weights, gains.astype(F32), bias_t)
     bias_part = jnp.einsum("car,hca->rh", hot, bias_rows, precision=lax.Precision.HIGHEST)
     gain_part = jnp.sum(gain_part.reshape(3, 8, DIM), axis=1)
-
-    small = jnp.concatenate([gain_part.reshape(-1), bias_part.reshape(-1)])
-    small = lax.psum(small, ("model", "data"))
-    gain_sums = small[:3 * DIM].reshape(3, DIM)
-    gain_len = norm_self.shape[0]
-    gain_mine = lax.dynamic_slice_in_dim(gain_sums, data_idx * gain_len, gain_len, 1)
-    bias_sum = small[3 * DIM:].reshape(bias_part.shape)
-    grad_bias = lax.dynamic_slice_in_dim(bias_sum, model_idx * rel_bias.shape[1], rel_bias.shape[1], 1)
-
-    o_sq, o_sk, o_sv, o_so, o_cq, o_ck, o_cv, o_co, o_i0, o_i1, o_wo = scatter_grads(grad_all, widths)
-
-    def both(arr, length):
-        return lax.all_gather(arr.reshape(half, length, DIM), "model", axis=0, tiled=True)
-
-    return (both(dec_out, SEQ), both(grad_dec, SEQ), both(grad_enc, ENC), grad_bias, o_sq, o_sk, o_sv, o_so.T, o_cq, o_ck, o_cv, o_co.T, o_i0, o_i1, o_wo.T, gain_mine[0], gain_mine[1], gain_mine[2])
+    grads, d_gains, grad_bias = scatter_grads(grad_all, gain_part, bias_part, widths)
+    o_sq, o_sk, o_sv, o_so, o_cq, o_ck, o_cv, o_co, o_i0, o_i1, o_wo = grads
+    return (dec_out.reshape(dec_in.shape), grad_dec.reshape(dec_in.shape), grad_enc.reshape(enc_out.shape), grad_bias, o_sq, o_sk, o_sv, o_so.T, o_cq, o_ck, o_cv, o_co.T, o_i0, o_i1, o_wo.T, d_gains[:, 0], d_gains[:, 1], d_gains[:, 2])
 
 
 def solution(mesh):

time: 592 us -> 436 us (0.74)
  waiting for transfers between devices: 293 us -> 144 us
  blocking collectives: 59.2 us -> 13.5 us
  Pallas kernels: 182 us -> 200 us
  other arithmetic: 1.76 us -> 15.9 us
    all_gather x4 -> x1, waiting for transfers between devices: 181 us -> 32.6 us  [gather_weights(): full = lax.all_gather(both, 'data', axis=0, tiled=True)]
    psum x1 -> x0, blocking collectives: 32.6 us -> none  [layer_shard(): small = lax.psum(small, ('model', 'data'))]
    pallas_call x1, Pallas kernels: 182 us -> 200 us  [layer_call(): pl.pallas_call(layer_kernel, out_shape=outs, grid=(steps,), in_specs=[par...]
    all_gather x2 -> x0, blocking collectives: 13.3 us -> none  [the longest x1 9.09 us: layer_shard(): lax.all_gather(jnp.stack([norm_self, norm_cross, norm_mlp]), 'data', axis...]
    concatenate x1 -> x3, other arithmetic: 0.01 us -> 10.9 us  [the longest x1 10.2 us: scatter_grads(): jnp.concatenate([grad_all, extra], axis=1)]
    dynamic_slice x4 -> x0, local copies, waits for them, and re-layouts: 8.99 us -> none  [the longest x2 8.84 us: mine(): part = lax.dynamic_slice_in_dim(arr, model_idx * half, half, 0)]
    eq x0 -> x1, local copies, waits for them, and re-layouts: none -> 8.5 us  [layer_shard(): hot = (ids[:, :, None] == jnp.arange(NUM_BUCKETS)).astype(F32)]
    unnamed x29 -> x18, local copies, waits for them, and re-layouts: 13 us -> 14.2 us
  transfers between devices with their start and end apart: 6 -> 3, of which waited for: 6 -> 3; matrix products, arithmetic and copies ran while one was open for 4% -> 2% of each run, Pallas kernels for 0% -> 0%
where the time goes in v3:
time: 436 us; the launch traced here: 435 us
  Pallas kernels  200 us (46%)
  waiting for transfers between devices  144 us (33%)
  local copies, waits for them, and re-layouts  41.9 us (10%)
  other arithmetic  15.9 us (4%)
  between operations  14 us (3%)
  blocking collectives  13.5 us (3%)
  matrix products  5.54 us (1%)
    pallas_call x1, Pallas kernels, layer_call(): pl.pallas_call(layer_kernel, out_shape=outs, grid=(steps,), in_specs=[par...  200 us
    reduce_scatter x1, waiting for transfers between devices, scatter_grads(): lax.psum_scatter(jnp.concatenate([grad_all, extra], axis=1), 'data', scat...  86.5 us
    all_gather x1, waiting for transfers between devices, gather_weights(): full = lax.all_gather(both, 'data', axis=0, tiled=True)  32.6 us
    reduce_scatter x1, waiting for transfers between devices, scatter_grads(): mine = lax.psum_scatter(pair, 'model', scatter_dimension=0)  25 us
    unnamed x18, local copies, waits for them, and re-layouts  14.2 us
    all_gather x1, blocking collectives, gather_weights(): pair = lax.all_gather(local, 'model', axis=0)  13.5 us
    concatenate x1, other arithmetic, scatter_grads(): jnp.concatenate([grad_all, extra], axis=1)  10.2 us
  transfers between devices with their start and end apart: 3, of which 3 were waited for; matrix products, arithmetic and copies ran while one was open for 2% of the time, Pallas kernels for 0%

profile of v3, /device:TPU:0, one launch (start us, length us, event | category | flops | bytes accessed | tf_op | source)
XLA Modules:
  0.0 434.9 jit_solution(12575873452462301262)
XLA Ops:
  8.7 1.2 concatenate.23
  10.0 13.5 %all-gather = bf16[128,3200]{1,0:T(8,128)(2,1)S(1)} all-gather(bf16[64,3200]{1,0:T(8,128)(2,1)S(1)} %concatenate.23), channel_id=2, replica_groups=mesh['model'=2,'data'=8] {'model'}, dimensions={0}, use_global_device_ids=true | all-gather | bytes 1228800 | tf_op jit(solution)/shard_map/all_gather | solution.py:359
  23.7 1.1 concatenate.24
  27.0 8.5 %copy.90 = pred[384,128,32]{1,2,0:T(32,128)(4,1)S(1)} copy(pred[384,128,32]{0,2,1:T(32,128)(4,1)S(1)} %iota_compare_fusion.1) | data formatting | bytes 3145728 | tf_op jit(solution)/shard_map/eq | solution.py:434
  35.6 32.6 %all-gather.3.cloned.1.call-done.w_ref = bf16[512,6272]{1,0:T(8,128)(2,1)} async-done(((bf16[64,6272]{1,0:T(8,128)(2,1)}), bf16[512,6272]{1,0:T(8,128)(2,1)}) %all-gather.3.cloned.1.call-update) | async-done | bytes 6422544 | tf_op jit(solution)/shard_map/all_gather | solution.py:369
  69.8 1.6 fusion.1
  71.4 1.2 copy.91.bias_ref
  72.6 199.8 %layer.1 = (bf16[6144,512]{1,0:T(8,128)(2,1)}, bf16[6144,512]{1,0:T(8,128)(2,1)}, bf16[3072,512]{1,0:T(8,128)(2,1)}, f32[512,6144]{1,0:T(8,128)}, f32[24,512]{1,0:T(8,128)}, /*index=5*/f32[6,384,128]{2,1,0:T(8,128)}) custom-call(bf16[6144,512]{1,0:T(8,128)(2,1)} %bitcast.90, bf16[3072,512]{1,0:T(8,128)(2,1)} %bitcast.99, bf16[6144,512]{1,0:T(8,128)(2,1)} %bitcast.91, ...), custom_call_target="tpu_custom_call" | custom-call | tf_op jit(solution)/shard_map/layer/pallas_call | solution.py:407
  273.2 1.8 copy.92
  275.1 4.0 convolution_bitcast_fusion
  279.3 10.2 %select_maximum_fusion = f32[512,6272]{1,0:T(8,128)} fusion(f32[512,9]{1,0:T(8,128)S(1)} %copy.93, f32[512,6144]{1,0:T(8,128)} %get-tuple-element.27), kind=kLoop, calls=%fused_computation | loop fusion | flops 9633792 | bytes 25446400 | tf_op jit(solution)/shard_map/concatenate | solution.py:379
  289.6 86.5 %reduce-scatter.3.cloned.1.call-done = f32[64,6272]{1,0:T(8,128)} async-done(((f32[512,6272]{1,0:T(8,128)}), f32[64,6272]{1,0:T(8,128)}) %reduce-scatter.3.cloned.1.call-update) | async-done | bytes 1605648 | tf_op jit(solution)/shard_map/reduce_scatter | solution.py:379
  376.1 2.1 fusion.4
  378.1 2.3 fusion.5
  380.5 1.0 concatenate.27
  381.6 1.4 concatenate.28
  383.0 1.3 pad_maximum_fusion
  384.3 25.0 %reduce-scatter.5.cloned.1.call-done = f32[1,64,3200]{2,1,0:T(8,128)} async-done(((f32[2,64,3200]{2,1,0:T(8,128)}), f32[1,64,3200]{2,1,0:T(8,128)}) %reduce-scatter.5.cloned.1.call-update) | async-done | bytes 819216 | tf_op jit(solution)/shard_map/reduce_scatter | solution.py:389
  409.3 1.6 slice_reduce_fusion
  411.7 1.8 slice_bitcast_fusion
  413.5 2.1 slice_bitcast_fusion.1
  416.3 6.2 %copy.104 = bf16[16,384,512]{2,1,0:T(8,128)(2,1)} copy(bf16[16,384,512]{2,1,0:T(8,128)(2,1)} %bitcast.89) | data formatting | bytes 12582912
  422.5 3.2 copy.105
  426.7 1.7 copy.106
  (50 shorter events, 9.2 us)
Async XLA Ops:
  7.2 61.0 %all-gather.3.cloned.1.call-start = ((), (), s32[]{:S(2)}) async-start(), calls=%async_computation.2 | async-start | bytes 7225344 | tf_op jit(solution)/shard_map/all_gather | solution.py:369
  9.9 15.0 %copy-start.3 = (s32[15]{0:T(128)S(1)}, s32[15]{0:T(128)}, u32[]{:S(2)}) copy-start(s32[15]{0:T(128)} %constant.14.clone) | copy-start | bytes 184
  24.8 351.2 %reduce-scatter.3.cloned.1.call-start = ((), (), s32[]{:S(2)}) async-start(), calls=%async_computation.3 | async-start | bytes 14450688 | tf_op jit(solution)/shard_map/reduce_scatter | solution.py:379
  25.5 0.7 copy-start.2
  289.5 119.8 %reduce-scatter.5.cloned.1.call-start = ((), (), s32[]{:S(2)}) async-start(), calls=%async_computation.4 | async-start | bytes 2457600 | tf_op jit(solution)/shard_map/reduce_scatter | solution.py:389
  376.1 4.4 %slice-start.2 = ((f32[64,6272]{1,0:T(8,128)}), f32[64,128]{1,0:T(8,128)S(1)}, s32[]{:S(2)}) async-start(f32[64,6272]{1,0:T(8,128)} %reduce-scatter.3.cloned.1.call-done), calls=%async_computation.7 | async-start | bytes 65536 | tf_op jit(solution)/shard_map/slice | solution.py:386
  376.1 5.4 %copy-start.1 = (f32[64,6272]{1,0:T(8,128)S(1)}, f32[64,6272]{1,0:T(8,128)}, u32[]{:S(2)}) copy-start(f32[64,6272]{1,0:T(8,128)} %reduce-scatter.3.cloned.1.call-done) | copy-start | bytes 4816900
  376.1 5.5 %slice-start.3 = ((f32[64,6272]{1,0:T(8,128)}), f32[64,3]{1,0:T(8,128)S(1)}, s32[]{:S(2)}) async-start(f32[64,6272]{1,0:T(8,128)} %reduce-scatter.3.cloned.1.call-done), calls=%async_computation.8 | async-start | bytes 65536 | tf_op jit(solution)/shard_map/slice | solution.py:387
  376.1 5.5 %slice-start.4 = ((f32[64,6272]{1,0:T(8,128)}), f32[64,515]{1,0:T(8,128)S(1)}, s32[]{:S(2)}) async-start(f32[64,6272]{1,0:T(8,128)} %reduce-scatter.3.cloned.1.call-done), calls=%async_computation.9 | async-start | bytes 327680 | tf_op jit(solution)/shard_map/slice | solution.py:384
  413.5 9.0 %slice-start = ((s8[6291456]{0:T(1024)(128)(4,1)}), s8[2097152]{0:T(1024)(128)(4,1)S(1)}, s32[]{:S(2)}) async-start(s8[6291456]{0:T(1024)(128)(4,1)} %bitcast.86), calls=%async_computation.5 | async-start | bytes 4194304
  416.3 6.2 %slice-start.1 = ((s8[6291456]{0:T(1024)(128)(4,1)}), s8[4194304]{0:T(1024)(128)(4,1)S(1)}, s32[]{:S(2)}) async-start(s8[6291456]{0:T(1024)(128)(4,1)} %bitcast.86), calls=%async_computation.6 | async-start | bytes 8388608
  422.5 4.2 copy-start
Sparse Core Ops, SparseCore 0:
  25.0 43.1 all-gather.2
  289.6 86.3 reduce-scatter.2
  384.4 24.8 reduce-scatter.4

commit v4 on v3

--- a/solution.py
+++ b/solution.py
@@ -70,7 +70,7 @@
         return pl.ds(pl.multiple_of(r0 + off, CHUNK), CHUNK)
 
     chunks = range(0, SEQ, CHUNK)
-    slot, wait_slot, send = exchange
+    slot, wait_slot, send, weights_here = exchange
     lane_idx = lax.broadcasted_iota(jnp.int32, (SEQ, QB), 1)
     tri = lax.broadcasted_iota(jnp.int32, (QB, QB), 0) <= lax.broadcasted_iota(jnp.int32, (QB, QB), 1)
 
@@ -102,6 +102,8 @@
 
     lax.fori_loop(0, PAIRS, self_pair, 0)
 
+    weights_here(1)
+
     delta = nt(ctx_s[rows, :], w_ref[:, C_SO:C_SO + INNER])
     for off in chunks:
         mid = (x_ref[chunk_rows(off), :].astype(F32) + delta[off:off + CHUNK]).astype(BF)
@@ -132,6 +134,8 @@
         return carry
 
     lax.fori_loop(0, PAIRS, cross_pair, 0)
+
+    weights_here(2)
 
     delta = nt(cctx_s[rows, :], w_ref[:, C_CO:C_CO + INNER])
     for off in chunks:
@@ -280,8 +284,140 @@
     add(n1_s, dqkv_s, C_SQ, 3 * INNER)
 
 
-def layer_kernel(x_ref, e_ref, dy_ref, w_ref, gain_ref, bias_ref, y_hbm, dx_hbm, de_hbm, g_ref, dg_ref, db_ref, *scratch):
-    *scratch, y_buf, dx_buf, de_buf, local_sem, send_sem, recv_sem = scratch
+O_I0, O_I1, O_WO, O_EX, O_END = 2048, 2560, 3072, 3584, 3712
+PACKED = (((0, 1024), (O_EX, QB)), ((1024, 1024),), ((O_I0, 1536),))
+WHOLE = (((0, 1536), (C_END, QB)), ((1536, 1536),), ((C_I0, 3072),))
+X_FIRST = (((0, 768),), ((1536, 768),), ((C_I0, 1536),))
+Y_FIRST = (((768, 768), (C_END, QB)), ((2304, 768),), ((C_I0 + 1536, 1536),))
+GATHER_SEMS = 48
+THRESHOLDS = tuple(range(1, 17)) + BUCKET_EDGES
+
+
+def gather_plan(loc_ref, rz_s, w_s, send_sem, recv_sem):
+    m, d = lax.axis_index("model"), lax.axis_index("data")
+    core, x, y = lax.rem(d, 2), lax.rem(d // 2, 2), d // 4
+    d_core, d_x, d_y = d + 1 - 2 * core, d + 2 - 4 * x, d + 4 - 8 * y
+    count = [0]
+
+    def copy(src, dst, peer):
+        number = count[0]
+        count[0] += 1
+        return lambda: pltpu.make_async_remote_copy(src_ref=src, dst_ref=dst, send_sem=send_sem.at[number], recv_sem=recv_sem.at[number],
+                                                    device_id=peer, device_id_type=MESH)
+
+    def block(owner, run):
+        return w_s.at[pl.ds(pl.multiple_of(owner * 64, 64), 64), run[0]:run[0] + run[1]]
+
+    def blocks(owners, runs, peer):
+        return [copy(block(owner, run), block(owner, run), peer) for owner in owners for run in runs]
+
+    plan = []
+    for group in range(3):
+        z = [copy(loc_ref.at[:, a:a + n], rz_s.at[:, a:a + n], {"model": 1 - m}) for a, n in PACKED[group]]
+        second = blocks([d], X_FIRST[group], {"data": d_x}) + blocks([d], Y_FIRST[group], {"data": d_y})
+        third = blocks([d, d_x], X_FIRST[group], {"data": d_y}) + blocks([d, d_y], Y_FIRST[group], {"data": d_x})
+        mine = [core, core + 2, core + 4, core + 6]
+        plan.append((z, second, third, blocks(mine, WHOLE[group], {"data": d_core})))
+    return plan
+
+
+def pack_share(attn, mlp, ext_ref, loc_s):
+    m = lax.axis_index("model")
+    for b, ref in enumerate(attn):
+        left = jnp.concatenate([ref[...].astype(F32), jnp.zeros((64, 64), F32)], axis=1)
+        loc_s[:, 256 * b:256 * b + 256] = jnp.where(m == 0, left, pltpu.roll(left, 64, 1)).astype(BF)
+    for col, ref in zip((O_I0, O_I1, O_WO), mlp):
+        loc_s[:, col:col + 512] = ref[...]
+    loc_s[:, O_EX:O_END] = ext_ref[...]
+
+
+def fill_gains(w_s, gain_s):
+    low = lax.broadcasted_iota(jnp.int32, (8, QB), 1) < 64
+    for pair in range(4):
+        even = w_s[128 * pair:128 * pair + 16, C_END:C_END + QB].astype(F32)[0:8]
+        odd = w_s[128 * pair + 64:128 * pair + 80, C_END:C_END + QB].astype(F32)[0:8]
+        gain_s[:, QB * pair:QB * pair + QB] = jnp.where(low, even, pltpu.roll(odd, 64, 1))
+
+
+def small_grads(dg_s, db_s, ext_ref):
+    dist = jnp.maximum(SEQ - QB + lax.broadcasted_iota(jnp.int32, (SEQ, QB), 1) - lax.broadcasted_iota(jnp.int32, (SEQ, QB), 0), 0)
+    ids = jnp.zeros((SEQ, QB), jnp.int32)
+    for edge in THRESHOLDS:
+        ids = ids + (dist >= edge).astype(jnp.int32)
+    lane = lax.broadcasted_iota(jnp.int32, (NUM_BUCKETS, QB), 1)
+    row = lax.broadcasted_iota(jnp.int32, (NUM_BUCKETS, QB), 0)
+    bias = jnp.zeros((NUM_BUCKETS, QB), F32)
+    for head in range(HEADS):
+        def bucket_sum(bucket, sums):
+            part = jnp.sum(jnp.where(ids == bucket, db_s[head], 0.0), axis=0, keepdims=True)
+            return jnp.where(row == bucket, part, sums)
+        sums = lax.fori_loop(0, NUM_BUCKETS, bucket_sum, jnp.zeros((NUM_BUCKETS, QB), F32))
+        bias = jnp.where(lane == 64 + head, jnp.sum(sums, axis=1, keepdims=True), bias)
+    row8 = lax.broadcasted_iota(jnp.int32, (8, DIM), 0)
+    gains = jnp.zeros((8, DIM), F32)
+    for idx in range(3):
+        gains = jnp.where(row8 == idx, jnp.sum(dg_s[8 * idx:8 * idx + 8, :], axis=0, keepdims=True), gains)
+    low = lax.broadcasted_iota(jnp.int32, (8, QB), 1) < 64
+    for d in range(8):
+        tile = gains[:, QB * (d // 2):QB * (d // 2) + QB]
+        if d % 2:
+            tile = pltpu.roll(tile, 64, 1)
+        ext_ref[64 * d:64 * d + 8, :] = jnp.where(low, tile, bias[0:8])
+        ext_ref[64 * d + 8:64 * d + NUM_BUCKETS, :] = bias[8:]
+        ext_ref[64 * d + NUM_BUCKETS:64 * d + 64, :] = jnp.zeros((32, QB), F32)
+
+
+def merge_share(group, loc_ref, rz_s, w_s):
+    m, d = lax.axis_index("model"), lax.axis_index("data")
+    rows = pl.ds(pl.multiple_of(d * 64, 64), 64)
+
+    def both(a, n):
+        here, there = loc_ref[:, a:a + n].astype(F32), rz_s[:, a:a + n].astype(F32)
+        return jnp.where(m == 0, here, there), jnp.where(m == 0, there, here)
+
+    if group == 2:
+        for a, col in ((O_I0, C_I0), (O_I1, C_I1), (O_WO, C_WO)):
+            low, high = both(a, 512)
+            w_s[rows, col:col + 512] = low.astype(BF)
+            w_s[rows, col + 512:col + 1024] = high.astype(BF)
+        return
+    for b in range(4 * group, 4 * group + 4):
+        low, high = both(256 * b, 256)
+        w_s[rows, INNER * b:INNER * b + QB] = low[:, :QB].astype(BF)
+        w_s[rows, INNER * b + QB:INNER * b + 2 * QB] = (low[:, QB:] + high[:, :QB]).astype(BF)
+        w_s[rows, INNER * b + 2 * QB:INNER * b + 3 * QB] = high[:, QB:].astype(BF)
+    if group == 0:
+        w_s[rows, C_END:C_END + QB] = loc_ref[:, O_EX:O_END]
+
+
+def begin(copies):
+    for make in copies:
+        make().start()
+
+
+def arrive_all(copies):
+    for make in copies:
+        make().wait_recv()
+
+
+def fill_bias(loc_ref, rz_s, bias_s):
+    m = lax.axis_index("model")
+    here, there = loc_ref[0:NUM_BUCKETS, O_EX:O_END].astype(F32), rz_s[0:NUM_BUCKETS, O_EX:O_END].astype(F32)
+    tables = jnp.where(m == 0, here, there), jnp.where(m == 0, there, here)
+    dist = SEQ - QB + lax.broadcasted_iota(jnp.int32, (SEQ, QB), 1) - lax.broadcasted_iota(jnp.int32, (SEQ, QB), 0)
+    for head in range(HEADS):
+        table = tables[head // 3]
+        lane = 64 + head % 3
+        value = jnp.broadcast_to(table[0:1, lane:lane + 1], (SEQ, QB))
+        for bucket, edge in enumerate(THRESHOLDS):
+            value = jnp.where(dist >= edge, table[bucket + 1:bucket + 2, lane:lane + 1], value)
+        bias_s[head] = value
+
+
+def layer_kernel(x_ref, e_ref, dy_ref, *refs):
+    attn, mlp, (extra_ref, y_hbm, dx_hbm, de_hbm, g_ref, ext_ref), scratch = refs[:8], refs[8:11], refs[11:17], refs[17:]
+    *scratch, y_buf, dx_buf, de_buf, w_ref, rz_s, gain_ref, bias_ref, loc_ref, dg_ref, db_ref, local_sem, send_sem, recv_sem, w_send, w_recv = scratch
+    plan = gather_plan(loc_ref, rz_s, w_ref, w_send, w_recv)
     (n1_s, n2_s, n3_s, dm1_s, dm2_s, qkv_s, dqkv_s, ctx_s, cq_s, ckv_s, dcq_s, dckv_s, cctx_s,
      hid_s, d01_s, x1_s, x2_s, dctx_s, pf_s, pt_s, cpf_s, cpt_s, ds_s, cds_s, km_s, vm_s) = scratch
     me = lax.axis_index("model")
@@ -292,14 +428,40 @@
 
     @pl.when(step == 0)
     def _():
+        d = lax.axis_index("data")
+        core, x, y = lax.rem(d, 2), lax.rem(d // 2, 2), d // 4
         barrier = pltpu.get_barrier_semaphore()
-        pl.semaphore_signal(barrier, inc=1, device_id={"model": other}, device_id_type=MESH)
-        pl.semaphore_wait(barrier, 1)
+        for peer in ({"model": other}, {"data": d + 1 - 2 * core}, {"data": d + 2 - 4 * x}, {"data": d + 4 - 8 * y}):
+            pl.semaphore_signal(barrier, inc=1, device_id=peer, device_id_type=MESH)
+        pl.semaphore_wait(barrier, 4)
+        pack_share(attn, mlp, extra_ref, loc_ref)
+        for group in range(3):
+            begin(plan[group][0])
+        arrive_all(plan[0][0])
+        merge_share(0, loc_ref, rz_s, w_ref)
+        begin(plan[0][1])
+        arrive_all(plan[1][0])
+        merge_share(1, loc_ref, rz_s, w_ref)
+        begin(plan[1][1])
+        arrive_all(plan[0][1])
+        begin(plan[0][2])
+        arrive_all(plan[2][0])
+        merge_share(2, loc_ref, rz_s, w_ref)
+        begin(plan[2][1])
+        arrive_all(plan[1][1])
+        begin(plan[1][2])
+        fill_bias(loc_ref, rz_s, bias_ref)
         pt_s[...] = jnp.zeros_like(pt_s)
         ds_s[...] = jnp.zeros_like(ds_s)
         dg_ref[...] = jnp.zeros_like(dg_ref)
         db_ref[...] = jnp.zeros_like(db_ref)
+        arrive_all(plan[0][2])
+        begin(plan[0][3])
+        arrive_all(plan[2][1])
+        begin(plan[2][2])
         g_ref[...] = jnp.zeros_like(g_ref)
+        arrive_all(plan[0][3])
+        fill_gains(w_ref, gain_ref)
 
     def copies(which, number):
         buf, hbm, length = bufs[which]
@@ -326,7 +488,19 @@
             remote.start()
             local.start()
 
-        seq_body(s, (lax.rem(number, 2), wait_slot, send), x_ref, e_ref, dy_ref, w_ref, gain_ref, bias_ref, y_buf, dx_buf, de_buf, dg_ref, db_ref, *scratch)
+        def weights_here(group):
+            @pl.when(number == 0)
+            def _():
+                arrive_all(plan[group][2])
+                begin(plan[group][3])
+                arrive_all(plan[group][3])
+                if group == 2:
+                    for phases in plan:
+                        for phase in phases:
+                            for make in phase:
+                                make().wait_send()
+
+        seq_body(s, (lax.rem(number, 2), wait_slot, send, weights_here), x_ref, e_ref, dy_ref, w_ref, gain_ref, bias_ref, y_buf, dx_buf, de_buf, dg_ref, db_ref, *scratch)
         return carry
 
     lax.fori_loop(0, SEQS_STEP, body, 0)
@@ -334,6 +508,7 @@
 
     @pl.when(step == pl.num_programs(0) - 1)
     def _():
+        small_grads(dg_ref, db_ref, ext_ref)
         for which in range(3):
             for back in (2, 1):
                 local, remote = copies(which, seqs - back)
@@ -347,55 +522,172 @@
             lax.fori_loop(0, seqs, arrived, 0)
 
 
-def pack_local(sq, sk, sv, so, cq, ck, cv, co, wi0, wi1, wo):
-    return [sq, sk, sv, so.T, cq, ck, cv, co.T, wi0, wi1, wo.T]
-
-
-def gather_weights(blocks, gains, rel_bias):
-    rows, heads_dev = gains.shape[1], rel_bias.shape[1]
-    extra = jnp.concatenate([gains.T, jnp.pad(rel_bias, ((0, rows - rel_bias.shape[0]), (0, 0)))], axis=1)
-    extra = jnp.pad(extra, ((0, 0), (0, QB - extra.shape[1])))
-    local = jnp.concatenate(blocks + [extra], axis=1)
-    pair = lax.all_gather(local, "model", axis=0)
-    cols = []
+RUNS = (((0, 1920), (C_END, QB)), ((1920, 1152), (C_WO, FF)), ((C_I0, 2 * FF),))
+
+
+def z_pieces(group):
+    attn = [(INNER * b, QB, 256, 256 * b) for b in range(8)]
+    if group == 0:
+        return attn[:5] + [(C_END, 0, QB, O_EX)]
+    if group == 1:
+        return attn[5:] + [(C_WO, 512, 512, O_WO)]
+    return [(C_I0, 512, 512, O_I0), (C_I1, 512, 512, O_I1)]
+
+
+Z_WIDTH = tuple(sum(piece[2] for piece in z_pieces(group)) for group in range(3))
+RUN_WIDTH = tuple(sum(run[1] for run in RUNS[group]) for group in range(3))
+REDUCE_SCRATCH = [(2, 2, 64, C_END + QB), (2, 2, 64, C_END + QB),
+                  (2, 64, RUN_WIDTH[0]), (64, RUN_WIDTH[0]), (64, Z_WIDTH[0]),
+                  (2, 64, RUN_WIDTH[1]), (2, 64, Z_WIDTH[1]), (64, Z_WIDTH[1]),
+                  (2, 2, 64, Z_WIDTH[2]), (2, 64, Z_WIDTH[2]), (64, Z_WIDTH[2])]
+REDUCE_SEMS = 64
+
+
+def reduce_kernel(g_hbm, ext_hbm, out_ref, acc, first, a1, a2, a3, b1, b2, b3, c1, c2, c3, local_sem, send_sem, recv_sem):
+    m, d = lax.axis_index("model"), lax.axis_index("data")
+    core, x, y = lax.rem(d, 2), lax.rem(d // 2, 2), d // 4
+    to_core, to_x, to_y, to_z = {"data": d + 1 - 2 * core}, {"data": d + 2 - 4 * x}, {"data": d + 4 - 8 * y}, {"model": 1 - m}
+    barrier = pltpu.get_barrier_semaphore()
+    for peer in (to_core, to_x, to_y, to_z):
+        pl.semaphore_signal(barrier, inc=1, device_id=peer, device_id_type=MESH)
+    pl.semaphore_wait(barrier, 4)
+    sent = []
+
+    def push(src, dst, peer):
+        number = len(sent)
+        copy = pltpu.make_async_remote_copy(src_ref=src, dst_ref=dst, send_sem=send_sem.at[number], recv_sem=recv_sem.at[number],
+                                            device_id=peer, device_id_type=MESH)
+        copy.start()
+        sent.append(copy)
+        return copy
+
+    def cols(piece, who):
+        return pl.ds(pl.multiple_of(piece[0] + who * piece[1], QB), piece[2])
+
+    loads, pend = {}, {}
+    number = 0
+    for group in (2, 0, 1):
+        loads[group], pend[group] = [], []
+        for col, width in RUNS[group]:
+            src = ext_hbm if col == C_END else g_hbm
+            src_cols = pl.ds(0 if col == C_END else col, width)
+            here = pltpu.make_async_copy(src.at[:, :, core, :, src_cols], acc.at[:, :, :, pl.ds(col, width)], local_sem.at[number])
+            number += 1
+            pend[group].append(push(src.at[:, :, 1 - core, :, src_cols], first.at[:, :, :, pl.ds(col, width)], to_core))
+            here.start()
+            loads[group].append(here)
+
+    def run_push(group, src_of, dst, peer):
+        off, out = 0, []
+        for col, width in RUNS[group]:
+            out.append(push(src_of(pl.ds(col, width)), dst.at[..., pl.ds(off, width)], peer))
+            off += width
+        return out
+
+    def z_push(group, src_of, dst, peer, who):
+        off, out = 0, []
+        for piece in z_pieces(group):
+            out.append(push(src_of(cols(piece, who)), dst.at[..., pl.ds(off, piece[2])], peer))
+            off += piece[2]
+        return out
+
+    for group in (2, 0, 1):
+        for here in loads[group]:
+            here.wait()
+        for copy in pend[group]:
+            copy.wait_recv()
+        for col, width in RUNS[group]:
+            for yy in range(2):
+                for xx in range(2):
+                    acc[yy, xx, :, col:col + width] += first[yy, xx, :, col:col + width]
+        if group == 0:
+            pend[0] = run_push(0, lambda c: acc.at[:, 1 - x, :, c], a1, to_x)
+        elif group == 1:
+            pend[1] = run_push(1, lambda c: acc.at[1 - y, :, :, c], b1, to_y)
+        else:
+            pend[2] = z_push(2, lambda c: acc.at[:, :, :, c], c1, to_z, 1 - m)
+
+    def arrive(group):
+        for copy in pend[group]:
+            copy.wait_recv()
+
+    arrive(0)
     off = 0
-    for blk in blocks:
-        width = blk.shape[1]
-        cols.append(pair[0, :, off:off + width])
-        cols.append(pair[1, :, off:off + width])
+    for col, width in RUNS[0]:
+        for yy in range(2):
+            acc[yy, x, :, col:col + width] += a1[yy, :, off:off + width]
         off += width
-    cols += [pair[0, :, off:off + 3 + heads_dev], pair[1, :, off + 3:off + QB - heads_dev]]
-    both = jnp.concatenate(cols, axis=1)
-    full = lax.all_gather(both, "data", axis=0, tiled=True)
-    return full, full[:, 2 * off:2 * off + 3].T, full[:NUM_BUCKETS, 2 * off + 3:2 * off + 3 + 2 * heads_dev]
-
-
-def scatter_grads(grad_all, gain_part, bias_part, widths):
-    blocks = grad_all.shape[0] // 64
-    rep_bias = jnp.tile(jnp.pad(bias_part, ((0, 64 - bias_part.shape[0]), (0, 0))), (blocks, 1))
-    extra = jnp.concatenate([gain_part.T, rep_bias], axis=1)
-    extra = jnp.pad(extra, ((0, 0), (0, QB - extra.shape[1])))
-    heads_dev = bias_part.shape[1] // 2
-    rows = lax.psum_scatter(jnp.concatenate([grad_all, extra], axis=1), "data", scatter_dimension=0, tiled=True)
-    lo, hi = [], []
+    pend[0] = run_push(0, lambda c: acc.at[1 - y, x, :, c], a2, to_y)
+    arrive(1)
     off = 0
-    for width in widths:
-        lo.append(rows[:, off:off + width])
-        hi.append(rows[:, off + width:off + 2 * width])
-        off += 2 * width
-    lo.append(rows[:, off:off + QB])
-    hi += [rows[:, off:off + 3], rows[:, off + 3 + heads_dev:off + QB], rows[:, :heads_dev]]
-    pair = jnp.stack([jnp.concatenate(lo, axis=1), jnp.concatenate(hi, axis=1)])
-    mine = lax.psum_scatter(pair, "model", scatter_dimension=0)
-    outs = []
+    for col, width in RUNS[1]:
+        for xx in range(2):
+            acc[y, xx, :, col:col + width] += b1[xx, :, off:off + width]
+        off += width
+    pend[1] = z_push(1, lambda c: acc.at[y, :, :, c], b2, to_z, 1 - m)
+    arrive(2)
     off = 0
-    for width in widths:
-        outs.append(mine[:, off:off + width])
+    for piece in z_pieces(2):
+        for yy in range(2):
+            for xx in range(2):
+                acc[yy, xx, :, cols(piece, m)] += c1[yy, xx, :, off:off + piece[2]]
+        off += piece[2]
+    pend[2] = z_push(2, lambda c: acc.at[:, 1 - x, :, c], c2, to_x, m)
+
+    arrive(0)
+    off = 0
+    for col, width in RUNS[0]:
+        acc[y, x, :, col:col + width] += a2[:, off:off + width]
         off += width
-    return outs, mine[:, off:off + 3], mine[:NUM_BUCKETS, off + 3:off + 3 + heads_dev]
-
-
-def layer_call(x, e, dy, weights, gains, bias_t):
+    pend[0] = z_push(0, lambda c: acc.at[y, x, :, c], a3, to_z, 1 - m)
+    held = pend[1]
+    for copy in held:
+        copy.wait_recv()
+        copy.wait_send()
+    off = 0
+    for piece in z_pieces(1):
+        for xx in range(2):
+            acc[y, xx, :, cols(piece, m)] += b2[xx, :, off:off + piece[2]]
+        off += piece[2]
+    pend[1] = z_push(1, lambda c: acc.at[y, 1 - x, :, c], b3, to_x, m)
+    arrive(2)
+    off = 0
+    for piece in z_pieces(2):
+        for yy in range(2):
+            acc[yy, x, :, cols(piece, m)] += c2[yy, :, off:off + piece[2]]
+        off += piece[2]
+    pend[2] = z_push(2, lambda c: acc.at[1 - y, x, :, c], c3, to_y, m)
+
+    for group, last in ((0, a3), (1, b3), (2, c3)):
+        arrive(group)
+        off = 0
+        for piece in z_pieces(group):
+            out_ref[:, piece[3]:piece[3] + piece[2]] = acc[y, x, :, cols(piece, m)] + last[:, off:off + piece[2]]
+            off += piece[2]
+    for copy in sent:
+        if not any(copy is other for other in held):
+            copy.wait_send()
+
+
+def scatter_grads(grad_all, ext):
+    m = lax.axis_index("model")
+    mine = pl.pallas_call(
+        reduce_kernel,
+        out_shape=jax.ShapeDtypeStruct((64, O_END), F32),
+        in_specs=[pl.BlockSpec(memory_space=pl.ANY)] * 2,
+        out_specs=pl.BlockSpec(memory_space=pltpu.VMEM),
+        scratch_shapes=[pltpu.VMEM(item, F32) for item in REDUCE_SCRATCH] + [
+            pltpu.SemaphoreType.DMA((8,)), pltpu.SemaphoreType.DMA((REDUCE_SEMS,)), pltpu.SemaphoreType.DMA((REDUCE_SEMS,))],
+        compiler_params=pltpu.CompilerParams(vmem_limit_bytes=67043328, collective_id=1, has_side_effects=True),
+        name="reduce",
+    )(grad_all.reshape(2, 2, 2, 64, C_END), ext.reshape(2, 2, 2, 64, QB))
+    outs = [jnp.where(m == 0, mine[:, 256 * b:256 * b + 192], mine[:, 256 * b + 64:256 * b + 256]) for b in range(8)]
+    outs += [mine[:, O_I0:O_I1], mine[:, O_I1:O_WO], mine[:, O_WO:O_EX]]
+    bias = jnp.where(m == 0, mine[:NUM_BUCKETS, O_EX + 64:O_EX + 67], mine[:NUM_BUCKETS, O_EX + 67:O_EX + 70])
+    return outs, mine[0:3, O_EX:O_EX + 64], bias
+
+
+def layer_call(x, e, dy, attn, mlp, extra):
     steps = x.shape[0] // (2 * SEQS_STEP * SEQ)
     part = lambda rows: pl.BlockSpec((rows, DIM), lambda i: (lax.axis_index("model") * steps + i, 0))
     fixed = lambda arr_shape: pl.BlockSpec(arr_shape, lambda i: (0,) * len(arr_shape), pipeline_mode=pl.Buffered(1))
@@ -403,46 +695,36 @@
     rows, erows = SEQS_STEP * SEQ, SEQS_STEP * ENC
     seqs = SEQS_STEP * steps
     outs = [jax.ShapeDtypeStruct(x.shape, BF), jax.ShapeDtypeStruct(x.shape, BF), jax.ShapeDtypeStruct(e.shape, BF),
-            jax.ShapeDtypeStruct((DIM, C_END), F32), jax.ShapeDtypeStruct((24, DIM), F32), jax.ShapeDtypeStruct((HEADS, SEQ, QB), F32)]
+            jax.ShapeDtypeStruct((DIM, C_END), F32), jax.ShapeDtypeStruct((DIM, QB), F32)]
     return pl.pallas_call(
         layer_kernel,
         out_shape=outs,
         grid=(steps,),
-        in_specs=[part(rows), part(erows), part(rows), pl.BlockSpec((DIM, C_END), lambda i: (0, 0), pipeline_mode=pl.Buffered(1)), fixed(gains.shape), fixed(bias_t.shape)],
-        out_specs=[anywhere, anywhere, anywhere, fixed((DIM, C_END)), fixed((24, DIM)), fixed((HEADS, SEQ, QB))],
+        in_specs=[part(rows), part(erows), part(rows)] + [fixed(w.shape) for w in attn + mlp + [extra]],
+        out_specs=[anywhere, anywhere, anywhere, fixed((DIM, C_END)), fixed((DIM, QB))],
         scratch_shapes=[pltpu.VMEM(*item) for item in SCRATCH] + [
             pltpu.VMEM((2, SEQ, DIM), BF), pltpu.VMEM((2, SEQ, DIM), BF), pltpu.VMEM((2, ENC, DIM), BF),
-            pltpu.SemaphoreType.DMA((3, 2)), pltpu.SemaphoreType.DMA((3, 2)), pltpu.SemaphoreType.DMA((3, seqs))],
+            pltpu.VMEM((DIM, C_END + QB), BF), pltpu.VMEM((64, O_END), BF), pltpu.VMEM((8, DIM), F32), pltpu.VMEM((HEADS, SEQ, QB), F32),
+            pltpu.VMEM((64, O_END), BF), pltpu.VMEM((24, DIM), F32), pltpu.VMEM((HEADS, SEQ, QB), F32),
+            pltpu.SemaphoreType.DMA((3, 2)), pltpu.SemaphoreType.DMA((3, 2)), pltpu.SemaphoreType.DMA((3, seqs)),
+            pltpu.SemaphoreType.DMA((GATHER_SEMS,)), pltpu.SemaphoreType.DMA((GATHER_SEMS,))],
         compiler_params=pltpu.CompilerParams(dimension_semantics=("arbitrary",), vmem_limit_bytes=67043328, collective_id=0, has_side_effects=True),
         name="layer",
-    )(x, e, dy, weights, gains, bias_t)
-
-
-def bias_table():
-    dist = (SEQ - QB + jnp.arange(QB))[None, :] - jnp.arange(SEQ)[:, None]
-    dist = jnp.maximum(dist, 0)
-    edges = jnp.array(BUCKET_EDGES, dtype=jnp.int32)
-    ids = jnp.minimum(dist, 16) + jnp.sum((dist[:, :, None] >= edges).astype(jnp.int32), axis=-1)
-    return ids
+    )(x, e, dy, *attn, *mlp, extra)
 
 
 def layer_shard(dec_in, enc_out, grad_out, rel_bias, self_q, self_k, self_v, self_o, cross_q, cross_k, cross_v, cross_o, mlp_wi_0, mlp_wi_1, mlp_wo, norm_self, norm_cross, norm_mlp):
-    blocks = pack_local(self_q, self_k, self_v, self_o, cross_q, cross_k, cross_v, cross_o, mlp_wi_0, mlp_wi_1, mlp_wo)
-    widths = [blk.shape[1] for blk in blocks]
-    weights, gains, bias_pair = gather_weights(blocks, jnp.stack([norm_self, norm_cross, norm_mlp]), rel_bias)
-    ids = bias_table()
-    hot = (ids[:, :, None] == jnp.arange(NUM_BUCKETS)).astype(F32)
-    bias_t = jnp.einsum("car,rh->hca", hot, bias_pair.astype(F32), precision=lax.Precision.HIGHEST)
+    gains = jnp.stack([norm_self, norm_cross, norm_mlp])
+    extra = jnp.pad(gains, ((0, 61), (0, 64))) + jnp.pad(rel_bias, ((0, 32), (64, 61)))
 
     def flat(arr):
         return arr.reshape(-1, DIM)
 
-    dec_out, grad_dec, grad_enc, grad_all, gain_part, bias_rows = layer_call(flat(dec_in), flat(enc_out), flat(grad_out), weights, gains.astype(F32), bias_t)
-    bias_part = jnp.einsum("car,hca->rh", hot, bias_rows, precision=lax.Precision.HIGHEST)
-    gain_part = jnp.sum(gain_part.reshape(3, 8, DIM), axis=1)
-    grads, d_gains, grad_bias = scatter_grads(grad_all, gain_part, bias_part, widths)
+    attn = [self_q, self_k, self_v, self_o.T, cross_q, cross_k, cross_v, cross_o.T]
+    dec_out, grad_dec, grad_enc, grad_all, grad_ext = layer_call(flat(dec_in), flat(enc_out), flat(grad_out), attn, [mlp_wi_0, mlp_wi_1, mlp_wo.T], extra)
+    grads, d_gains, grad_bias = scatter_grads(grad_all, grad_ext)
     o_sq, o_sk, o_sv, o_so, o_cq, o_ck, o_cv, o_co, o_i0, o_i1, o_wo = grads
-    return (dec_out.reshape(dec_in.shape), grad_dec.reshape(dec_in.shape), grad_enc.reshape(enc_out.shape), grad_bias, o_sq, o_sk, o_sv, o_so.T, o_cq, o_ck, o_cv, o_co.T, o_i0, o_i1, o_wo.T, d_gains[:, 0], d_gains[:, 1], d_gains[:, 2])
+    return (dec_out.reshape(dec_in.shape), grad_dec.reshape(dec_in.shape), grad_enc.reshape(enc_out.shape), grad_bias, o_sq, o_sk, o_sv, o_so.T, o_cq, o_ck, o_cv, o_co.T, o_i0, o_i1, o_wo.T, d_gains[0], d_gains[1], d_gains[2])
 
 
 def solution(mesh):

time: 436 us -> 317 us (0.73)
  waiting for transfers between devices: 144 us -> 0 us
  Pallas kernels: 200 us -> 295 us
  local copies, waits for them, and re-layouts: 41.9 us -> 16.7 us
  blocking collectives: 13.5 us -> 0 us
  between operations: 14 us -> 0.69 us
  other arithmetic: 15.9 us -> 4.6 us
  matrix products: 5.54 us -> 0 us
    reduce_scatter x2 -> x0, waiting for transfers between devices: 112 us -> none  [the longest x1 86.5 us: scatter_grads(): lax.psum_scatter(jnp.concatenate([grad_all, extra], axis=1), 'data', scat...]
    pallas_call x0 -> x1, Pallas kernels: none -> 63.2 us  [scatter_grads(): pl.pallas_call(reduce_kernel, out_shape=jax.ShapeDtypeStruct((64, O_END),...]
    all_gather x1 -> x0, waiting for transfers between devices: 32.6 us -> none  [gather_weights(): full = lax.all_gather(both, 'data', axis=0, tiled=True)]
    pallas_call x1, Pallas kernels: 200 us -> 232 us  [layer_call(): pl.pallas_call(layer_kernel, out_shape=outs, grid=(steps,), in_specs=[par...]
    all_gather x1 -> x0, blocking collectives: 13.5 us -> none  [gather_weights(): pair = lax.all_gather(local, 'model', axis=0)]
    concatenate x3 -> x0, other arithmetic: 10.9 us -> none  [the longest x1 10.2 us: scatter_grads(): jnp.concatenate([grad_all, extra], axis=1)]
    eq x1 -> x0, local copies, waits for them, and re-layouts: 8.5 us -> none  [layer_shard(): hot = (ids[:, :, None] == jnp.arange(NUM_BUCKETS)).astype(F32)]
    slice x11 -> x0, local copies, waits for them, and re-layouts: 6.86 us -> none  [the longest x2 4.37 us: scatter_grads(): lo.append(rows[:, off:off + width])]
  transfers between devices with their start and end apart: 3 -> 0, of which waited for: 3 -> 0; matrix products, arithmetic and copies ran while one was open for 2% -> 0% of each run, Pallas kernels for 0% -> 0%
where the time goes in v4:
time: 317 us
  Pallas kernels  295 us (93%)
  local copies, waits for them, and re-layouts  16.7 us (5%)
  other arithmetic  4.6 us (1%)
    pallas_call x1, Pallas kernels, layer_call(): pl.pallas_call(layer_kernel, out_shape=outs, grid=(steps,), in_specs=[par...  232 us
    pallas_call x1, Pallas kernels, scatter_grads(): pl.pallas_call(reduce_kernel, out_shape=jax.ShapeDtypeStruct((64, O_END),...  63.2 us
    unnamed x11, local copies, waits for them, and re-layouts  13.5 us

profile of v4, /device:TPU:0, one launch (start us, length us, event | category | flops | bytes accessed | tf_op | source)
XLA Modules:
  0.0 316.9 jit_solution(10235278048698836196)
XLA Ops:
  0.7 0.8 copy.36
  1.4 1.4 fusion.9.refs_11_
  2.8 231.7 %layer.1 = (bf16[6144,512]{1,0:T(8,128)(2,1)}, bf16[6144,512]{1,0:T(8,128)(2,1)}, bf16[3072,512]{1,0:T(8,128)(2,1)}, f32[512,6144]{1,0:T(8,128)}, f32[512,128]{1,0:T(8,128)}) custom-call(bf16[6144,512]{1,0:T(8,128)(2,1)} %bitcast.27, bf16[3072,512]{1,0:T(8,128)(2,1)} %bitcast.34, bf16[6144,512]{1,0:T(8,128)(2,1)} %bitcast.28, bf16[64,192]{1,0:T(8,128)(2,1)} %refs_0_.1, ...), custom_call_target="tpu_custom_call" | custom-call | tf_op jit(solution)/shard_map/layer/pallas_call | solution.py:699
  234.5 63.2 %reduce.1 = f32[64,3712]{1,0:T(8,128)} custom-call(f32[2,2,2,64,6144]{4,3,2,1,0:T(8,128)} %bitcast.26, f32[2,2,2,64,128]{4,3,2,1,0:T(8,128)} %bitcast.35), custom_call_target="tpu_custom_call" | custom-call | tf_op jit(solution)/shard_map/reduce/pallas_call | solution.py:674
  297.8 2.4 select_bitcast_fusion
  300.1 0.0 slice-start
  300.1 1.9 slice_bitcast_fusion
  302.1 1.3 slice_bitcast_fusion.1
  303.4 0.9 slice_select_fusion.6
  304.3 0.7 copy.37
  304.9 0.0 slice-start.1
  304.9 6.2 %copy.41 = bf16[16,384,512]{2,1,0:T(8,128)(2,1)} copy(bf16[16,384,512]{2,1,0:T(8,128)(2,1)} %bitcast.32) | data formatting | bytes 12582912
  311.1 0.0 slice-done
  311.1 0.0 slice-done.1
  311.1 0.0 copy-start
  311.1 3.2 %copy.42 = bf16[16,384,512]{2,1,0:T(8,128)(2,1)} copy(bf16[16,384,512]{2,1,0:T(8,128)(2,1)S(1)} %bitcast.31) | data formatting | bytes 12582912
  314.3 1.0 copy-done
  315.3 1.7 copy.43
  (1 shorter events, 0.0 us)
Async XLA Ops:
  300.1 11.0 %slice-start = ((s8[6291456]{0:T(1024)(128)(4,1)}), s8[2097152]{0:T(1024)(128)(4,1)S(1)}, s32[]{:S(2)}) async-start(s8[6291456]{0:T(1024)(128)(4,1)} %bitcast.29), calls=%async_computation | async-start | bytes 4194304
  304.9 6.2 %slice-start.1 = ((s8[6291456]{0:T(1024)(128)(4,1)}), s8[4194304]{0:T(1024)(128)(4,1)S(1)}, s32[]{:S(2)}) async-start(s8[6291456]{0:T(1024)(128)(4,1)} %bitcast.29), calls=%async_computation.1 | async-start | bytes 8388608
  311.1 4.2 %copy-start = (bf16[3072,512]{1,0:T(8,128)(2,1)S(1)}, bf16[3072,512]{1,0:T(8,128)(2,1)}, u32[]{:S(2)}) copy-start(bf16[3072,512]{1,0:T(8,128)(2,1)} %get-tuple-element.25) | copy-start | bytes 9437188

commit v5 on v4

--- a/solution.py
+++ b/solution.py
@@ -1,3 +1,4 @@
+import itertools
 import math
 import jax
 import jax.numpy as jnp
@@ -21,6 +22,7 @@
 PAIRS = 3
 QB = 128
 CHUNK = 64
+MLP_ROWS = 192
 SEQS_STEP = 2
 C_SQ, C_SO, C_CQ, C_CK, C_CO, C_I0, C_I1, C_WO, C_END = 0, 1152, 1536, 1920, 2688, 3072, 4096, 5120, 6144
 BF = jnp.bfloat16
@@ -70,7 +72,7 @@
         return pl.ds(pl.multiple_of(r0 + off, CHUNK), CHUNK)
 
     chunks = range(0, SEQ, CHUNK)
-    slot, wait_slot, send, weights_here = exchange
+    slot, wait_slot, send, weights_here, tail = exchange
     lane_idx = lax.broadcasted_iota(jnp.int32, (SEQ, QB), 1)
     tri = lax.broadcasted_iota(jnp.int32, (QB, QB), 0) <= lax.broadcasted_iota(jnp.int32, (QB, QB), 1)
 
@@ -144,14 +146,15 @@
         unit, _ = unit_of(mid.astype(F32))
         n3_s[chunk_rows(off), :] = (unit * gain_ref[2:3, :]).astype(BF)
     step = 256
-    for col in range(0, FF, step):
-        pre_0 = nn(n3_s[rows, :], w_ref[:, C_I0 + col:C_I0 + col + step])
-        pre_1 = nn(n3_s[rows, :], w_ref[:, C_I1 + col:C_I1 + col + step])
-        d_hid = nn(dy_ref[rows, :], w_ref[:, C_WO + col:C_WO + col + step])
-        for off in chunks:
-            a0 = pre_0[off:off + CHUNK].astype(BF).astype(F32)
-            a1 = pre_1[off:off + CHUNK].astype(BF).astype(F32)
-            dh = d_hid[off:off + CHUNK].astype(BF).astype(F32)
+    for col, top in itertools.product(range(0, FF, step), range(0, SEQ, MLP_ROWS)):
+        part = pl.ds(pl.multiple_of(r0 + top, CHUNK), MLP_ROWS)
+        pre_0 = nn(n3_s[part, :], w_ref[:, C_I0 + col:C_I0 + col + step])
+        pre_1 = nn(n3_s[part, :], w_ref[:, C_I1 + col:C_I1 + col + step])
+        d_hid = nn(dy_ref[part, :], w_ref[:, C_WO + col:C_WO + col + step])
+        for off in range(top, top + MLP_ROWS, CHUNK):
+            a0 = pre_0[off - top:off - top + CHUNK].astype(BF).astype(F32)
+            a1 = pre_1[off - top:off - top + CHUNK].astype(BF).astype(F32)
+            dh = d_hid[off - top:off - top + CHUNK].astype(BF).astype(F32)
             sq = a0 * a0
             half = 0.5 * jnp.tanh(a0 * (GELU_C + (GELU_C * GELU_K) * sq)) + 0.5
             gelu = a0 * half
@@ -178,6 +181,8 @@
 
     d_norm = nt(d01_s[rows, :], w_ref[:, C_I0:C_I0 + 2 * FF])
     norm_back(d_norm, lambda off: x2_s[off:off + CHUNK, :], dy_ref, lambda off: dm2_s.at[chunk_rows(off), :], 2)
+
+    tail(0)
 
     dctx_s[...] = nn(dm2_s[rows, :], w_ref[:, C_CO:C_CO + INNER]).astype(BF)
 
@@ -205,6 +210,8 @@
     de_buf[slot] = nt(dckv_s[erows, :], w_ref[:, C_CK:C_CK + 2 * INNER]).astype(BF)
     send(2)
     norm_back(d_norm, lambda off: x1_s[off:off + CHUNK, :], dm2_s, lambda off: dm1_s.at[chunk_rows(off), :], 1)
+
+    tail(1)
 
     dctx_s[...] = nn(dm1_s[rows, :], w_ref[:, C_SO:C_SO + INNER]).astype(BF)
 
@@ -269,19 +276,23 @@
 ]
 
 
-def weight_grads(g_ref, e_ref, dy_ref, n1_s, n2_s, n3_s, dm1_s, dm2_s, dqkv_s, ctx_s, dcq_s, dckv_s, cctx_s, hid_s, d01_s):
-    def add(act, d_out, col, width):
-        for off in range(0, width, 384 if width % 384 == 0 else 512):
-            size = 384 if width % 384 == 0 else 512
-            g_ref[:, col + off:col + off + size] += tn(act[...], d_out[:, off:off + size])
-
-    add(n3_s, d01_s, C_I0, 2 * FF)
-    add(dy_ref, hid_s, C_WO, FF)
-    add(dm2_s, cctx_s, C_CO, INNER)
-    add(n2_s, dcq_s, C_CQ, INNER)
-    add(e_ref, dckv_s, C_CK, 2 * INNER)
-    add(dm1_s, ctx_s, C_SO, INNER)
-    add(n1_s, dqkv_s, C_SQ, 3 * INNER)
+def add_grad(g_ref, act, d_out, col, width):
+    size = 384 if width % 384 == 0 else 512
+    for off in range(0, width, size):
+        g_ref[:, col + off:col + off + size] += tn(act[...], d_out[:, off:off + size])
+
+
+def mlp_grads(gm_s, dy_ref, n3_s, hid_s, d01_s):
+    add_grad(gm_s, n3_s, d01_s, 0, 2 * FF)
+    add_grad(gm_s, dy_ref, hid_s, 2 * FF, FF)
+
+
+def attn_grads(g_ref, e_ref, n1_s, n2_s, dm1_s, dm2_s, dqkv_s, ctx_s, dcq_s, dckv_s, cctx_s):
+    add_grad(g_ref, dm2_s, cctx_s, C_CO, INNER)
+    add_grad(g_ref, n2_s, dcq_s, C_CQ, INNER)
+    add_grad(g_ref, e_ref, dckv_s, C_CK, 2 * INNER)
+    add_grad(g_ref, dm1_s, ctx_s, C_SO, INNER)
+    add_grad(g_ref, n1_s, dqkv_s, C_SQ, 3 * INNER)
 
 
 O_I0, O_I1, O_WO, O_EX, O_END = 2048, 2560, 3072, 3584, 3712
@@ -415,8 +426,8 @@
 
 
 def layer_kernel(x_ref, e_ref, dy_ref, *refs):
-    attn, mlp, (extra_ref, y_hbm, dx_hbm, de_hbm, g_ref, ext_ref), scratch = refs[:8], refs[8:11], refs[11:17], refs[17:]
-    *scratch, y_buf, dx_buf, de_buf, w_ref, rz_s, gain_ref, bias_ref, loc_ref, dg_ref, db_ref, local_sem, send_sem, recv_sem, w_send, w_recv = scratch
+    attn, mlp, (extra_ref, y_hbm, dx_hbm, de_hbm, g_ref, ext_ref, first_hbm, first_ext, mlp_ref), scratch = refs[:8], refs[8:11], refs[11:20], refs[20:]
+    *scratch, y_buf, dx_buf, de_buf, w_ref, rz_s, gain_ref, bias_ref, loc_ref, dg_ref, db_ref, local_sem, send_sem, recv_sem, w_send, w_recv, g_send, g_recv, gm_s, mf_s, mx_s, my_s, m_send, m_recv = scratch
     plan = gather_plan(loc_ref, rz_s, w_ref, w_send, w_recv)
     (n1_s, n2_s, n3_s, dm1_s, dm2_s, qkv_s, dqkv_s, ctx_s, cq_s, ckv_s, dcq_s, dckv_s, cctx_s,
      hid_s, d01_s, x1_s, x2_s, dctx_s, pf_s, pt_s, cpf_s, cpt_s, ds_s, cds_s, km_s, vm_s) = scratch
@@ -460,6 +471,7 @@
         arrive_all(plan[2][1])
         begin(plan[2][2])
         g_ref[...] = jnp.zeros_like(g_ref)
+        gm_s[...] = jnp.zeros_like(gm_s)
         arrive_all(plan[0][3])
         fill_gains(w_ref, gain_ref)
 
@@ -473,8 +485,44 @@
             recv_sem=recv_sem.at[which, number], device_id={"model": other}, device_id_type=MESH)
         return local, remote
 
+    d = lax.axis_index("data")
+    core, x, y = lax.rem(d, 2), lax.rem(d // 2, 2), d // 4
+    to_core, to_x, to_y = {"data": d + 1 - 2 * core}, {"data": d + 2 - 4 * x}, {"data": d + 4 - 8 * y}
+    half = (C_END - C_I0) // 2
+
+    def rows_of(yy, xx, cc):
+        return pl.ds(pl.multiple_of(64 * (4 * yy + 2 * xx + cc), 64), 64)
+
+    def mlp_copy(number, src, dst, peer):
+        return pltpu.make_async_remote_copy(src_ref=src, dst_ref=dst, send_sem=m_send.at[number], recv_sem=m_recv.at[number],
+                                            device_id=peer, device_id_type=MESH)
+
+    def mlp_phase(phase):
+        if phase == 0:
+            return [mlp_copy(b, gm_s.at[rows_of(b // 2, b % 2, 1 - core), :], mf_s.at[64 * b:64 * b + 64, :], to_core) for b in range(4)]
+        if phase == 1:
+            return ([mlp_copy(4 + b, gm_s.at[rows_of(b, 1 - x, core), 0:half], mx_s.at[64 * b:64 * b + 64, :], to_x) for b in range(2)]
+                    + [mlp_copy(6 + b, gm_s.at[rows_of(1 - y, b, core), half:2 * half], my_s.at[64 * b:64 * b + 64, :], to_y) for b in range(2)])
+        return []
+
     def body(s, carry):
         number = step * SEQS_STEP + s
+
+        def tail(point):
+            if point == 0:
+                @pl.when(s == SEQS_STEP - 1)
+                def _():
+                    mlp_grads(gm_s, dy_ref, n3_s, hid_s, d01_s)
+
+            @pl.when(number == seqs - 1)
+            def _():
+                if point == 1:
+                    for copy in mlp_phase(0):
+                        copy.wait_recv()
+                    for b in range(4):
+                        gm_s[rows_of(b // 2, b % 2, core), :] += mf_s[64 * b:64 * b + 64, :]
+                for copy in mlp_phase(point):
+                    copy.start()
 
         def wait_slot(which):
             @pl.when(number >= 2)
@@ -500,15 +548,35 @@
                             for make in phase:
                                 make().wait_send()
 
-        seq_body(s, (lax.rem(number, 2), wait_slot, send, weights_here), x_ref, e_ref, dy_ref, w_ref, gain_ref, bias_ref, y_buf, dx_buf, de_buf, dg_ref, db_ref, *scratch)
+        seq_body(s, (lax.rem(number, 2), wait_slot, send, weights_here, tail), x_ref, e_ref, dy_ref, w_ref, gain_ref, bias_ref, y_buf, dx_buf, de_buf, dg_ref, db_ref, *scratch)
         return carry
 
     lax.fori_loop(0, SEQS_STEP, body, 0)
-    weight_grads(g_ref, e_ref, dy_ref, n1_s, n2_s, n3_s, dm1_s, dm2_s, dqkv_s, ctx_s, dcq_s, dckv_s, cctx_s, hid_s, d01_s)
+    attn_grads(g_ref, e_ref, n1_s, n2_s, dm1_s, dm2_s, dqkv_s, ctx_s, dcq_s, dckv_s, cctx_s)
 
     @pl.when(step == pl.num_programs(0) - 1)
     def _():
+        def push_core(src, dst, b, number):
+            copy = pltpu.make_async_remote_copy(
+                src_ref=src.at[rows_of(b // 2, b % 2, 1 - core), :], dst_ref=dst.at[64 * b:64 * b + 64, :],
+                send_sem=g_send.at[number], recv_sem=g_recv.at[number], device_id=to_core, device_id_type=MESH)
+            copy.start()
+            return copy
+
+        pushed = [push_core(g_ref, first_hbm, b, b) for b in range(4)]
         small_grads(dg_ref, db_ref, ext_ref)
+        pushed += [push_core(ext_ref, first_ext, b, 4 + b) for b in range(4)]
+        for copy in mlp_phase(1):
+            copy.wait_recv()
+        for b in range(2):
+            blk = slice(64 * b, 64 * b + 64)
+            mlp_ref[blk, 0:half] = gm_s[rows_of(b, x, core), 0:half] + mx_s[blk, :]
+            mlp_ref[blk, half:2 * half] = gm_s[rows_of(y, b, core), half:2 * half] + my_s[blk, :]
+        for phase in range(2):
+            for copy in mlp_phase(phase):
+                copy.wait_send()
+        for copy in pushed:
+            copy.wait()
         for which in range(3):
             for back in (2, 1):
                 local, remote = copies(which, seqs - back)
@@ -522,35 +590,34 @@
             lax.fori_loop(0, seqs, arrived, 0)
 
 
-RUNS = (((0, 1920), (C_END, QB)), ((1920, 1152), (C_WO, FF)), ((C_I0, 2 * FF),))
+R_EX, R_END = C_I0, C_I0 + QB
+RUNS = (((0, 1152), (R_EX, QB)), ((1152, 1152),), ((2304, 768),))
+MLP_PIECES = ((0, 512, O_I0), (1024, 512, O_I1), (2048, 512, O_WO))
 
 
 def z_pieces(group):
     attn = [(INNER * b, QB, 256, 256 * b) for b in range(8)]
     if group == 0:
-        return attn[:5] + [(C_END, 0, QB, O_EX)]
-    if group == 1:
-        return attn[5:] + [(C_WO, 512, 512, O_WO)]
-    return [(C_I0, 512, 512, O_I0), (C_I1, 512, 512, O_I1)]
+        return attn[:3] + [(R_EX, 0, QB, O_EX)]
+    return attn[3:6] if group == 1 else attn[6:]
 
 
 Z_WIDTH = tuple(sum(piece[2] for piece in z_pieces(group)) for group in range(3))
 RUN_WIDTH = tuple(sum(run[1] for run in RUNS[group]) for group in range(3))
-REDUCE_SCRATCH = [(2, 2, 64, C_END + QB), (2, 2, 64, C_END + QB),
+REDUCE_SCRATCH = [(2, 2, 64, R_END), (2, 2, 64, R_END),
                   (2, 64, RUN_WIDTH[0]), (64, RUN_WIDTH[0]), (64, Z_WIDTH[0]),
                   (2, 64, RUN_WIDTH[1]), (2, 64, Z_WIDTH[1]), (64, Z_WIDTH[1]),
-                  (2, 2, 64, Z_WIDTH[2]), (2, 64, Z_WIDTH[2]), (64, Z_WIDTH[2])]
+                  (2, 2, 64, Z_WIDTH[2]), (2, 64, Z_WIDTH[2]), (64, Z_WIDTH[2]), (128, 3072), (64, 3072), (64, 3072), (64, 1536)]
 REDUCE_SEMS = 64
 
 
-def reduce_kernel(g_hbm, ext_hbm, out_ref, acc, first, a1, a2, a3, b1, b2, b3, c1, c2, c3, local_sem, send_sem, recv_sem):
+def reduce_kernel(g_hbm, ext_hbm, first_hbm, first_ext, mlp_hbm, out_ref, acc, first, a1, a2, a3, b1, b2, b3, c1, c2, c3, mlp_in, mlp_second, mlp_own, mlp_far, local_sem, send_sem, recv_sem):
     m, d = lax.axis_index("model"), lax.axis_index("data")
     core, x, y = lax.rem(d, 2), lax.rem(d // 2, 2), d // 4
-    to_core, to_x, to_y, to_z = {"data": d + 1 - 2 * core}, {"data": d + 2 - 4 * x}, {"data": d + 4 - 8 * y}, {"model": 1 - m}
+    to_x, to_y, to_z = {"data": d + 2 - 4 * x}, {"data": d + 4 - 8 * y}, {"model": 1 - m}
     barrier = pltpu.get_barrier_semaphore()
-    for peer in (to_core, to_x, to_y, to_z):
+    for peer in (to_x, to_y, to_z):
         pl.semaphore_signal(barrier, inc=1, device_id=peer, device_id_type=MESH)
-    pl.semaphore_wait(barrier, 4)
     sent = []
 
     def push(src, dst, peer):
@@ -567,15 +634,24 @@
     loads, pend = {}, {}
     number = 0
     for group in (2, 0, 1):
-        loads[group], pend[group] = [], []
+        loads[group] = []
         for col, width in RUNS[group]:
-            src = ext_hbm if col == C_END else g_hbm
-            src_cols = pl.ds(0 if col == C_END else col, width)
-            here = pltpu.make_async_copy(src.at[:, :, core, :, src_cols], acc.at[:, :, :, pl.ds(col, width)], local_sem.at[number])
-            number += 1
-            pend[group].append(push(src.at[:, :, 1 - core, :, src_cols], first.at[:, :, :, pl.ds(col, width)], to_core))
-            here.start()
-            loads[group].append(here)
+            own, far = (ext_hbm, first_ext) if col == R_EX else (g_hbm, first_hbm)
+            src_cols = pl.ds(0 if col == R_EX else col, width)
+            for src, dst in ((own.at[:, :, core, :, src_cols], acc), (far.at[:, :, :, src_cols], first)):
+                here = pltpu.make_async_copy(src, dst.at[:, :, :, pl.ds(col, width)], local_sem.at[number])
+                number += 1
+                here.start()
+                loads[group].append(here)
+    mlp_load = pltpu.make_async_copy(mlp_hbm, mlp_in, local_sem.at[number])
+    mlp_load.start()
+    pl.semaphore_wait(barrier, 3)
+    mlp_load.wait()
+    def rows64(blk):
+        return pl.ds(pl.multiple_of(64 * blk, 64), 64)
+
+    mlp_pend = [push(mlp_in.at[rows64(1 - y), 0:1536], mlp_second.at[:, 0:1536], to_y),
+                push(mlp_in.at[rows64(1 - x), 1536:3072], mlp_second.at[:, 1536:3072], to_x)]
 
     def run_push(group, src_of, dst, peer):
         off, out = 0, []
@@ -594,8 +670,6 @@
     for group in (2, 0, 1):
         for here in loads[group]:
             here.wait()
-        for copy in pend[group]:
-            copy.wait_recv()
         for col, width in RUNS[group]:
             for yy in range(2):
                 for xx in range(2):
@@ -606,6 +680,13 @@
             pend[1] = run_push(1, lambda c: acc.at[1 - y, :, :, c], b1, to_y)
         else:
             pend[2] = z_push(2, lambda c: acc.at[:, :, :, c], c1, to_z, 1 - m)
+
+    for copy in mlp_pend:
+        copy.wait_recv()
+    mlp_own[:, 0:1536] = mlp_in[rows64(y), 0:1536] + mlp_second[:, 0:1536]
+    mlp_own[:, 1536:3072] = mlp_in[rows64(x), 1536:3072] + mlp_second[:, 1536:3072]
+    mlp_pend = [push(mlp_own.at[:, pl.ds(pl.multiple_of(col + (1 - m) * width, QB), width)], mlp_far.at[:, width * n:width * n + width], to_z)
+                for n, (col, width, _) in enumerate(MLP_PIECES)]
 
     def arrive(group):
         for copy in pend[group]:
@@ -625,7 +706,10 @@
             acc[y, xx, :, col:col + width] += b1[xx, :, off:off + width]
         off += width
     pend[1] = z_push(1, lambda c: acc.at[y, :, :, c], b2, to_z, 1 - m)
-    arrive(2)
+    held_z = pend[2]
+    for copy in held_z:
+        copy.wait_recv()
+        copy.wait_send()
     off = 0
     for piece in z_pieces(2):
         for yy in range(2):
@@ -664,23 +748,27 @@
         for piece in z_pieces(group):
             out_ref[:, piece[3]:piece[3] + piece[2]] = acc[y, x, :, cols(piece, m)] + last[:, off:off + piece[2]]
             off += piece[2]
+    for n, (col, width, place) in enumerate(MLP_PIECES):
+        mlp_pend[n].wait_recv()
+        mine = pl.ds(pl.multiple_of(col + m * width, QB), width)
+        out_ref[:, place:place + width] = mlp_own[:, mine] + mlp_far[:, width * n:width * n + width]
     for copy in sent:
-        if not any(copy is other for other in held):
+        if not any(copy is other for other in held + held_z):
             copy.wait_send()
 
 
-def scatter_grads(grad_all, ext):
+def scatter_grads(grad_attn, ext, first, first_ext, mlp):
     m = lax.axis_index("model")
     mine = pl.pallas_call(
         reduce_kernel,
         out_shape=jax.ShapeDtypeStruct((64, O_END), F32),
-        in_specs=[pl.BlockSpec(memory_space=pl.ANY)] * 2,
+        in_specs=[pl.BlockSpec(memory_space=pl.ANY)] * 5,
         out_specs=pl.BlockSpec(memory_space=pltpu.VMEM),
         scratch_shapes=[pltpu.VMEM(item, F32) for item in REDUCE_SCRATCH] + [
-            pltpu.SemaphoreType.DMA((8,)), pltpu.SemaphoreType.DMA((REDUCE_SEMS,)), pltpu.SemaphoreType.DMA((REDUCE_SEMS,))],
+            pltpu.SemaphoreType.DMA((16,)), pltpu.SemaphoreType.DMA((REDUCE_SEMS,)), pltpu.SemaphoreType.DMA((REDUCE_SEMS,))],
         compiler_params=pltpu.CompilerParams(vmem_limit_bytes=67043328, collective_id=1, has_side_effects=True),
         name="reduce",
-    )(grad_all.reshape(2, 2, 2, 64, C_END), ext.reshape(2, 2, 2, 64, QB))
+    )(grad_attn.reshape(2, 2, 2, 64, C_I0), ext.reshape(2, 2, 2, 64, QB), first.reshape(2, 2, 64, C_I0), first_ext.reshape(2, 2, 64, QB), mlp)
     outs = [jnp.where(m == 0, mine[:, 256 * b:256 * b + 192], mine[:, 256 * b + 64:256 * b + 256]) for b in range(8)]
     outs += [mine[:, O_I0:O_I1], mine[:, O_I1:O_WO], mine[:, O_WO:O_EX]]
     bias = jnp.where(m == 0, mine[:NUM_BUCKETS, O_EX + 64:O_EX + 67], mine[:NUM_BUCKETS, O_EX + 67:O_EX + 70])
@@ -695,19 +783,23 @@
     rows, erows = SEQS_STEP * SEQ, SEQS_STEP * ENC
     seqs = SEQS_STEP * steps
     outs = [jax.ShapeDtypeStruct(x.shape, BF), jax.ShapeDtypeStruct(x.shape, BF), jax.ShapeDtypeStruct(e.shape, BF),
-            jax.ShapeDtypeStruct((DIM, C_END), F32), jax.ShapeDtypeStruct((DIM, QB), F32)]
+            jax.ShapeDtypeStruct((DIM, C_I0), F32), jax.ShapeDtypeStruct((DIM, QB), F32),
+            jax.ShapeDtypeStruct((DIM // 2, C_I0), F32), jax.ShapeDtypeStruct((DIM // 2, QB), F32),
+            jax.ShapeDtypeStruct((128, C_END - C_I0), F32)]
     return pl.pallas_call(
         layer_kernel,
         out_shape=outs,
         grid=(steps,),
         in_specs=[part(rows), part(erows), part(rows)] + [fixed(w.shape) for w in attn + mlp + [extra]],
-        out_specs=[anywhere, anywhere, anywhere, fixed((DIM, C_END)), fixed((DIM, QB))],
+        out_specs=[anywhere, anywhere, anywhere, fixed((DIM, C_I0)), fixed((DIM, QB)), anywhere, anywhere, fixed((128, C_END - C_I0))],
         scratch_shapes=[pltpu.VMEM(*item) for item in SCRATCH] + [
             pltpu.VMEM((2, SEQ, DIM), BF), pltpu.VMEM((2, SEQ, DIM), BF), pltpu.VMEM((2, ENC, DIM), BF),
             pltpu.VMEM((DIM, C_END + QB), BF), pltpu.VMEM((64, O_END), BF), pltpu.VMEM((8, DIM), F32), pltpu.VMEM((HEADS, SEQ, QB), F32),
             pltpu.VMEM((64, O_END), BF), pltpu.VMEM((24, DIM), F32), pltpu.VMEM((HEADS, SEQ, QB), F32),
             pltpu.SemaphoreType.DMA((3, 2)), pltpu.SemaphoreType.DMA((3, 2)), pltpu.SemaphoreType.DMA((3, seqs)),
-            pltpu.SemaphoreType.DMA((GATHER_SEMS,)), pltpu.SemaphoreType.DMA((GATHER_SEMS,))],
+            pltpu.SemaphoreType.DMA((GATHER_SEMS,)), pltpu.SemaphoreType.DMA((GATHER_SEMS,)), pltpu.SemaphoreType.DMA((8,)), pltpu.SemaphoreType.DMA((8,)),
+            pltpu.VMEM((DIM, C_END - C_I0), F32), pltpu.VMEM((256, C_END - C_I0), F32), pltpu.VMEM((128, 1536), F32), pltpu.VMEM((128, 1536), F32),
+            pltpu.SemaphoreType.DMA((8,)), pltpu.SemaphoreType.DMA((8,))],
         compiler_params=pltpu.CompilerParams(dimension_semantics=("arbitrary",), vmem_limit_bytes=67043328, collective_id=0, has_side_effects=True),
         name="layer",
     )(x, e, dy, *attn, *mlp, extra)
@@ -721,8 +813,8 @@
         return arr.reshape(-1, DIM)
 
     attn = [self_q, self_k, self_v, self_o.T, cross_q, cross_k, cross_v, cross_o.T]
-    dec_out, grad_dec, grad_enc, grad_all, grad_ext = layer_call(flat(dec_in), flat(enc_out), flat(grad_out), attn, [mlp_wi_0, mlp_wi_1, mlp_wo.T], extra)
-    grads, d_gains, grad_bias = scatter_grads(grad_all, grad_ext)
+    dec_out, grad_dec, grad_enc, *partial = layer_call(flat(dec_in), flat(enc_out), flat(grad_out), attn, [mlp_wi_0, mlp_wi_1, mlp_wo.T], extra)
+    grads, d_gains, grad_bias = scatter_grads(*partial)
     o_sq, o_sk, o_sv, o_so, o_cq, o_ck, o_cv, o_co, o_i0, o_i1, o_wo = grads
     return (dec_out.reshape(dec_in.shape), grad_dec.reshape(dec_in.shape), grad_enc.reshape(enc_out.shape), grad_bias, o_sq, o_sk, o_sv, o_so.T, o_cq, o_ck, o_cv, o_co.T, o_i0, o_i1, o_wo.T, d_gains[0], d_gains[1], d_gains[2])
 

time: 317 us -> 302 us (0.953)
  Pallas kernels: 295 us -> 279 us
    pallas_call x1, Pallas kernels: 63.2 us -> 45.4 us  [scatter_grads(): pl.pallas_call(reduce_kernel, out_shape=jax.ShapeDtypeStruct((64, O_END),...]
where the time goes in v5:
time: 302 us; the launch traced here: 301 us
  Pallas kernels  279 us (92%)
  local copies, waits for them, and re-layouts  16.7 us (6%)
  other arithmetic  4.59 us (2%)
    pallas_call x1, Pallas kernels, layer_call(): pl.pallas_call(layer_kernel, out_shape=outs, grid=(steps,), in_specs=[par...  234 us
    pallas_call x1, Pallas kernels, scatter_grads(): pl.pallas_call(reduce_kernel, out_shape=jax.ShapeDtypeStruct((64, O_END),...  45.4 us
    unnamed x11, local copies, waits for them, and re-layouts  13.5 us

profile of v5, /device:TPU:0, one launch (start us, length us, event | category | flops | bytes accessed | tf_op | source)
XLA Modules:
  0.0 301.4 jit_solution(1899349079224675439)
XLA Ops:
  0.7 0.8 copy.36
  1.4 1.4 fusion.9.refs_11_
  2.8 234.1 %layer.1 = (bf16[6144,512]{1,0:T(8,128)(2,1)}, bf16[6144,512]{1,0:T(8,128)(2,1)}, bf16[3072,512]{1,0:T(8,128)(2,1)}, f32[512,3072]{1,0:T(8,128)}, f32[512,128]{1...) custom-call(bf16[6144,512]{1,0:T(8,128)(2,1)} %bitcast.28, bf16[3072,512]{1,0:T(8,128)(2,1)} %bitcast.36, ...), custom_call_target="tpu_custom_call" | custom-call | tf_op jit(solution)/shard_map/layer/pallas_call | solution.py:789
  236.9 45.4 %reduce.1 = f32[64,3712]{1,0:T(8,128)} custom-call(f32[2,2,2,64,3072]{4,3,2,1,0:T(8,128)} %bitcast.34, f32[2,2,2,64,128]{4,3,2,1,0:T(8,128)} %bitcast.38, f32[2,2,64,3072]{3,2,1,0:T(8,128)} %bitcast.37, f32[2,2,64,128]{3,2,1,0:T(8,128)} %bitcast.39, f32[128,3072]{1,0:T(8,128)} %get-tuple-element.33.mlp_hbm), custom_call_target="tpu_custom_call" | custom-call | tf_op jit(solution)/shard_map/reduce/pallas_call | solution.py:762
  282.2 2.3 select_bitcast_fusion
  284.6 0.0 slice-start
  284.6 1.9 slice_bitcast_fusion
  286.5 1.3 slice_bitcast_fusion.1
  287.8 0.9 slice_select_fusion.6
  288.7 0.7 copy.37
  289.3 0.0 slice-start.1
  289.3 6.2 %copy.41 = bf16[16,384,512]{2,1,0:T(8,128)(2,1)} copy(bf16[16,384,512]{2,1,0:T(8,128)(2,1)} %bitcast.33) | data formatting | bytes 12582912
  295.5 0.0 slice-done
  295.5 0.0 slice-done.1
  295.5 0.0 copy-start
  295.6 3.2 %copy.42 = bf16[16,384,512]{2,1,0:T(8,128)(2,1)} copy(bf16[16,384,512]{2,1,0:T(8,128)(2,1)S(1)} %bitcast.32) | data formatting | bytes 12582912
  298.7 1.0 copy-done
  299.7 1.7 copy.43
  (1 shorter events, 0.0 us)
Async XLA Ops:
  284.6 11.0 %slice-start = ((s8[6291456]{0:T(1024)(128)(4,1)}), s8[2097152]{0:T(1024)(128)(4,1)S(1)}, s32[]{:S(2)}) async-start(s8[6291456]{0:T(1024)(128)(4,1)} %bitcast.30), calls=%async_computation | async-start | bytes 4194304
  289.3 6.2 %slice-start.1 = ((s8[6291456]{0:T(1024)(128)(4,1)}), s8[4194304]{0:T(1024)(128)(4,1)S(1)}, s32[]{:S(2)}) async-start(s8[6291456]{0:T(1024)(128)(4,1)} %bitcast.30), calls=%async_computation.1 | async-start | bytes 8388608
  295.5 4.2 %copy-start = (bf16[3072,512]{1,0:T(8,128)(2,1)S(1)}, bf16[3072,512]{1,0:T(8,128)(2,1)}, u32[]{:S(2)}) copy-start(bf16[3072,512]{1,0:T(8,128)(2,1)} %get-tuple-element.28) | copy-start | bytes 9437188
